TPU v7x, 32 devices: a whole 2x2x4 slice. The times are simulated.
32 devices in a mesh: band: 16 (over z, y, core), grid: 2 (over x).
Axes of the slice: x: 2, y: 2, z: 4, core: 2. Of those that a mesh axis runs over, the one named last changes fastest.
Arguments:
- orbitals: float32 [32, 64, 4096], P('band', 'grid'), may hold values from -4 to 4
- pair_list: int32 [16, 4, 2], P('band'), may hold values from 0 to 31, as said below
- pair_count: int32 [16], P('band'), may hold values from 1 to 4, 32 in all
Outputs:
- exchange_proj: float32 [32, 64, 4096], P('band', 'grid')
Inputs may be any that keep to these rules, and one draw needn't show every extreme that they name: `pair_list`: entry 0 is an orbital index 0 to 1 within the row's band group; entry 1 is a global orbital index owned by the same band group or by one of the next 2 groups, counted cyclically; the two never name the same orbital. Band group b uses its first pair_count[b] slots.
All inputs are finite; a program needn't handle non-finite values.
Results may differ from a plain program's by a relative error of at most 0.0003.
Values sent between devices are 32-bit elements; how exact they have to be, the bound alone decides.
A program may use at most 64 MiB of HBM per device.

v0:
```python
import functools
import math

import jax
import jax.numpy as jnp
import numpy as np
from jax import lax
from jax.experimental import pallas as pl
from jax.experimental.pallas import tpu as pltpu
from jax.sharding import PartitionSpec as P

REACH = 2
GROUP = 8


def rotated(value, axis, steps):
    count = lax.axis_size(axis)
    pairs = [(source, (source + steps) % count) for source in range(count)]
    return lax.ppermute(value, axis, pairs)


def swapped(value, axis):
    count = lax.axis_size(axis)
    return lax.ppermute(value, axis, [(source, source ^ 1) for source in range(count)])


def split(value):
    high = value.astype(jnp.bfloat16)
    return high, (value - high.astype(jnp.float32)).astype(jnp.bfloat16)


def tables(side, half_rows):
    points = np.arange(side)
    angles = (points[:, None] * points[None, :] % side) * (2.0 * math.pi / side)
    hartley = (np.cos(angles) + np.sin(angles)).astype(np.float32)
    high = hartley.astype(jnp.bfloat16)
    low = (hartley - high.astype(np.float32)).astype(jnp.bfloat16)
    eye = np.eye(2, dtype=np.float32)
    wide_high = np.kron(eye, high.astype(np.float32))
    wide_low = np.kron(eye, low.astype(np.float32))
    right = np.block([[wide_high, wide_low], [wide_high, wide_low]]).astype(jnp.bfloat16)
    left = np.concatenate([high, high, low], 1)
    eigenvalues = 2.0 - 2.0 * np.cos(points * (2.0 * math.pi / side))
    shift = 1.0 / side**2 + eigenvalues[:, None] + np.tile(eigenvalues, 2)[None, :]
    ratio = 1.0 + shift / 2 - np.sqrt(shift + shift**2 / 4)
    power = ratio**half_rows
    reach = ratio**GROUP
    scale = 1.0 / side / (1.0 / ratio - ratio) / side**2
    wrap = 1.0 / (1.0 - power**4)
    decay = np.stack([ratio, power, scale, wrap, reach]).astype(np.float32)
    return right, left, decay


def along_last(value, right):
    width = value.shape[1]
    product = jnp.dot(
        jnp.concatenate(split(value), 1), right, preferred_element_type=jnp.float32
    )
    return product[:, :width] + product[:, width:]


def along_second(planes, left):
    width = planes[0].shape[1]
    out = []
    for start in range(0, len(planes), 2):
        both = jnp.concatenate(planes[start : start + 2], 1)
        high, low = split(both)
        stacked = jnp.concatenate([high, low, high], 0)
        product = jnp.dot(left, stacked, preferred_element_type=jnp.float32)
        out.append(product[:, :width])
        out.append(product[:, width:])
    return out


def halves(value):
    return pltpu.roll(value, value.shape[-1] // 2, axis=value.ndim - 1)


def arrange_kernel(row, source, *refs):
    packed = refs[-1]
    _, slab_rows, cells = source.shape
    width = packed.shape[-1]
    half = slab_rows // 2
    lower = lax.broadcasted_iota(jnp.int32, (GROUP, width), 1) < width // 2
    tiles = 4

    def tile_step(step, carry):
        ys = pl.ds(pl.multiple_of(step * 2 * tiles, 2 * tiles), 2 * tiles)
        for start in range(0, half, GROUP):
            lines = []
            for k in range(tiles):
                lanes = pl.ds(pl.multiple_of((step * tiles + k) * width, width), width)
                near = source[row, pl.ds(start, GROUP), lanes]
                far = source[row, pl.ds(start + half, GROUP), lanes]
                lines.append(jnp.where(lower, near, halves(far)))
                lines.append(jnp.where(lower, halves(near), far))
            packed[pl.ds(start, GROUP), ys, :] = jnp.swapaxes(jnp.stack(lines, 0), 0, 1)
        return carry

    lax.fori_loop(0, cells // (width * tiles), tile_step, 0)


def stack_kernel(first, second, own):
    own[0] = first[...]
    own[1] = second[...]


def restore_kernel(row, flag, own, passed, arrived, *refs):
    out = refs[-1]
    _, slab_rows, cells = out.shape
    width = own.shape[-1]
    half = slab_rows // 2
    lower = lax.broadcasted_iota(jnp.int32, (GROUP, width), 1) < width // 2
    weight = flag[0].astype(jnp.float32)
    tiles = 4

    def tile_step(step, carry):
        ys = pl.ds(pl.multiple_of(step * 2 * tiles, 2 * tiles), 2 * tiles)
        for start in range(0, half, GROUP):
            planes = pl.ds(start, GROUP)
            block = own[row, planes, ys, :] + weight * passed[planes, ys, :] + arrived[planes, ys, :]
            block = jnp.swapaxes(block, 0, 1)
            for k in range(tiles):
                lanes = pl.ds(pl.multiple_of((step * tiles + k) * width, width), width)
                even, odd = block[2 * k], block[2 * k + 1]
                out[0, planes, lanes] = jnp.where(lower, even, halves(odd))
                out[0, pl.ds(start + half, GROUP), lanes] = jnp.where(lower, halves(even), odd)
        return carry

    lax.fori_loop(0, cells // (width * tiles), tile_step, 0)


def pick_kernel(flag, after, far, own, out):
    @pl.when(flag[0] == 0)
    def _():
        out[...] = far[...]

    @pl.when(flag[0] == 1)
    def _():
        out[...] = own[...]


def join_kernel(flag, after, distant, handed, out):
    weight = 1.0 - flag[0].astype(jnp.float32)
    out[...] = distant[...] + weight * handed[...]


def slab_moments(moments, i, reach):
    count = moments.shape[1]
    ahead = moments[i, 0, 0]
    behind = moments[i, count - 1, 1]
    for k in range(1, count):
        ahead = ahead * reach + moments[i, k, 0]
        behind = behind * reach + moments[i, count - 1 - k, 1]
    return ahead, behind


def forward_kernel(base, counts, after, own, other, right_ref, left_ref, decay, spectrum, moments, mine):
    owned, rows, side, width = own.shape
    chunks = rows // GROUP
    lower = lax.broadcasted_iota(jnp.int32, (side, width), 1) < width // 2

    def orbital_step(i, carry):
        live = counts[base + i] > 0

        def chunk_step(c, carry):
            block = pl.ds(pl.multiple_of(c * GROUP, GROUP), GROUP)
            density = own[i, block] * other[block]
            value = along_last(density.reshape(GROUP * side, width), right_ref[...])
            planes = [value[k * side : (k + 1) * side] for k in range(GROUP)]
            planes = along_second(planes, left_ref[...])
            ratio = decay[0]
            ahead = planes[0]
            behind = planes[-1]
            for k in range(GROUP):
                spectrum[i, c * GROUP + k] = planes[k]
                if k:
                    ahead = ahead * ratio + planes[k]
                    behind = behind * ratio + planes[GROUP - 1 - k]
            moments[i, c, 0] = ahead
            moments[i, c, 1] = behind
            return carry

        lax.fori_loop(0, jnp.where(live, chunks, 0), chunk_step, 0)

        @pl.when(live)
        def _():
            power = decay[1]
            ahead, behind = slab_moments(moments, i, decay[4])
            mine[i] = jnp.where(lower, behind + power * halves(behind), ahead + power * halves(ahead))

        return carry

    lax.fori_loop(0, owned, orbital_step, 0)


def backward_kernel(
    base, inside, counts, after, own, other, spectrum, moments, mine, arrived,
    right_ref, left_ref, decay, *refs
):
    edge = refs[-1]
    if inside:
        before, total = refs[:2]
        total[...] = before[...]
    else:
        total, partner = refs[-3:-1]
        total[...] = refs[0][...] if len(refs) > 3 else jnp.zeros_like(total)
        partner[...] = jnp.zeros_like(partner)
    owned, rows, side, width = own.shape
    chunks = rows // GROUP
    lower = lax.broadcasted_iota(jnp.int32, (side, width), 1) < width // 2

    def orbital_step(i, carry):
        number = counts[base + i]

        @pl.when(number > 0)
        def _():
            power, reach = decay[1], decay[4]
            ahead_all, behind_all = slab_moments(moments, i, reach)
            entering = (arrived[i] + power * power * mine[i]) * decay[3]
            turned = halves(entering)
            ahead = jnp.where(lower, turned, halves(ahead_all) + power * entering)
            behind = jnp.where(lower, halves(behind_all) + power * entering, turned)
            edge[0, 0] = ahead
            edge[chunks - 1, 1] = behind
            for k in range(1, chunks):
                ahead = ahead * reach + moments[i, k - 1, 0]
                edge[k, 0] = ahead
                behind = behind * reach + moments[i, chunks - k, 1]
                edge[chunks - 1 - k, 1] = behind

        def chunk_step(c, carry):
            block = pl.ds(pl.multiple_of(c * GROUP, GROUP), GROUP)
            ratio = decay[0]
            scale = decay[2] * number.astype(jnp.float32)
            ahead = edge[c, 0]
            behind = edge[c, 1]
            tails = []
            for k in reversed(range(GROUP)):
                spilled = ratio * behind
                tails.insert(0, spilled)
                behind = spectrum[i, c * GROUP + k] + spilled
            planes = []
            for k in range(GROUP):
                ahead = spectrum[i, c * GROUP + k] + ratio * ahead
                planes.append(scale * (ahead + tails[k]))
            planes = along_second(planes, left_ref[...])
            value = along_last(jnp.concatenate(planes, 0), right_ref[...])
            potential = value.reshape(GROUP, side, width)
            total[i, block] += potential * other[block]
            if inside:
                total[1, block] += potential * own[i, block]
            else:
                partner[block] += potential * own[i, block]
            return carry

        lax.fori_loop(0, jnp.where(number > 0, chunks, 0), chunk_step, 0)
        return carry

    lax.fori_loop(0, owned, orbital_step, 0)


def pair_counts(pair_list, pair_count, owned, band_index, band_count):
    first, partner = pair_list[0, :, 0], pair_list[0, :, 1]
    live = jnp.arange(first.shape[0]) < pair_count[0]
    distance = (partner // owned - band_index) % band_count
    inside = (REACH * owned) * owned
    place = ((partner % owned) * REACH + distance - 1) * owned + first
    place = jnp.where(distance == 0, inside, place)
    places = jnp.arange(inside + owned)
    return jnp.sum(jnp.where(live[None, :] & (place[None, :] == places[:, None]), 1, 0), axis=1)


def on_device(orbitals, pair_list, pair_count):
    owned, slab_rows, plane_cells = orbitals.shape
    side = math.isqrt(plane_cells)
    assert lax.axis_size("grid") == 2 and REACH == 2 and owned == 2
    rows = slab_rows // 2
    chunks = rows // GROUP
    band_count = lax.axis_size("band")
    band_index = lax.axis_index("band")
    right, left, decay = tables(side, rows)
    smem = pl.BlockSpec(memory_space=pltpu.SMEM)
    vmem = pl.BlockSpec(memory_space=pltpu.VMEM)
    free = pl.BlockSpec(memory_space=pl.ANY)
    params = pltpu.CompilerParams(vmem_limit_bytes=12 * 2**20)
    shape = (rows, side, 2 * side)
    one = jax.ShapeDtypeStruct(shape, jnp.float32)
    both = jax.ShapeDtypeStruct((owned,) + shape, jnp.float32)

    def call(kernel, out_shape, in_specs, out_specs=vmem, scratch=(), aliases={}, grid=()):
        if isinstance(out_shape, tuple):
            out_specs = (vmem,) * len(out_shape)
        return pl.pallas_call(
            kernel,
            out_shape=out_shape,
            grid=grid,
            in_specs=in_specs,
            out_specs=out_specs,
            scratch_shapes=scratch,
            compiler_params=params,
            input_output_aliases=aliases,
            cost_estimate=pl.CostEstimate(flops=0, bytes_accessed=1 << 20, transcendentals=0),
        )

    fields, far = [], []
    for row in range(owned):
        field = call(
            functools.partial(arrange_kernel, row), one, [vmem] + [free] * row
        )(orbitals, *fields)
        fields.append(field)
        far.append(rotated(field, "band", -2))
    own = call(stack_kernel, both, [vmem, vmem])(*fields)
    flag = (band_index % 2).reshape(1)
    counts = pair_counts(pair_list, pair_count, owned, band_index, band_count)

    def forward(base, after, other):
        spectrum, moments, mine = call(
            functools.partial(forward_kernel, base),
            (
                both,
                jax.ShapeDtypeStruct((owned, chunks, 2) + shape[1:], jnp.float32),
                jax.ShapeDtypeStruct((owned,) + shape[1:], jnp.float32),
            ),
            [smem, free] + [vmem] * 5,
        )(counts, after, own, other, right, left, decay)
        return (other, spectrum, moments, mine, swapped(mine, "grid"))

    def backward(base, after, state, total, inside=False):
        return call(
            functools.partial(backward_kernel, base, inside),
            both if inside else (both, one),
            [smem, free] + [vmem] * (9 + len(total)),
            scratch=[pltpu.VMEM((chunks, 2) + shape[1:], jnp.float32)],
        )(counts, after, own, *state, right, left, decay, *total)

    inner_base = REACH * owned * owned
    inner = forward(inner_base, own, fields[1])
    after = inner[3]
    total, passed, arrived = (), [], []
    for row in range(owned):
        base = row * REACH * owned
        picked = call(pick_kernel, one, [smem, free, vmem, vmem])(
            flag, after, far[row], fields[row]
        )
        near = swapped(picked, "band")
        distant_state = forward(base + owned, picked, far[row])
        near_state = forward(base, distant_state[3], near)
        acc, handed = backward(base, near_state[3], near_state, total)
        handed_over = swapped(handed, "band")
        acc, distant = backward(base + owned, handed, distant_state, (acc,))
        total = (acc,)
        joined = call(join_kernel, one, [smem, free, vmem, vmem])(
            flag, distant, distant, handed_over
        )
        passed.append(handed_over)
        arrived.append(rotated(joined, "band", 2))
        after = joined
    total = backward(inner_base, after, inner, total, inside=True)
    out = jax.ShapeDtypeStruct(orbitals.shape, jnp.float32)
    result = None
    for row in range(owned):
        earlier = [] if result is None else [result]
        result = call(
            functools.partial(restore_kernel, row),
            out,
            [smem] + [vmem] * 3 + [free] * len(earlier),
            out_specs=pl.BlockSpec(
                (1,) + orbitals.shape[1:], functools.partial(lambda r, step: (r, 0, 0), row)
            ),
            grid=(1,),
            aliases={4: 0} if earlier else {},
        )(flag, total, passed[row], arrived[row], *earlier)
    return result


def solution(mesh):
    in_specs = (P("band", "grid", None), P("band", None, None), P("band"))
    out_specs = P("band", "grid", None)

    return jax.shard_map(
        on_device, mesh=mesh, in_specs=in_specs, out_specs=out_specs, check_vma=False
    )
```

profile of v0, /device:TPU:0, one launch (start us, length us, event | category | flops | bytes accessed | tf_op | source)
XLA Modules:
  0.0 85.5 jit_solution(12508034089762707345)
XLA Ops:
  0.0 0.0 copy-start.2
  0.0 1.2 %copy-done.2 = f32[2,32,4096]{2,1,0:T(8,128)S(1)} copy-done((f32[2,32,4096]{2,1,0:T(8,128)S(1)}, f32[2,32,4096]{2,1,0:T(8,128)}, u32[]{:S(2)}) %copy-start.2) | copy-done | bytes 1048600
  1.2 0.0 copy-start.3
  1.2 0.7 shard_map.64.refs_0_.first.own
  2.0 6.1 %collective-permute-start = (f32[16,64,128]{2,1,0:T(8,128)S(1)}, f32[16,64,128]{2,1,0:T(8,128)S(1)}, u32[]{:S(2)}, u32[]{:S(2)}) collective-permute-start(f32[16,64,128]{2,1,0:T(8,128)S(1)} %shard_map.64.refs_0_.first.own), channel_id=1, source_target_pairs={{0,28},{2,30},{4,0},{6,2},{8,4},{10,6},{12,8},{14,10},{16,12},{18,... | collective-permute-start | bytes 1572872 | tf_op jit(solution)/shard_map/ppermute | solution.py:19
  8.1 0.0 copy-done.3
  8.1 0.7 shard_map.65.second.other.own
  8.8 0.0 copy-start
  8.8 0.0 copy-start.1
  8.8 0.0 copy-start.4
  8.9 0.1 shard_map.66.after.own
  9.6 0.0 copy-start.5
  9.7 0.7 copy-done.5
  10.3 0.1 select_reduce_fusion.counts
  10.4 0.0 copy-done
  10.4 0.0 copy-done.1
  10.5 0.0 copy-done.4
  10.5 0.6 shard_map.67
  11.1 8.2 %collective-permute-done.far.other = f32[16,64,128]{2,1,0:T(8,128)S(1)} collective-permute-done((f32[16,64,128]{2,1,0:T(8,128)S(1)}, f32[16,64,128]{2,1,0:T(8,128)S(1)}, u32[]{:S(2)}, u32[]{:S(2)}) %collective-permute-start) | collective-permute-done | bytes 524320 | tf_op jit(solution)/shard_map/ppermute | solution.py:19
  19.3 0.1 collective-permute-start.1
  19.4 0.6 shard_map.69
  20.0 1.3 %collective-permute-done.1.other = f32[16,64,128]{2,1,0:T(8,128)S(1)} collective-permute-done((f32[16,64,128]{2,1,0:T(8,128)S(1)}, f32[16,64,128]{2,1,0:T(8,128)S(1)}, u32[]{:S(2)}, u32[]{:S(2)}) %collective-permute-start.1) | collective-permute-done | bytes 524320 | tf_op jit(solution)/shard_map/ppermute | solution.py:24
  21.3 0.6 shard_map.70
  21.9 1.6 %collective-permute-start.2 = (f32[2,64,128]{2,1,0:T(8,128)S(1)}, f32[2,64,128]{2,1,0:T(8,128)S(1)}, u32[]{:S(2)}, u32[]{:S(2)}) collective-permute-start(f32[2,64,128]{2,1,0:T(8,128)S(1)} %get-tuple-element.30.after.mine), channel_id=1, source_target_pairs={{0,1},{1,0},{2,3},{3,2},{4,5},{5,4},{6,7},{7,6},{8,9},{9,8},{10,11... | collective-permute-start | bytes 196616 | tf_op jit(solution)/shard_map/ppermute | solution.py:24
  23.4 2.8 %collective-permute-done.2.arrived = f32[2,64,128]{2,1,0:T(8,128)S(1)} collective-permute-done((f32[2,64,128]{2,1,0:T(8,128)S(1)}, f32[2,64,128]{2,1,0:T(8,128)S(1)}, u32[]{:S(2)}, u32[]{:S(2)}) %collective-permute-start.2) | collective-permute-done | bytes 65568 | tf_op jit(solution)/shard_map/ppermute | solution.py:24
  26.2 0.7 shard_map.71
  26.9 0.1 collective-permute-start.4
  27.0 7.2 %collective-permute-start.5 = (f32[16,64,128]{2,1,0:T(8,128)S(1)}, f32[16,64,128]{2,1,0:T(8,128)S(1)}, u32[]{:S(2)}, u32[]{:S(2)}) collective-permute-start(f32[16,64,128]{2,1,0:T(8,128)S(1)} %shard_map.65.second.other.own), channel_id=1, source_target_pairs={{0,28},{2,30},{4,0},{6,2},{8,4},{10,6},{12,8},{14,10},{16,12},{18,... | collective-permute-start | bytes 1572872 | tf_op jit(solution)/shard_map/ppermute | solution.py:19
  34.1 1.5 %collective-permute-start.3 = (f32[2,64,128]{2,1,0:T(8,128)S(1)}, f32[2,64,128]{2,1,0:T(8,128)S(1)}, u32[]{:S(2)}, u32[]{:S(2)}) collective-permute-start(f32[2,64,128]{2,1,0:T(8,128)S(1)} %get-tuple-element.29.after.mine), channel_id=1, source_target_pairs={{0,1},{1,0},{2,3},{3,2},{4,5},{5,4},{6,7},{7,6},{8,9},{9,8},{10,11... | collective-permute-start | bytes 196616 | tf_op jit(solution)/shard_map/ppermute | solution.py:24
  35.6 2.8 %collective-permute-done.3.arrived = f32[2,64,128]{2,1,0:T(8,128)S(1)} collective-permute-done((f32[2,64,128]{2,1,0:T(8,128)S(1)}, f32[2,64,128]{2,1,0:T(8,128)S(1)}, u32[]{:S(2)}, u32[]{:S(2)}) %collective-permute-start.3) | collective-permute-done | bytes 65568 | tf_op jit(solution)/shard_map/ppermute | solution.py:24
  38.4 0.7 shard_map.72
  39.1 0.0 collective-permute-done.4.handed.passed
  39.1 0.1 shard_map.73.after
  39.2 6.8 %collective-permute-done.5.far.other = f32[16,64,128]{2,1,0:T(8,128)S(1)} collective-permute-done((f32[16,64,128]{2,1,0:T(8,128)S(1)}, f32[16,64,128]{2,1,0:T(8,128)S(1)}, u32[]{:S(2)}, u32[]{:S(2)}) %collective-permute-start.5) | collective-permute-done | bytes 524320 | tf_op jit(solution)/shard_map/ppermute | solution.py:19
  46.0 0.1 collective-permute-start.6
  46.1 1.6 %shard_map.75 = (f32[2,16,64,128]{3,2,1,0:T(8,128)S(1)}, f32[2,2,2,64,128]{4,3,2,1,0:T(8,128)S(1)}, f32[2,64,128]{2,1,0:T(8,128)S(1)}) custom-call(s32[10]{0:T(128)S(1)} %select_reduce_fusion.counts, f32[16,64,128]{2,1,0:T(8,128)S(1)} %shard_map.74.after, f32[2,16,64,128]{3,2,1,0:T(8,128)S(1)} %shard_map.66.after.own, ...), custom_call_target="tpu_custom_call" | custom-call | bytes 1048576 | tf_op jit(solution)/shard_map/pallas_call | solution.py:318
  47.7 0.3 collective-permute-done.6.other
  47.9 0.6 shard_map.76
  48.5 1.6 %collective-permute-start.7 = (f32[2,64,128]{2,1,0:T(8,128)S(1)}, f32[2,64,128]{2,1,0:T(8,128)S(1)}, u32[]{:S(2)}, u32[]{:S(2)}) collective-permute-start(f32[2,64,128]{2,1,0:T(8,128)S(1)} %get-tuple-element.39.after.mine), channel_id=1, source_target_pairs={{0,1},{1,0},{2,3},{3,2},{4,5},{5,4},{6,7},{7,6},{8,9},{9,8},{10,11... | collective-permute-start | bytes 196616 | tf_op jit(solution)/shard_map/ppermute | solution.py:24
  50.1 2.8 %collective-permute-done.7.arrived = f32[2,64,128]{2,1,0:T(8,128)S(1)} collective-permute-done((f32[2,64,128]{2,1,0:T(8,128)S(1)}, f32[2,64,128]{2,1,0:T(8,128)S(1)}, u32[]{:S(2)}, u32[]{:S(2)}) %collective-permute-start.7) | collective-permute-done | bytes 65568 | tf_op jit(solution)/shard_map/ppermute | solution.py:24
  52.9 0.7 shard_map.77
  53.6 0.1 collective-permute-start.9
  53.6 1.6 %collective-permute-start.8 = (f32[2,64,128]{2,1,0:T(8,128)S(1)}, f32[2,64,128]{2,1,0:T(8,128)S(1)}, u32[]{:S(2)}, u32[]{:S(2)}) collective-permute-start(f32[2,64,128]{2,1,0:T(8,128)S(1)} %get-tuple-element.38.after.mine), channel_id=1, source_target_pairs={{0,1},{1,0},{2,3},{3,2},{4,5},{5,4},{6,7},{7,6},{8,9},{9,8},{10,11... | collective-permute-start | bytes 196616 | tf_op jit(solution)/shard_map/ppermute | solution.py:24
  55.2 0.0 collective-permute-start.12
  55.2 2.9 %collective-permute-done.8.arrived = f32[2,64,128]{2,1,0:T(8,128)S(1)} collective-permute-done((f32[2,64,128]{2,1,0:T(8,128)S(1)}, f32[2,64,128]{2,1,0:T(8,128)S(1)}, u32[]{:S(2)}, u32[]{:S(2)}) %collective-permute-start.8) | collective-permute-done | bytes 65568 | tf_op jit(solution)/shard_map/ppermute | solution.py:24
  58.1 1.6 %shard_map.78 = (f32[2,16,64,128]{3,2,1,0:T(8,128)S(1)}, f32[16,64,128]{2,1,0:T(8,128)S(1)}) custom-call(s32[10]{0:T(128)S(1)} %select_reduce_fusion.counts, f32[16,64,128]{2,1,0:T(8,128)S(1)} %get-tuple-element.43.after, f32[2,16,64,128]{3,2,1,0:T(8,128)S(1)} %shard_map.66.after.own, f32[16,64,128]{2,1,0:T(8,128)S(1)} %collective-permute-done.5.far.other, ...), custom_call_target="tpu_custom_call" | custom-call | bytes 1048576 | tf_op jit(solution)/shard_map/pallas_call | solution.py:330
  59.7 0.0 collective-permute-done.9.handed.passed
  59.8 0.1 shard_map.79.after
  59.8 0.1 collective-permute-start.11
  59.9 1.6 %collective-permute-start.10 = (f32[2,64,128]{2,1,0:T(8,128)S(1)}, f32[2,64,128]{2,1,0:T(8,128)S(1)}, u32[]{:S(2)}, u32[]{:S(2)}) collective-permute-start(f32[2,64,128]{2,1,0:T(8,128)S(1)} %get-tuple-element.28.after.mine), channel_id=1, source_target_pairs={{0,1},{1,0},{2,3},{3,2},{4,5},{5,4},{6,7},{7,6},{8,9},{9,8},{10,11... | collective-permute-start | bytes 196616 | tf_op jit(solution)/shard_map/ppermute | solution.py:24
  61.4 2.8 %collective-permute-done.10.arrived = f32[2,64,128]{2,1,0:T(8,128)S(1)} collective-permute-done((f32[2,64,128]{2,1,0:T(8,128)S(1)}, f32[2,64,128]{2,1,0:T(8,128)S(1)}, u32[]{:S(2)}, u32[]{:S(2)}) %collective-permute-start.10) | collective-permute-done | bytes 65568 | tf_op jit(solution)/shard_map/ppermute | solution.py:24
  64.2 0.6 shard_map.80.own
  64.9 8.3 %collective-permute-done.12.arrived = f32[16,64,128]{2,1,0:T(8,128)S(1)} collective-permute-done((f32[16,64,128]{2,1,0:T(8,128)S(1)}, f32[16,64,128]{2,1,0:T(8,128)S(1)}, u32[]{:S(2)}, u32[]{:S(2)}) %collective-permute-start.12) | collective-permute-done | bytes 524320 | tf_op jit(solution)/shard_map/ppermute | solution.py:19
  73.2 1.7 %shard_map.81.refs_0_ = f32[2,32,4096]{2,1,0:T(8,128)} custom-call(s32[1]{0:T(128)} %bitcast.flag, f32[2,16,64,128]{3,2,1,0:T(8,128)S(1)} %shard_map.80.own, f32[16,64,128]{2,1,0:T(8,128)S(1)} %collective-permute-done.4.handed.passed, f32[16,64,128]{2,1,0:T(8,128)S(1)} %collective-permute-done.12.arrived), custom_call_target="tpu_custom_call" | custom-call | bytes 1048576 | tf_op jit(solution)/shard_map/pallas_call | solution.py:364
  74.8 9.0 %collective-permute-done.11.arrived = f32[16,64,128]{2,1,0:T(8,128)S(1)} collective-permute-done((f32[16,64,128]{2,1,0:T(8,128)S(1)}, f32[16,64,128]{2,1,0:T(8,128)S(1)}, u32[]{:S(2)}, u32[]{:S(2)}) %collective-permute-start.11) | collective-permute-done | bytes 524320 | tf_op jit(solution)/shard_map/ppermute | solution.py:19
  83.9 1.7 %shard_map.82 = f32[2,32,4096]{2,1,0:T(8,128)} custom-call(s32[1]{0:T(128)} %bitcast.flag, f32[2,16,64,128]{3,2,1,0:T(8,128)S(1)} %shard_map.80.own, f32[16,64,128]{2,1,0:T(8,128)S(1)} %collective-permute-done.9.handed.passed, f32[16,64,128]{2,1,0:T(8,128)S(1)} %collective-permute-done.11.arrived, ...), custom_call_target="tpu_custom_call", output_to_operand_aliasing={{}: (4, {})} | custom-call | bytes 1048576 | tf_op jit(solution)/shard_map/pallas_call | solution.py:364
  (4 shorter events, 0.1 us)
Async XLA Ops:
  0.0 1.2 %copy-start.2 = (f32[2,32,4096]{2,1,0:T(8,128)S(1)}, f32[2,32,4096]{2,1,0:T(8,128)}, u32[]{:S(2)}) copy-start(f32[2,32,4096]{2,1,0:T(8,128)} %source.3) | copy-start | bytes 3145732
  1.2 6.8 %copy-start.3 = (f32[2,32,4096]{2,1,0:T(8,128)S(1)}, f32[2,32,4096]{2,1,0:T(8,128)}, u32[]{:S(2)}) copy-start(f32[2,32,4096]{2,1,0:T(8,128)} %source.3) | copy-start | bytes 3145732
  2.0 17.3 %collective-permute-start = (f32[16,64,128]{2,1,0:T(8,128)S(1)}, f32[16,64,128]{2,1,0:T(8,128)S(1)}, u32[]{:S(2)}, u32[]{:S(2)}) collective-permute-start(f32[16,64,128]{2,1,0:T(8,128)S(1)} %shard_map.64.refs_0_.first.own), channel_id=1, source_target_pairs={{0,28},{2,30},{4,0},{6,2},{8,4},{10,6},{12,8},{14,10},{16,12},{18,... | collective-permute-start | bytes 1572872 | tf_op jit(solution)/shard_map/ppermute | solution.py:19
  8.8 1.6 %copy-start = (f32[5,64,128]{2,1,0:T(8,128)S(1)}, f32[5,64,128]{2,1,0:T(8,128)}, u32[]{:S(2)}) copy-start(f32[5,64,128]{2,1,0:T(8,128)} %constant.65.clone.decay) | copy-start | bytes 491524
  8.8 1.6 %copy-start.1 = (bf16[256,256]{1,0:T(8,128)(2,1)S(1)}, bf16[256,256]{1,0:T(8,128)(2,1)}, u32[]{:S(2)}) copy-start(bf16[256,256]{1,0:T(8,128)(2,1)} %constant.63.clone.right_ref) | copy-start | bytes 393220
  8.8 1.6 %copy-start.4 = (bf16[64,192]{1,0:T(8,128)(2,1)S(1)}, bf16[64,192]{1,0:T(8,128)(2,1)}, u32[]{:S(2)}) copy-start(bf16[64,192]{1,0:T(8,128)(2,1)} %constant.64.clone.left_ref) | copy-start | bytes 73732
  9.6 0.7 copy-start.5
  19.3 2.0 %collective-permute-start.1 = (f32[16,64,128]{2,1,0:T(8,128)S(1)}, f32[16,64,128]{2,1,0:T(8,128)S(1)}, u32[]{:S(2)}, u32[]{:S(2)}) collective-permute-start(f32[16,64,128]{2,1,0:T(8,128)S(1)} %shard_map.68.after), channel_id=1, source_target_pairs={{0,2},{2,0},{4,6},{6,4},{8,10},{10,8},{12,14},{14,12},{16,18},{18,... | collective-permute-start | bytes 1572872 | tf_op jit(solution)/shard_map/ppermute | solution.py:24
  21.9 4.3 %collective-permute-start.2 = (f32[2,64,128]{2,1,0:T(8,128)S(1)}, f32[2,64,128]{2,1,0:T(8,128)S(1)}, u32[]{:S(2)}, u32[]{:S(2)}) collective-permute-start(f32[2,64,128]{2,1,0:T(8,128)S(1)} %get-tuple-element.30.after.mine), channel_id=1, source_target_pairs={{0,1},{1,0},{2,3},{3,2},{4,5},{5,4},{6,7},{7,6},{8,9},{9,8},{10,11... | collective-permute-start | bytes 196616 | tf_op jit(solution)/shard_map/ppermute | solution.py:24
  26.9 12.2 %collective-permute-start.4 = (f32[16,64,128]{2,1,0:T(8,128)S(1)}, f32[16,64,128]{2,1,0:T(8,128)S(1)}, u32[]{:S(2)}, u32[]{:S(2)}) collective-permute-start(f32[16,64,128]{2,1,0:T(8,128)S(1)} %get-tuple-element.33.after), channel_id=1, source_target_pairs={{0,2},{2,0},{4,6},{6,4},{8,10},{10,8},{12,14},{14,12},{16,18},{18,... | collective-permute-start | bytes 1572872 | tf_op jit(solution)/shard_map/ppermute | solution.py:24
  27.0 19.0 %collective-permute-start.5 = (f32[16,64,128]{2,1,0:T(8,128)S(1)}, f32[16,64,128]{2,1,0:T(8,128)S(1)}, u32[]{:S(2)}, u32[]{:S(2)}) collective-permute-start(f32[16,64,128]{2,1,0:T(8,128)S(1)} %shard_map.65.second.other.own), channel_id=1, source_target_pairs={{0,28},{2,30},{4,0},{6,2},{8,4},{10,6},{12,8},{14,10},{16,12},{18,... | collective-permute-start | bytes 1572872 | tf_op jit(solution)/shard_map/ppermute | solution.py:19
  34.1 4.3 %collective-permute-start.3 = (f32[2,64,128]{2,1,0:T(8,128)S(1)}, f32[2,64,128]{2,1,0:T(8,128)S(1)}, u32[]{:S(2)}, u32[]{:S(2)}) collective-permute-start(f32[2,64,128]{2,1,0:T(8,128)S(1)} %get-tuple-element.29.after.mine), channel_id=1, source_target_pairs={{0,1},{1,0},{2,3},{3,2},{4,5},{5,4},{6,7},{7,6},{8,9},{9,8},{10,11... | collective-permute-start | bytes 196616 | tf_op jit(solution)/shard_map/ppermute | solution.py:24
  46.0 2.0 %collective-permute-start.6 = (f32[16,64,128]{2,1,0:T(8,128)S(1)}, f32[16,64,128]{2,1,0:T(8,128)S(1)}, u32[]{:S(2)}, u32[]{:S(2)}) collective-permute-start(f32[16,64,128]{2,1,0:T(8,128)S(1)} %shard_map.74.after), channel_id=1, source_target_pairs={{0,2},{2,0},{4,6},{6,4},{8,10},{10,8},{12,14},{14,12},{16,18},{18,... | collective-permute-start | bytes 1572872 | tf_op jit(solution)/shard_map/ppermute | solution.py:24
  48.5 4.3 %collective-permute-start.7 = (f32[2,64,128]{2,1,0:T(8,128)S(1)}, f32[2,64,128]{2,1,0:T(8,128)S(1)}, u32[]{:S(2)}, u32[]{:S(2)}) collective-permute-start(f32[2,64,128]{2,1,0:T(8,128)S(1)} %get-tuple-element.39.after.mine), channel_id=1, source_target_pairs={{0,1},{1,0},{2,3},{3,2},{4,5},{5,4},{6,7},{7,6},{8,9},{9,8},{10,11... | collective-permute-start | bytes 196616 | tf_op jit(solution)/shard_map/ppermute | solution.py:24
  53.6 6.2 %collective-permute-start.9 = (f32[16,64,128]{2,1,0:T(8,128)S(1)}, f32[16,64,128]{2,1,0:T(8,128)S(1)}, u32[]{:S(2)}, u32[]{:S(2)}) collective-permute-start(f32[16,64,128]{2,1,0:T(8,128)S(1)} %get-tuple-element.43.after), channel_id=1, source_target_pairs={{0,2},{2,0},{4,6},{6,4},{8,10},{10,8},{12,14},{14,12},{16,18},{18,... | collective-permute-start | bytes 1572872 | tf_op jit(solution)/shard_map/ppermute | solution.py:24
  53.6 4.5 %collective-permute-start.8 = (f32[2,64,128]{2,1,0:T(8,128)S(1)}, f32[2,64,128]{2,1,0:T(8,128)S(1)}, u32[]{:S(2)}, u32[]{:S(2)}) collective-permute-start(f32[2,64,128]{2,1,0:T(8,128)S(1)} %get-tuple-element.38.after.mine), channel_id=1, source_target_pairs={{0,1},{1,0},{2,3},{3,2},{4,5},{5,4},{6,7},{7,6},{8,9},{9,8},{10,11... | collective-permute-start | bytes 196616 | tf_op jit(solution)/shard_map/ppermute | solution.py:24
  55.2 18.0 %collective-permute-start.12 = (f32[16,64,128]{2,1,0:T(8,128)S(1)}, f32[16,64,128]{2,1,0:T(8,128)S(1)}, u32[]{:S(2)}, u32[]{:S(2)}) collective-permute-start(f32[16,64,128]{2,1,0:T(8,128)S(1)} %shard_map.73.after), channel_id=1, source_target_pairs={{0,4},{2,6},{4,8},{6,10},{8,12},{10,14},{12,16},{14,18},{16,20},{1... | collective-permute-start | bytes 1572872 | tf_op jit(solution)/shard_map/ppermute | solution.py:19
  59.8 24.0 %collective-permute-start.11 = (f32[16,64,128]{2,1,0:T(8,128)S(1)}, f32[16,64,128]{2,1,0:T(8,128)S(1)}, u32[]{:S(2)}, u32[]{:S(2)}) collective-permute-start(f32[16,64,128]{2,1,0:T(8,128)S(1)} %shard_map.79.after), channel_id=1, source_target_pairs={{0,4},{2,6},{4,8},{6,10},{8,12},{10,14},{12,16},{14,18},{16,20},{1... | collective-permute-start | bytes 1572872 | tf_op jit(solution)/shard_map/ppermute | solution.py:19
  59.9 4.3 %collective-permute-start.10 = (f32[2,64,128]{2,1,0:T(8,128)S(1)}, f32[2,64,128]{2,1,0:T(8,128)S(1)}, u32[]{:S(2)}, u32[]{:S(2)}) collective-permute-start(f32[2,64,128]{2,1,0:T(8,128)S(1)} %get-tuple-element.28.after.mine), channel_id=1, source_target_pairs={{0,1},{1,0},{2,3},{3,2},{4,5},{5,4},{6,7},{7,6},{8,9},{9,8},{10,11... | collective-permute-start | bytes 196616 | tf_op jit(solution)/shard_map/ppermute | solution.py:24
where the time goes:
time: 85.7 us; the launch traced here: 85.5 us
  waiting for transfers between devices  47.9 us (56%)
  starting transfers between devices  21.3 us (25%)
  Pallas kernels  13.3 us (16%)
  local copies, waits for them, and re-layouts  1.91 us (2%)
  between operations  0.96 us (1%)
    ppermute x4, waiting for transfers between devices, rotated(): return lax.ppermute(value, axis, pairs)  32.3 us
    ppermute x9, waiting for transfers between devices, swapped(): lax.ppermute(value, axis, [(source, source ^ 1) for source in range(count)])  15.6 us
    ppermute x4, starting transfers between devices, rotated(): return lax.ppermute(value, axis, pairs)  13.3 us
    ppermute x9, starting transfers between devices, swapped(): lax.ppermute(value, axis, [(source, source ^ 1) for source in range(count)])  8.02 us
    pallas_call x5, Pallas kernels, backward(): call(functools.partial(backward_kernel, base, inside), both if inside els...  4.29 us
    pallas_call x5, Pallas kernels, forward(): call(functools.partial(forward_kernel, base), (both, jax.ShapeDtypeStruct...  3.93 us
    pallas_call x2, Pallas kernels, on_device(): call(functools.partial(restore_kernel, row), out, [smem] + [vmem] * 3 + [...  3.31 us
    unnamed x12, local copies, waits for them, and re-layouts  1.91 us
  transfers between devices with their start and end apart: 13, of which 11 were waited for; matrix products, arithmetic and copies ran while one was open for 0% of the time, Pallas kernels for 10%

commit v1 on v0

--- a/solution.py
+++ b/solution.py
@@ -76,13 +76,26 @@
     return pltpu.roll(value, value.shape[-1] // 2, axis=value.ndim - 1)
 
 
+PARTS = 4
+DIGIT = 3
+
+
 def arrange_kernel(row, source, *refs):
-    packed = refs[-1]
-    _, slab_rows, cells = source.shape
+    packed, raw, arrivals = refs[-3:]
+    slab_rows, cells = raw.shape
     width = packed.shape[-1]
     half = slab_rows // 2
     lower = lax.broadcasted_iota(jnp.int32, (GROUP, width), 1) < width // 2
     tiles = 4
+    parts = arrivals.shape[0]
+    part = cells // parts
+    copies = []
+    for k in range(parts):
+        lanes = pl.ds(k * part, part)
+        copies.append(
+            pltpu.make_async_copy(source.at[row, :, lanes], raw.at[:, lanes], arrivals.at[k])
+        )
+        copies[-1].start()
 
     def tile_step(step, carry):
         ys = pl.ds(pl.multiple_of(step * 2 * tiles, 2 * tiles), 2 * tiles)
@@ -90,14 +103,17 @@
             lines = []
             for k in range(tiles):
                 lanes = pl.ds(pl.multiple_of((step * tiles + k) * width, width), width)
-                near = source[row, pl.ds(start, GROUP), lanes]
-                far = source[row, pl.ds(start + half, GROUP), lanes]
+                near = raw[pl.ds(start, GROUP), lanes]
+                far = raw[pl.ds(start + half, GROUP), lanes]
                 lines.append(jnp.where(lower, near, halves(far)))
                 lines.append(jnp.where(lower, halves(near), far))
             packed[pl.ds(start, GROUP), ys, :] = jnp.swapaxes(jnp.stack(lines, 0), 0, 1)
         return carry
 
-    lax.fori_loop(0, cells // (width * tiles), tile_step, 0)
+    steps = part // (width * tiles)
+    for k in range(parts):
+        copies[k].wait()
+        lax.fori_loop(k * steps, (k + 1) * steps, tile_step, 0)
 
 
 def stack_kernel(first, second, own):
@@ -114,8 +130,11 @@
     weight = flag[0].astype(jnp.float32)
     tiles = 4
 
+    steps = cells // (width * tiles)
+    base = pl.program_id(0) * steps
+
     def tile_step(step, carry):
-        ys = pl.ds(pl.multiple_of(step * 2 * tiles, 2 * tiles), 2 * tiles)
+        ys = pl.ds(pl.multiple_of((base + step) * 2 * tiles, 2 * tiles), 2 * tiles)
         for start in range(0, half, GROUP):
             planes = pl.ds(start, GROUP)
             block = own[row, planes, ys, :] + weight * passed[planes, ys, :] + arrived[planes, ys, :]
@@ -127,7 +146,7 @@
                 out[0, pl.ds(start + half, GROUP), lanes] = jnp.where(lower, halves(even), odd)
         return carry
 
-    lax.fori_loop(0, cells // (width * tiles), tile_step, 0)
+    lax.fori_loop(0, steps, tile_step, 0)
 
 
 def pick_kernel(flag, after, far, own, out):
@@ -155,13 +174,17 @@
     return ahead, behind
 
 
-def forward_kernel(base, counts, after, own, other, right_ref, left_ref, decay, spectrum, moments, mine):
+def forward_kernel(base, counts, after, own, other, right_ref, left_ref, decay, *refs):
+    spectrum, moments, mine = refs[-3:]
+    offset = mine.shape[0] - own.shape[0]
+    if offset:
+        mine[:offset] = refs[0][...]
     owned, rows, side, width = own.shape
     chunks = rows // GROUP
     lower = lax.broadcasted_iota(jnp.int32, (side, width), 1) < width // 2
 
     def orbital_step(i, carry):
-        live = counts[base + i] > 0
+        live = count_at(counts, base + i) > 0
 
         def chunk_step(c, carry):
             block = pl.ds(pl.multiple_of(c * GROUP, GROUP), GROUP)
@@ -187,7 +210,7 @@
         def _():
             power = decay[1]
             ahead, behind = slab_moments(moments, i, decay[4])
-            mine[i] = jnp.where(lower, behind + power * halves(behind), ahead + power * halves(ahead))
+            mine[offset + i] = jnp.where(lower, behind + power * halves(behind), ahead + power * halves(ahead))
 
         return carry
 
@@ -195,7 +218,7 @@
 
 
 def backward_kernel(
-    base, inside, counts, after, own, other, spectrum, moments, mine, arrived,
+    base, inside, offset, counts, after, own, other, spectrum, moments, mine, arrived,
     right_ref, left_ref, decay, *refs
 ):
     edge = refs[-1]
@@ -211,13 +234,13 @@
     lower = lax.broadcasted_iota(jnp.int32, (side, width), 1) < width // 2
 
     def orbital_step(i, carry):
-        number = counts[base + i]
+        number = count_at(counts, base + i)
 
         @pl.when(number > 0)
         def _():
             power, reach = decay[1], decay[4]
             ahead_all, behind_all = slab_moments(moments, i, reach)
-            entering = (arrived[i] + power * power * mine[i]) * decay[3]
+            entering = (arrived[offset + i] + power * power * mine[offset + i]) * decay[3]
             turned = halves(entering)
             ahead = jnp.where(lower, turned, halves(ahead_all) + power * entering)
             behind = jnp.where(lower, halves(behind_all) + power * entering, turned)
@@ -267,8 +290,11 @@
     inside = (REACH * owned) * owned
     place = ((partner % owned) * REACH + distance - 1) * owned + first
     place = jnp.where(distance == 0, inside, place)
-    places = jnp.arange(inside + owned)
-    return jnp.sum(jnp.where(live[None, :] & (place[None, :] == places[:, None]), 1, 0), axis=1)
+    return jnp.sum(jnp.where(live, lax.shift_left(1, DIGIT * place), 0)).reshape(1)
+
+
+def count_at(counts, place):
+    return lax.shift_right_logical(counts[0], DIGIT * place) & (2**DIGIT - 1)
 
 
 def on_device(orbitals, pair_list, pair_count):
@@ -283,6 +309,7 @@
     smem = pl.BlockSpec(memory_space=pltpu.SMEM)
     vmem = pl.BlockSpec(memory_space=pltpu.VMEM)
     free = pl.BlockSpec(memory_space=pl.ANY)
+    hbm = pl.BlockSpec(memory_space=pltpu.HBM)
     params = pltpu.CompilerParams(vmem_limit_bytes=12 * 2**20)
     shape = (rows, side, 2 * side)
     one = jax.ShapeDtypeStruct(shape, jnp.float32)
@@ -306,7 +333,13 @@
     fields, far = [], []
     for row in range(owned):
         field = call(
-            functools.partial(arrange_kernel, row), one, [vmem] + [free] * row
+            functools.partial(arrange_kernel, row),
+            one,
+            [hbm] + [free] * row,
+            scratch=[
+                pltpu.VMEM(orbitals.shape[1:], jnp.float32),
+                pltpu.SemaphoreType.DMA((PARTS,)),
+            ],
         )(orbitals, *fields)
         fields.append(field)
         far.append(rotated(field, "band", -2))
@@ -314,29 +347,32 @@
     flag = (band_index % 2).reshape(1)
     counts = pair_counts(pair_list, pair_count, owned, band_index, band_count)
 
-    def forward(base, after, other):
-        spectrum, moments, mine = call(
+    def forward(base, after, other, *earlier):
+        return call(
             functools.partial(forward_kernel, base),
             (
                 both,
                 jax.ShapeDtypeStruct((owned, chunks, 2) + shape[1:], jnp.float32),
-                jax.ShapeDtypeStruct((owned,) + shape[1:], jnp.float32),
+                jax.ShapeDtypeStruct(((1 + len(earlier)) * owned,) + shape[1:], jnp.float32),
             ),
-            [smem, free] + [vmem] * 5,
-        )(counts, after, own, other, right, left, decay)
-        return (other, spectrum, moments, mine, swapped(mine, "grid"))
-
-    def backward(base, after, state, total, inside=False):
+            [smem, free] + [vmem] * (5 + len(earlier)),
+        )(counts, after, own, other, right, left, decay, *earlier)
+
+    def exchanged(mine):
+        return swapped(mine, "grid")
+
+    def backward(base, after, state, total, inside=False, offset=0):
         return call(
-            functools.partial(backward_kernel, base, inside),
+            functools.partial(backward_kernel, base, inside, offset),
             both if inside else (both, one),
             [smem, free] + [vmem] * (9 + len(total)),
             scratch=[pltpu.VMEM((chunks, 2) + shape[1:], jnp.float32)],
         )(counts, after, own, *state, right, left, decay, *total)
 
     inner_base = REACH * owned * owned
-    inner = forward(inner_base, own, fields[1])
-    after = inner[3]
+    spectrum, moments, mine = forward(inner_base, own, fields[1])
+    inner = (fields[1], spectrum, moments, mine, exchanged(mine))
+    after = mine
     total, passed, arrived = (), [], []
     for row in range(owned):
         base = row * REACH * owned
@@ -345,8 +381,12 @@
         )
         near = swapped(picked, "band")
         distant_state = forward(base + owned, picked, far[row])
-        near_state = forward(base, distant_state[3], near)
-        acc, handed = backward(base, near_state[3], near_state, total)
+        near_state = forward(base, distant_state[2], near, distant_state[2])
+        mine = near_state[2]
+        ends = (mine, exchanged(mine))
+        near_state = (near,) + tuple(near_state[:2]) + ends
+        distant_state = (far[row],) + tuple(distant_state[:2]) + ends
+        acc, handed = backward(base, mine, near_state, total, offset=owned)
         handed_over = swapped(handed, "band")
         acc, distant = backward(base + owned, handed, distant_state, (acc,))
         total = (acc,)
@@ -366,9 +406,10 @@
             out,
             [smem] + [vmem] * 3 + [free] * len(earlier),
             out_specs=pl.BlockSpec(
-                (1,) + orbitals.shape[1:], functools.partial(lambda r, step: (r, 0, 0), row)
+                (1, slab_rows, plane_cells // PARTS),
+                functools.partial(lambda r, step: (r, 0, step), row),
             ),
-            grid=(1,),
+            grid=(PARTS,),
             aliases={4: 0} if earlier else {},
         )(flag, total, passed[row], arrived[row], *earlier)
     return result

time: 85.7 us -> 87.4 us (1.020)
  starting transfers between devices: 21.3 us -> 17.8 us
  waiting for transfers between devices: 47.9 us -> 50.7 us
  Pallas kernels: 13.3 us -> 15.1 us
    ppermute x4, waiting for transfers between devices: 32.3 us -> 38.3 us  [rotated(): return lax.ppermute(value, axis, pairs)]
    ppermute x9 -> x7, waiting for transfers between devices: 15.6 us -> 12.4 us  [swapped(): lax.ppermute(value, axis, [(source, source ^ 1) for source in range(count)])]
    ppermute x9 -> x7, starting transfers between devices: 8.02 us -> 4.95 us  [swapped(): lax.ppermute(value, axis, [(source, source ^ 1) for source in range(count)])]
  transfers between devices with their start and end apart: 13 -> 11, of which waited for: 11 -> 10; matrix products, arithmetic and copies ran while one was open for 0% -> 1% of each run, Pallas kernels for 10% -> 11%
where the time goes in v1:
time: 87.4 us; the launch traced here: 87.1 us
  waiting for transfers between devices  50.7 us (58%)
  starting transfers between devices  17.8 us (20%)
  Pallas kernels  15.1 us (17%)
  local copies, waits for them, and re-layouts  1.92 us (2%)
  between operations  0.93 us (1%)
    ppermute x4, waiting for transfers between devices, rotated(): return lax.ppermute(value, axis, pairs)  38.3 us
    ppermute x4, starting transfers between devices, rotated(): return lax.ppermute(value, axis, pairs)  12.8 us
    ppermute x7, waiting for transfers between devices, swapped(): lax.ppermute(value, axis, [(source, source ^ 1) for source in range(count)])  12.4 us
    ppermute x7, starting transfers between devices, swapped(): lax.ppermute(value, axis, [(source, source ^ 1) for source in range(count)])  4.95 us
    pallas_call x5, Pallas kernels, backward(): call(functools.partial(backward_kernel, base, inside, offset), both if in...  4.71 us
    pallas_call x5, Pallas kernels, forward(): call(functools.partial(forward_kernel, base), (both, jax.ShapeDtypeStruct...  4.36 us
    pallas_call x2, Pallas kernels, on_device(): call(functools.partial(restore_kernel, row), out, [smem] + [vmem] * 3 + [...  3.94 us
    unnamed x12, local copies, waits for them, and re-layouts  1.92 us
  transfers between devices with their start and end apart: 11, of which 10 were waited for; matrix products, arithmetic and copies ran while one was open for 1% of the time, Pallas kernels for 11%

profile of v1, /device:TPU:0, one launch (start us, length us, event | category | flops | bytes accessed | tf_op | source)
XLA Modules:
  0.0 87.1 jit_solution(194063793158603563)
XLA Ops:
  0.0 0.0 copy-start.2
  0.0 1.2 %copy-done.2 = f32[2,32,4096]{2,1,0:T(8,128)S(1)} copy-done((f32[2,32,4096]{2,1,0:T(8,128)S(1)}, f32[2,32,4096]{2,1,0:T(8,128)}, u32[]{:S(2)}) %copy-start.2) | copy-done | bytes 1048600
  1.2 0.0 copy-start.3
  1.2 0.9 %shard_map.64.refs_0_.first.own = f32[16,64,128]{2,1,0:T(8,128)S(1)} custom-call(f32[2,32,4096]{2,1,0:T(8,128)S(1)} %copy-done.2), custom_call_target="tpu_custom_call" | custom-call | bytes 1048576 | tf_op jit(solution)/shard_map/pallas_call | solution.py:335
  2.2 6.1 %collective-permute-start = (f32[16,64,128]{2,1,0:T(8,128)S(1)}, f32[16,64,128]{2,1,0:T(8,128)S(1)}, u32[]{:S(2)}, u32[]{:S(2)}) collective-permute-start(f32[16,64,128]{2,1,0:T(8,128)S(1)} %shard_map.64.refs_0_.first.own), channel_id=1, source_target_pairs={{0,28},{2,30},{4,0},{6,2},{8,4},{10,6},{12,8},{14,10},{16,12},{18,... | collective-permute-start | bytes 1572872 | tf_op jit(solution)/shard_map/ppermute | solution.py:19
  8.3 0.0 copy-done.3
  8.3 0.9 %shard_map.65.second.other.own = f32[16,64,128]{2,1,0:T(8,128)S(1)} custom-call(f32[2,32,4096]{2,1,0:T(8,128)S(1)} %copy-done.3, f32[16,64,128]{2,1,0:T(8,128)S(1)} %shard_map.64.refs_0_.first.own), custom_call_target="tpu_custom_call" | custom-call | bytes 1048576 | tf_op jit(solution)/shard_map/pallas_call | solution.py:335
  9.2 0.0 copy-start
  9.2 0.0 copy-start.1
  9.2 0.0 copy-start.4
  9.2 0.1 shard_map.66.after.own
  10.0 0.0 copy-start.5
  10.0 0.7 copy-done.5
  10.7 0.7 fusion
  11.4 0.0 copy-done
  11.4 0.0 copy-done.1
  11.4 0.0 copy-done.4
  11.4 0.7 shard_map.67
  12.1 7.4 %collective-permute-done.far.other = f32[16,64,128]{2,1,0:T(8,128)S(1)} collective-permute-done((f32[16,64,128]{2,1,0:T(8,128)S(1)}, f32[16,64,128]{2,1,0:T(8,128)S(1)}, u32[]{:S(2)}, u32[]{:S(2)}) %collective-permute-start) | collective-permute-done | bytes 524320 | tf_op jit(solution)/shard_map/ppermute | solution.py:19
  19.5 0.1 collective-permute-start.1
  19.6 0.7 shard_map.69
  20.2 1.2 %collective-permute-done.1.other = f32[16,64,128]{2,1,0:T(8,128)S(1)} collective-permute-done((f32[16,64,128]{2,1,0:T(8,128)S(1)}, f32[16,64,128]{2,1,0:T(8,128)S(1)}, u32[]{:S(2)}, u32[]{:S(2)}) %collective-permute-start.1) | collective-permute-done | bytes 524320 | tf_op jit(solution)/shard_map/ppermute | solution.py:24
  21.5 0.7 shard_map.70
  22.1 1.6 %collective-permute-start.2 = (f32[4,64,128]{2,1,0:T(8,128)S(1)}, f32[4,64,128]{2,1,0:T(8,128)S(1)}, u32[]{:S(2)}, u32[]{:S(2)}) collective-permute-start(f32[4,64,128]{2,1,0:T(8,128)S(1)} %get-tuple-element.30.after.mine), channel_id=1, source_target_pairs={{0,1},{1,0},{2,3},{3,2},{4,5},{5,4},{6,7},{7,6},{8,9},{9,8},{10,11... | collective-permute-start | bytes 393224 | tf_op jit(solution)/shard_map/ppermute | solution.py:24
  23.7 4.0 %collective-permute-done.2.arrived = f32[4,64,128]{2,1,0:T(8,128)S(1)} collective-permute-done((f32[4,64,128]{2,1,0:T(8,128)S(1)}, f32[4,64,128]{2,1,0:T(8,128)S(1)}, u32[]{:S(2)}, u32[]{:S(2)}) %collective-permute-start.2) | collective-permute-done | bytes 131104 | tf_op jit(solution)/shard_map/ppermute | solution.py:24
  27.7 0.8 shard_map.71
  28.5 0.1 collective-permute-start.3
  28.6 6.6 %collective-permute-start.4 = (f32[16,64,128]{2,1,0:T(8,128)S(1)}, f32[16,64,128]{2,1,0:T(8,128)S(1)}, u32[]{:S(2)}, u32[]{:S(2)}) collective-permute-start(f32[16,64,128]{2,1,0:T(8,128)S(1)} %shard_map.65.second.other.own), channel_id=1, source_target_pairs={{0,28},{2,30},{4,0},{6,2},{8,4},{10,6},{12,8},{14,10},{16,12},{18,... | collective-permute-start | bytes 1572872 | tf_op jit(solution)/shard_map/ppermute | solution.py:19
  35.2 0.8 shard_map.72
  36.0 0.0 collective-permute-done.3.handed.passed
  36.0 0.1 shard_map.73.after
  36.1 10.9 %collective-permute-done.4.far.other = f32[16,64,128]{2,1,0:T(8,128)S(1)} collective-permute-done((f32[16,64,128]{2,1,0:T(8,128)S(1)}, f32[16,64,128]{2,1,0:T(8,128)S(1)}, u32[]{:S(2)}, u32[]{:S(2)}) %collective-permute-start.4) | collective-permute-done | bytes 524320 | tf_op jit(solution)/shard_map/ppermute | solution.py:19
  47.0 0.1 collective-permute-start.5
  47.1 1.7 %shard_map.75 = (f32[2,16,64,128]{3,2,1,0:T(8,128)S(1)}, f32[2,2,2,64,128]{4,3,2,1,0:T(8,128)S(1)}, f32[2,64,128]{2,1,0:T(8,128)S(1)}) custom-call(s32[1]{0:T(128)} %bitcast.4.counts, f32[16,64,128]{2,1,0:T(8,128)S(1)} %shard_map.74.after, f32[2,16,64,128]{3,2,1,0:T(8,128)S(1)} %shard_map.66.after.own, f32[16,64,128]{2,1,0:T(8,128)S(1)} %collective-permute-done.4.far.other, ...), custom_call_target="tpu_custom_call" | custom-call | bytes 1048576 | tf_op jit(solution)/shard_map/pallas_call | solution.py:351
  48.8 0.2 collective-permute-done.5.other
  49.0 0.7 shard_map.76
  49.7 1.6 %collective-permute-start.6 = (f32[4,64,128]{2,1,0:T(8,128)S(1)}, f32[4,64,128]{2,1,0:T(8,128)S(1)}, u32[]{:S(2)}, u32[]{:S(2)}) collective-permute-start(f32[4,64,128]{2,1,0:T(8,128)S(1)} %get-tuple-element.39.after.mine), channel_id=1, source_target_pairs={{0,1},{1,0},{2,3},{3,2},{4,5},{5,4},{6,7},{7,6},{8,9},{9,8},{10,11... | collective-permute-start | bytes 393224 | tf_op jit(solution)/shard_map/ppermute | solution.py:24
  51.3 4.0 %collective-permute-done.6.arrived = f32[4,64,128]{2,1,0:T(8,128)S(1)} collective-permute-done((f32[4,64,128]{2,1,0:T(8,128)S(1)}, f32[4,64,128]{2,1,0:T(8,128)S(1)}, u32[]{:S(2)}, u32[]{:S(2)}) %collective-permute-start.6) | collective-permute-done | bytes 131104 | tf_op jit(solution)/shard_map/ppermute | solution.py:24
  55.3 0.8 shard_map.77
  56.1 0.1 collective-permute-start.7
  56.2 0.1 collective-permute-start.10
  56.2 1.7 %shard_map.78 = (f32[2,16,64,128]{3,2,1,0:T(8,128)S(1)}, f32[16,64,128]{2,1,0:T(8,128)S(1)}) custom-call(s32[1]{0:T(128)} %bitcast.4.counts, f32[16,64,128]{2,1,0:T(8,128)S(1)} %get-tuple-element.43.after, f32[2,16,64,128]{3,2,1,0:T(8,128)S(1)} %shard_map.66.after.own, f32[16,64,128]{2,1,0:T(8,128)S(1)} %collective-permute-done.4.far.other, ...), custom_call_target="tpu_custom_call" | custom-call | bytes 1048576 | tf_op jit(solution)/shard_map/pallas_call | solution.py:365
  57.9 0.1 collective-permute-done.7.handed.passed
  58.1 0.1 shard_map.79.after
  58.1 0.1 collective-permute-start.9
  58.2 1.6 %collective-permute-start.8 = (f32[2,64,128]{2,1,0:T(8,128)S(1)}, f32[2,64,128]{2,1,0:T(8,128)S(1)}, u32[]{:S(2)}, u32[]{:S(2)}) collective-permute-start(f32[2,64,128]{2,1,0:T(8,128)S(1)} %get-tuple-element.28.after.mine), channel_id=1, source_target_pairs={{0,1},{1,0},{2,3},{3,2},{4,5},{5,4},{6,7},{7,6},{8,9},{9,8},{10,11... | collective-permute-start | bytes 196616 | tf_op jit(solution)/shard_map/ppermute | solution.py:24
  59.7 2.8 %collective-permute-done.8.arrived = f32[2,64,128]{2,1,0:T(8,128)S(1)} collective-permute-done((f32[2,64,128]{2,1,0:T(8,128)S(1)}, f32[2,64,128]{2,1,0:T(8,128)S(1)}, u32[]{:S(2)}, u32[]{:S(2)}) %collective-permute-start.8) | collective-permute-done | bytes 65568 | tf_op jit(solution)/shard_map/ppermute | solution.py:24
  62.5 0.7 shard_map.80.own
  63.3 10.9 %collective-permute-done.10.arrived = f32[16,64,128]{2,1,0:T(8,128)S(1)} collective-permute-done((f32[16,64,128]{2,1,0:T(8,128)S(1)}, f32[16,64,128]{2,1,0:T(8,128)S(1)}, u32[]{:S(2)}, u32[]{:S(2)}) %collective-permute-start.10) | collective-permute-done | bytes 524320 | tf_op jit(solution)/shard_map/ppermute | solution.py:19
  74.2 2.0 %shard_map.81.refs_0_ = f32[2,32,4096]{2,1,0:T(8,128)} custom-call(s32[1]{0:T(128)} %bitcast.flag, f32[2,16,64,128]{3,2,1,0:T(8,128)S(1)} %shard_map.80.own, f32[16,64,128]{2,1,0:T(8,128)S(1)} %collective-permute-done.3.handed.passed, f32[16,64,128]{2,1,0:T(8,128)S(1)} %collective-permute-done.10.arrived), custom_call_target="tpu_custom_call" | custom-call | bytes 1048576 | tf_op jit(solution)/shard_map/pallas_call | solution.py:404
  76.1 9.0 %collective-permute-done.9.arrived = f32[16,64,128]{2,1,0:T(8,128)S(1)} collective-permute-done((f32[16,64,128]{2,1,0:T(8,128)S(1)}, f32[16,64,128]{2,1,0:T(8,128)S(1)}, u32[]{:S(2)}, u32[]{:S(2)}) %collective-permute-start.9) | collective-permute-done | bytes 524320 | tf_op jit(solution)/shard_map/ppermute | solution.py:19
  85.2 2.0 %shard_map.82 = f32[2,32,4096]{2,1,0:T(8,128)} custom-call(s32[1]{0:T(128)} %bitcast.flag, f32[2,16,64,128]{3,2,1,0:T(8,128)S(1)} %shard_map.80.own, f32[16,64,128]{2,1,0:T(8,128)S(1)} %collective-permute-done.7.handed.passed, f32[16,64,128]{2,1,0:T(8,128)S(1)} %collective-permute-done.9.arrived, ...), custom_call_target="tpu_custom_call", output_to_operand_aliasing={{}: (4, {})} | custom-call | bytes 1048576 | tf_op jit(solution)/shard_map/pallas_call | solution.py:404
  (2 shorter events, 0.1 us)
Async XLA Ops:
  0.0 1.2 %copy-start.2 = (f32[2,32,4096]{2,1,0:T(8,128)S(1)}, f32[2,32,4096]{2,1,0:T(8,128)}, u32[]{:S(2)}) copy-start(f32[2,32,4096]{2,1,0:T(8,128)} %source.3) | copy-start | bytes 3145732
  1.2 7.0 %copy-start.3 = (f32[2,32,4096]{2,1,0:T(8,128)S(1)}, f32[2,32,4096]{2,1,0:T(8,128)}, u32[]{:S(2)}) copy-start(f32[2,32,4096]{2,1,0:T(8,128)} %source.3) | copy-start | bytes 3145732
  2.2 17.3 %collective-permute-start = (f32[16,64,128]{2,1,0:T(8,128)S(1)}, f32[16,64,128]{2,1,0:T(8,128)S(1)}, u32[]{:S(2)}, u32[]{:S(2)}) collective-permute-start(f32[16,64,128]{2,1,0:T(8,128)S(1)} %shard_map.64.refs_0_.first.own), channel_id=1, source_target_pairs={{0,28},{2,30},{4,0},{6,2},{8,4},{10,6},{12,8},{14,10},{16,12},{18,... | collective-permute-start | bytes 1572872 | tf_op jit(solution)/shard_map/ppermute | solution.py:19
  9.2 2.2 %copy-start = (f32[5,64,128]{2,1,0:T(8,128)S(1)}, f32[5,64,128]{2,1,0:T(8,128)}, u32[]{:S(2)}) copy-start(f32[5,64,128]{2,1,0:T(8,128)} %constant.66.clone.decay) | copy-start | bytes 491524
  9.2 2.2 %copy-start.1 = (bf16[256,256]{1,0:T(8,128)(2,1)S(1)}, bf16[256,256]{1,0:T(8,128)(2,1)}, u32[]{:S(2)}) copy-start(bf16[256,256]{1,0:T(8,128)(2,1)} %constant.64.clone.right_ref) | copy-start | bytes 393220
  9.2 2.1 %copy-start.4 = (bf16[64,192]{1,0:T(8,128)(2,1)S(1)}, bf16[64,192]{1,0:T(8,128)(2,1)}, u32[]{:S(2)}) copy-start(bf16[64,192]{1,0:T(8,128)(2,1)} %constant.65.clone.left_ref) | copy-start | bytes 73732
  10.0 0.7 copy-start.5
  19.5 2.0 %collective-permute-start.1 = (f32[16,64,128]{2,1,0:T(8,128)S(1)}, f32[16,64,128]{2,1,0:T(8,128)S(1)}, u32[]{:S(2)}, u32[]{:S(2)}) collective-permute-start(f32[16,64,128]{2,1,0:T(8,128)S(1)} %shard_map.68.after), channel_id=1, source_target_pairs={{0,2},{2,0},{4,6},{6,4},{8,10},{10,8},{12,14},{14,12},{16,18},{18,... | collective-permute-start | bytes 1572872 | tf_op jit(solution)/shard_map/ppermute | solution.py:24
  22.1 5.6 %collective-permute-start.2 = (f32[4,64,128]{2,1,0:T(8,128)S(1)}, f32[4,64,128]{2,1,0:T(8,128)S(1)}, u32[]{:S(2)}, u32[]{:S(2)}) collective-permute-start(f32[4,64,128]{2,1,0:T(8,128)S(1)} %get-tuple-element.30.after.mine), channel_id=1, source_target_pairs={{0,1},{1,0},{2,3},{3,2},{4,5},{5,4},{6,7},{7,6},{8,9},{9,8},{10,11... | collective-permute-start | bytes 393224 | tf_op jit(solution)/shard_map/ppermute | solution.py:24
  28.5 7.5 %collective-permute-start.3 = (f32[16,64,128]{2,1,0:T(8,128)S(1)}, f32[16,64,128]{2,1,0:T(8,128)S(1)}, u32[]{:S(2)}, u32[]{:S(2)}) collective-permute-start(f32[16,64,128]{2,1,0:T(8,128)S(1)} %get-tuple-element.33.after), channel_id=1, source_target_pairs={{0,2},{2,0},{4,6},{6,4},{8,10},{10,8},{12,14},{14,12},{16,18},{18,... | collective-permute-start | bytes 1572872 | tf_op jit(solution)/shard_map/ppermute | solution.py:24
  28.6 18.4 %collective-permute-start.4 = (f32[16,64,128]{2,1,0:T(8,128)S(1)}, f32[16,64,128]{2,1,0:T(8,128)S(1)}, u32[]{:S(2)}, u32[]{:S(2)}) collective-permute-start(f32[16,64,128]{2,1,0:T(8,128)S(1)} %shard_map.65.second.other.own), channel_id=1, source_target_pairs={{0,28},{2,30},{4,0},{6,2},{8,4},{10,6},{12,8},{14,10},{16,12},{18,... | collective-permute-start | bytes 1572872 | tf_op jit(solution)/shard_map/ppermute | solution.py:19
  47.0 2.0 %collective-permute-start.5 = (f32[16,64,128]{2,1,0:T(8,128)S(1)}, f32[16,64,128]{2,1,0:T(8,128)S(1)}, u32[]{:S(2)}, u32[]{:S(2)}) collective-permute-start(f32[16,64,128]{2,1,0:T(8,128)S(1)} %shard_map.74.after), channel_id=1, source_target_pairs={{0,2},{2,0},{4,6},{6,4},{8,10},{10,8},{12,14},{14,12},{16,18},{18,... | collective-permute-start | bytes 1572872 | tf_op jit(solution)/shard_map/ppermute | solution.py:24
  49.7 5.6 %collective-permute-start.6 = (f32[4,64,128]{2,1,0:T(8,128)S(1)}, f32[4,64,128]{2,1,0:T(8,128)S(1)}, u32[]{:S(2)}, u32[]{:S(2)}) collective-permute-start(f32[4,64,128]{2,1,0:T(8,128)S(1)} %get-tuple-element.39.after.mine), channel_id=1, source_target_pairs={{0,1},{1,0},{2,3},{3,2},{4,5},{5,4},{6,7},{7,6},{8,9},{9,8},{10,11... | collective-permute-start | bytes 393224 | tf_op jit(solution)/shard_map/ppermute | solution.py:24
  56.1 2.0 %collective-permute-start.7 = (f32[16,64,128]{2,1,0:T(8,128)S(1)}, f32[16,64,128]{2,1,0:T(8,128)S(1)}, u32[]{:S(2)}, u32[]{:S(2)}) collective-permute-start(f32[16,64,128]{2,1,0:T(8,128)S(1)} %get-tuple-element.43.after), channel_id=1, source_target_pairs={{0,2},{2,0},{4,6},{6,4},{8,10},{10,8},{12,14},{14,12},{16,18},{18,... | collective-permute-start | bytes 1572872 | tf_op jit(solution)/shard_map/ppermute | solution.py:24
  56.2 18.0 %collective-permute-start.10 = (f32[16,64,128]{2,1,0:T(8,128)S(1)}, f32[16,64,128]{2,1,0:T(8,128)S(1)}, u32[]{:S(2)}, u32[]{:S(2)}) collective-permute-start(f32[16,64,128]{2,1,0:T(8,128)S(1)} %shard_map.73.after), channel_id=1, source_target_pairs={{0,4},{2,6},{4,8},{6,10},{8,12},{10,14},{12,16},{14,18},{16,20},{1... | collective-permute-start | bytes 1572872 | tf_op jit(solution)/shard_map/ppermute | solution.py:19
  58.1 27.0 %collective-permute-start.9 = (f32[16,64,128]{2,1,0:T(8,128)S(1)}, f32[16,64,128]{2,1,0:T(8,128)S(1)}, u32[]{:S(2)}, u32[]{:S(2)}) collective-permute-start(f32[16,64,128]{2,1,0:T(8,128)S(1)} %shard_map.79.after), channel_id=1, source_target_pairs={{0,4},{2,6},{4,8},{6,10},{8,12},{10,14},{12,16},{14,18},{16,20},{1... | collective-permute-start | bytes 1572872 | tf_op jit(solution)/shard_map/ppermute | solution.py:19
  58.2 4.3 %collective-permute-start.8 = (f32[2,64,128]{2,1,0:T(8,128)S(1)}, f32[2,64,128]{2,1,0:T(8,128)S(1)}, u32[]{:S(2)}, u32[]{:S(2)}) collective-permute-start(f32[2,64,128]{2,1,0:T(8,128)S(1)} %get-tuple-element.28.after.mine), channel_id=1, source_target_pairs={{0,1},{1,0},{2,3},{3,2},{4,5},{5,4},{6,7},{7,6},{8,9},{9,8},{10,11... | collective-permute-start | bytes 196616 | tf_op jit(solution)/shard_map/ppermute | solution.py:24

commit v2 on v1

--- a/solution.py
+++ b/solution.py
@@ -122,19 +122,18 @@
 
 
 def restore_kernel(row, flag, own, passed, arrived, *refs):
-    out = refs[-1]
-    _, slab_rows, cells = out.shape
+    out, raw, departures = refs[-3:]
+    slab_rows, cells = raw.shape
     width = own.shape[-1]
     half = slab_rows // 2
     lower = lax.broadcasted_iota(jnp.int32, (GROUP, width), 1) < width // 2
     weight = flag[0].astype(jnp.float32)
     tiles = 4
-
-    steps = cells // (width * tiles)
-    base = pl.program_id(0) * steps
+    parts = departures.shape[0]
+    part = cells // parts
 
     def tile_step(step, carry):
-        ys = pl.ds(pl.multiple_of((base + step) * 2 * tiles, 2 * tiles), 2 * tiles)
+        ys = pl.ds(pl.multiple_of(step * 2 * tiles, 2 * tiles), 2 * tiles)
         for start in range(0, half, GROUP):
             planes = pl.ds(start, GROUP)
             block = own[row, planes, ys, :] + weight * passed[planes, ys, :] + arrived[planes, ys, :]
@@ -142,11 +141,21 @@
             for k in range(tiles):
                 lanes = pl.ds(pl.multiple_of((step * tiles + k) * width, width), width)
                 even, odd = block[2 * k], block[2 * k + 1]
-                out[0, planes, lanes] = jnp.where(lower, even, halves(odd))
-                out[0, pl.ds(start + half, GROUP), lanes] = jnp.where(lower, halves(even), odd)
+                raw[planes, lanes] = jnp.where(lower, even, halves(odd))
+                raw[pl.ds(start + half, GROUP), lanes] = jnp.where(lower, halves(even), odd)
         return carry
 
-    lax.fori_loop(0, steps, tile_step, 0)
+    steps = part // (width * tiles)
+    copies = []
+    for k in range(parts):
+        lax.fori_loop(k * steps, (k + 1) * steps, tile_step, 0)
+        lanes = pl.ds(k * part, part)
+        copies.append(
+            pltpu.make_async_copy(raw.at[:, lanes], out.at[row, :, lanes], departures.at[k])
+        )
+        copies[-1].start()
+    for copy in copies:
+        copy.wait()
 
 
 def pick_kernel(flag, after, far, own, out):
@@ -315,13 +324,12 @@
     one = jax.ShapeDtypeStruct(shape, jnp.float32)
     both = jax.ShapeDtypeStruct((owned,) + shape, jnp.float32)
 
-    def call(kernel, out_shape, in_specs, out_specs=vmem, scratch=(), aliases={}, grid=()):
+    def call(kernel, out_shape, in_specs, out_specs=vmem, scratch=(), aliases={}):
         if isinstance(out_shape, tuple):
             out_specs = (vmem,) * len(out_shape)
         return pl.pallas_call(
             kernel,
             out_shape=out_shape,
-            grid=grid,
             in_specs=in_specs,
             out_specs=out_specs,
             scratch_shapes=scratch,
@@ -330,6 +338,7 @@
             cost_estimate=pl.CostEstimate(flops=0, bytes_accessed=1 << 20, transcendentals=0),
         )
 
+    source = pltpu.with_memory_space_constraint(orbitals, pltpu.HBM)
     fields, far = [], []
     for row in range(owned):
         field = call(
@@ -340,7 +349,7 @@
                 pltpu.VMEM(orbitals.shape[1:], jnp.float32),
                 pltpu.SemaphoreType.DMA((PARTS,)),
             ],
-        )(orbitals, *fields)
+        )(source, *fields)
         fields.append(field)
         far.append(rotated(field, "band", -2))
     own = call(stack_kernel, both, [vmem, vmem])(*fields)
@@ -373,14 +382,18 @@
     spectrum, moments, mine = forward(inner_base, own, fields[1])
     inner = (fields[1], spectrum, moments, mine, exchanged(mine))
     after = mine
-    total, passed, arrived = (), [], []
-    for row in range(owned):
-        base = row * REACH * owned
+
+    def brought(row, after):
         picked = call(pick_kernel, one, [smem, free, vmem, vmem])(
             flag, after, far[row], fields[row]
         )
-        near = swapped(picked, "band")
-        distant_state = forward(base + owned, picked, far[row])
+        return picked, swapped(picked, "band")
+
+    total, passed, arrived = (), [], []
+    after, near = brought(0, after)
+    for row in range(owned):
+        base = row * REACH * owned
+        distant_state = forward(base + owned, after, far[row])
         near_state = forward(base, distant_state[2], near, distant_state[2])
         mine = near_state[2]
         ends = (mine, exchanged(mine))
@@ -388,7 +401,10 @@
         distant_state = (far[row],) + tuple(distant_state[:2]) + ends
         acc, handed = backward(base, mine, near_state, total, offset=owned)
         handed_over = swapped(handed, "band")
-        acc, distant = backward(base + owned, handed, distant_state, (acc,))
+        after = handed
+        if row + 1 < owned:
+            after, near = brought(row + 1, handed)
+        acc, distant = backward(base + owned, after, distant_state, (acc,))
         total = (acc,)
         joined = call(join_kernel, one, [smem, free, vmem, vmem])(
             flag, distant, distant, handed_over
@@ -404,12 +420,12 @@
         result = call(
             functools.partial(restore_kernel, row),
             out,
-            [smem] + [vmem] * 3 + [free] * len(earlier),
-            out_specs=pl.BlockSpec(
-                (1, slab_rows, plane_cells // PARTS),
-                functools.partial(lambda r, step: (r, 0, step), row),
-            ),
-            grid=(PARTS,),
+            [smem] + [vmem] * 3 + [hbm] * len(earlier),
+            out_specs=hbm,
+            scratch=[
+                pltpu.VMEM(orbitals.shape[1:], jnp.float32),
+                pltpu.SemaphoreType.DMA((PARTS,)),
+            ],
             aliases={4: 0} if earlier else {},
         )(flag, total, passed[row], arrived[row], *earlier)
     return result

time: 87.4 us -> 76.1 us (0.87)
  waiting for transfers between devices: 50.7 us -> 40.8 us
  local copies, waits for them, and re-layouts: 1.92 us -> 0.69 us
  starting transfers between devices: 17.8 us -> 16.9 us
    ppermute x4, waiting for transfers between devices: 38.3 us -> 30.5 us  [rotated(): return lax.ppermute(value, axis, pairs)]
    ppermute x7, waiting for transfers between devices: 12.4 us -> 10.3 us  [swapped(): lax.ppermute(value, axis, [(source, source ^ 1) for source in range(count)])]
    pallas_call x2, Pallas kernels: 1.87 us -> 3.35 us  [on_device(): call(functools.partial(arrange_kernel, row), one, [hbm] + [free] * row, s...]
    unnamed x12 -> x8, local copies, waits for them, and re-layouts: 1.92 us -> 0.69 us
  transfers between devices with their start and end apart: 11 -> 11, of which waited for: 10 -> 7; matrix products, arithmetic and copies ran while one was open for 1% -> 1% of each run, Pallas kernels for 11% -> 15%
where the time goes in v2:
time: 76.1 us; the launch traced here: 75.8 us
  waiting for transfers between devices  40.8 us (54%)
  starting transfers between devices  16.9 us (22%)
  Pallas kernels  15.8 us (21%)
  between operations  0.95 us (1%)
    ppermute x4, waiting for transfers between devices, rotated(): return lax.ppermute(value, axis, pairs)  30.5 us
    ppermute x4, starting transfers between devices, rotated(): return lax.ppermute(value, axis, pairs)  12 us
    ppermute x7, waiting for transfers between devices, swapped(): lax.ppermute(value, axis, [(source, source ^ 1) for source in range(count)])  10.3 us
    ppermute x7, starting transfers between devices, swapped(): lax.ppermute(value, axis, [(source, source ^ 1) for source in range(count)])  4.89 us
    pallas_call x5, Pallas kernels, backward(): call(functools.partial(backward_kernel, base, inside, offset), both if in...  4.74 us
    pallas_call x5, Pallas kernels, forward(): call(functools.partial(forward_kernel, base), (both, jax.ShapeDtypeStruct...  4.38 us
    pallas_call x2, Pallas kernels, on_device(): call(functools.partial(arrange_kernel, row), one, [hbm] + [free] * row, s...  3.35 us
    pallas_call x2, Pallas kernels, on_device(): call(functools.partial(restore_kernel, row), out, [smem] + [vmem] * 3 + [...  3.09 us
  transfers between devices with their start and end apart: 11, of which 7 were waited for; matrix products, arithmetic and copies ran while one was open for 1% of the time, Pallas kernels for 15%

profile of v2, /device:TPU:0, one launch (start us, length us, event | category | flops | bytes accessed | tf_op | source)
XLA Modules:
  0.0 75.8 jit_solution(15064185533099313123)
XLA Ops:
  0.0 1.7 %shard_map.64.refs_0_.first.own = f32[16,64,128]{2,1,0:T(8,128)S(1)} custom-call(f32[2,32,4096]{2,1,0:T(8,128)} %source.3), custom_call_target="tpu_custom_call" | custom-call | bytes 1048576 | tf_op jit(solution)/shard_map/pallas_call | solution.py:344
  1.7 6.1 %collective-permute-start = (f32[16,64,128]{2,1,0:T(8,128)S(1)}, f32[16,64,128]{2,1,0:T(8,128)S(1)}, u32[]{:S(2)}, u32[]{:S(2)}) collective-permute-start(f32[16,64,128]{2,1,0:T(8,128)S(1)} %shard_map.64.refs_0_.first.own), channel_id=1, source_target_pairs={{0,28},{2,30},{4,0},{6,2},{8,4},{10,6},{12,8},{14,10},{16,12},{18,... | collective-permute-start | bytes 1572872 | tf_op jit(solution)/shard_map/ppermute | solution.py:19
  7.8 1.7 %shard_map.65.second.other.own = f32[16,64,128]{2,1,0:T(8,128)S(1)} custom-call(f32[2,32,4096]{2,1,0:T(8,128)} %source.3, f32[16,64,128]{2,1,0:T(8,128)S(1)} %shard_map.64.refs_0_.first.own), custom_call_target="tpu_custom_call" | custom-call | bytes 1048576 | tf_op jit(solution)/shard_map/pallas_call | solution.py:344
  9.5 0.0 copy-start
  9.5 0.0 copy-start.1
  9.5 0.0 copy-start.2
  9.5 0.1 shard_map.66.after.own
  10.3 0.0 copy-start.3
  10.3 0.7 copy-done.3
  11.0 0.7 fusion
  11.6 0.0 copy-done
  11.7 0.0 copy-done.1
  11.7 0.0 copy-done.2
  11.7 0.7 shard_map.67
  12.3 6.6 %collective-permute-done.far.other = f32[16,64,128]{2,1,0:T(8,128)S(1)} collective-permute-done((f32[16,64,128]{2,1,0:T(8,128)S(1)}, f32[16,64,128]{2,1,0:T(8,128)S(1)}, u32[]{:S(2)}, u32[]{:S(2)}) %collective-permute-start) | collective-permute-done | bytes 524320 | tf_op jit(solution)/shard_map/ppermute | solution.py:19
  19.0 0.1 collective-permute-start.1
  19.1 5.2 %collective-permute-start.3 = (f32[16,64,128]{2,1,0:T(8,128)S(1)}, f32[16,64,128]{2,1,0:T(8,128)S(1)}, u32[]{:S(2)}, u32[]{:S(2)}) collective-permute-start(f32[16,64,128]{2,1,0:T(8,128)S(1)} %shard_map.65.second.other.own), channel_id=1, source_target_pairs={{0,28},{2,30},{4,0},{6,2},{8,4},{10,6},{12,8},{14,10},{16,12},{18,... | collective-permute-start | bytes 1572872 | tf_op jit(solution)/shard_map/ppermute | solution.py:19
  24.3 0.7 shard_map.69
  25.0 0.0 collective-permute-done.1.other
  25.0 0.7 shard_map.70
  25.7 1.6 %collective-permute-start.2 = (f32[4,64,128]{2,1,0:T(8,128)S(1)}, f32[4,64,128]{2,1,0:T(8,128)S(1)}, u32[]{:S(2)}, u32[]{:S(2)}) collective-permute-start(f32[4,64,128]{2,1,0:T(8,128)S(1)} %get-tuple-element.30.after.mine), channel_id=1, source_target_pairs={{0,1},{1,0},{2,3},{3,2},{4,5},{5,4},{6,7},{7,6},{8,9},{9,8},{10,11... | collective-permute-start | bytes 393224 | tf_op jit(solution)/shard_map/ppermute | solution.py:24
  27.2 4.1 %collective-permute-done.2.arrived = f32[4,64,128]{2,1,0:T(8,128)S(1)} collective-permute-done((f32[4,64,128]{2,1,0:T(8,128)S(1)}, f32[4,64,128]{2,1,0:T(8,128)S(1)}, u32[]{:S(2)}, u32[]{:S(2)}) %collective-permute-start.2) | collective-permute-done | bytes 131104 | tf_op jit(solution)/shard_map/ppermute | solution.py:24
  31.3 0.8 %shard_map.71 = (f32[2,16,64,128]{3,2,1,0:T(8,128)S(1)}, f32[16,64,128]{2,1,0:T(8,128)S(1)}) custom-call(s32[1]{0:T(128)} %bitcast.4.counts, f32[4,64,128]{2,1,0:T(8,128)S(1)} %get-tuple-element.30.after.mine, f32[2,16,64,128]{3,2,1,0:T(8,128)S(1)} %shard_map.66.after.own, f32[16,64,128]{2,1,0:T(8,128)S(1)} %collective-permute-done.1.other, ...), custom_call_target="tpu_custom_call" | custom-call | bytes 1048576 | tf_op jit(solution)/shard_map/pallas_call | solution.py:374
  32.1 0.1 collective-permute-start.4
  32.2 3.9 %collective-permute-done.3.far.other = f32[16,64,128]{2,1,0:T(8,128)S(1)} collective-permute-done((f32[16,64,128]{2,1,0:T(8,128)S(1)}, f32[16,64,128]{2,1,0:T(8,128)S(1)}, u32[]{:S(2)}, u32[]{:S(2)}) %collective-permute-start.3) | collective-permute-done | bytes 524320 | tf_op jit(solution)/shard_map/ppermute | solution.py:19
  36.1 0.1 collective-permute-start.5
  36.2 0.8 %shard_map.73 = (f32[2,16,64,128]{3,2,1,0:T(8,128)S(1)}, f32[16,64,128]{2,1,0:T(8,128)S(1)}) custom-call(s32[1]{0:T(128)} %bitcast.4.counts, f32[16,64,128]{2,1,0:T(8,128)S(1)} %shard_map.72.after, f32[2,16,64,128]{3,2,1,0:T(8,128)S(1)} %shard_map.66.after.own, f32[16,64,128]{2,1,0:T(8,128)S(1)} %collective-permute-done.far.other, ...), custom_call_target="tpu_custom_call" | custom-call | bytes 1048576 | tf_op jit(solution)/shard_map/pallas_call | solution.py:374
  37.0 0.0 collective-permute-done.4.handed.passed
  37.0 0.1 shard_map.74.after
  37.1 1.7 %shard_map.75 = (f32[2,16,64,128]{3,2,1,0:T(8,128)S(1)}, f32[2,2,2,64,128]{4,3,2,1,0:T(8,128)S(1)}, f32[2,64,128]{2,1,0:T(8,128)S(1)}) custom-call(s32[1]{0:T(128)} %bitcast.4.counts, f32[16,64,128]{2,1,0:T(8,128)S(1)} %shard_map.74.after, f32[2,16,64,128]{3,2,1,0:T(8,128)S(1)} %shard_map.66.after.own, f32[16,64,128]{2,1,0:T(8,128)S(1)} %collective-permute-done.3.far.other, ...), custom_call_target="tpu_custom_call" | custom-call | bytes 1048576 | tf_op jit(solution)/shard_map/pallas_call | solution.py:360
  38.8 0.0 collective-permute-done.5.other
  38.8 0.7 shard_map.76
  39.5 1.6 %collective-permute-start.6 = (f32[4,64,128]{2,1,0:T(8,128)S(1)}, f32[4,64,128]{2,1,0:T(8,128)S(1)}, u32[]{:S(2)}, u32[]{:S(2)}) collective-permute-start(f32[4,64,128]{2,1,0:T(8,128)S(1)} %get-tuple-element.39.after.mine), channel_id=1, source_target_pairs={{0,1},{1,0},{2,3},{3,2},{4,5},{5,4},{6,7},{7,6},{8,9},{9,8},{10,11... | collective-permute-start | bytes 393224 | tf_op jit(solution)/shard_map/ppermute | solution.py:24
  41.0 3.5 %collective-permute-done.6.arrived = f32[4,64,128]{2,1,0:T(8,128)S(1)} collective-permute-done((f32[4,64,128]{2,1,0:T(8,128)S(1)}, f32[4,64,128]{2,1,0:T(8,128)S(1)}, u32[]{:S(2)}, u32[]{:S(2)}) %collective-permute-start.6) | collective-permute-done | bytes 131104 | tf_op jit(solution)/shard_map/ppermute | solution.py:24
  44.5 0.8 %shard_map.77 = (f32[2,16,64,128]{3,2,1,0:T(8,128)S(1)}, f32[16,64,128]{2,1,0:T(8,128)S(1)}) custom-call(s32[1]{0:T(128)} %bitcast.4.counts, f32[4,64,128]{2,1,0:T(8,128)S(1)} %get-tuple-element.39.after.mine, f32[2,16,64,128]{3,2,1,0:T(8,128)S(1)} %shard_map.66.after.own, f32[16,64,128]{2,1,0:T(8,128)S(1)} %collective-permute-done.5.other, ...), custom_call_target="tpu_custom_call" | custom-call | bytes 1048576 | tf_op jit(solution)/shard_map/pallas_call | solution.py:374
  45.3 0.1 collective-permute-start.7
  45.4 0.5 collective-permute-start.10
  45.8 1.7 %shard_map.78 = (f32[2,16,64,128]{3,2,1,0:T(8,128)S(1)}, f32[16,64,128]{2,1,0:T(8,128)S(1)}) custom-call(s32[1]{0:T(128)} %bitcast.4.counts, f32[16,64,128]{2,1,0:T(8,128)S(1)} %get-tuple-element.43.after, f32[2,16,64,128]{3,2,1,0:T(8,128)S(1)} %shard_map.66.after.own, f32[16,64,128]{2,1,0:T(8,128)S(1)} %collective-permute-done.3.far.other, ...), custom_call_target="tpu_custom_call" | custom-call | bytes 1048576 | tf_op jit(solution)/shard_map/pallas_call | solution.py:374
  47.5 0.0 collective-permute-done.7.handed.passed
  47.6 0.1 shard_map.79.after
  47.6 0.2 collective-permute-start.9
  47.8 1.5 %collective-permute-start.8 = (f32[2,64,128]{2,1,0:T(8,128)S(1)}, f32[2,64,128]{2,1,0:T(8,128)S(1)}, u32[]{:S(2)}, u32[]{:S(2)}) collective-permute-start(f32[2,64,128]{2,1,0:T(8,128)S(1)} %get-tuple-element.28.after.mine), channel_id=1, source_target_pairs={{0,1},{1,0},{2,3},{3,2},{4,5},{5,4},{6,7},{7,6},{8,9},{9,8},{10,11... | collective-permute-start | bytes 196616 | tf_op jit(solution)/shard_map/ppermute | solution.py:24
  49.3 2.8 %collective-permute-done.8.arrived = f32[2,64,128]{2,1,0:T(8,128)S(1)} collective-permute-done((f32[2,64,128]{2,1,0:T(8,128)S(1)}, f32[2,64,128]{2,1,0:T(8,128)S(1)}, u32[]{:S(2)}, u32[]{:S(2)}) %collective-permute-start.8) | collective-permute-done | bytes 65568 | tf_op jit(solution)/shard_map/ppermute | solution.py:24
  52.1 0.7 shard_map.80.own
  52.8 10.5 %collective-permute-done.10.arrived = f32[16,64,128]{2,1,0:T(8,128)S(1)} collective-permute-done((f32[16,64,128]{2,1,0:T(8,128)S(1)}, f32[16,64,128]{2,1,0:T(8,128)S(1)}, u32[]{:S(2)}, u32[]{:S(2)}) %collective-permute-start.10) | collective-permute-done | bytes 524320 | tf_op jit(solution)/shard_map/ppermute | solution.py:19
  63.3 1.5 %shard_map.81.refs_0_ = f32[2,32,4096]{2,1,0:T(8,128)} custom-call(s32[1]{0:T(128)} %bitcast.flag, f32[2,16,64,128]{3,2,1,0:T(8,128)S(1)} %shard_map.80.own, f32[16,64,128]{2,1,0:T(8,128)S(1)} %collective-permute-done.4.handed.passed, f32[16,64,128]{2,1,0:T(8,128)S(1)} %collective-permute-done.10.arrived), custom_call_target="tpu_custom_call" | custom-call | bytes 1048576 | tf_op jit(solution)/shard_map/pallas_call | solution.py:420
  64.9 9.4 %collective-permute-done.9.arrived = f32[16,64,128]{2,1,0:T(8,128)S(1)} collective-permute-done((f32[16,64,128]{2,1,0:T(8,128)S(1)}, f32[16,64,128]{2,1,0:T(8,128)S(1)}, u32[]{:S(2)}, u32[]{:S(2)}) %collective-permute-start.9) | collective-permute-done | bytes 524320 | tf_op jit(solution)/shard_map/ppermute | solution.py:19
  74.3 1.5 %shard_map.82 = f32[2,32,4096]{2,1,0:T(8,128)} custom-call(s32[1]{0:T(128)} %bitcast.flag, f32[2,16,64,128]{3,2,1,0:T(8,128)S(1)} %shard_map.80.own, f32[16,64,128]{2,1,0:T(8,128)S(1)} %collective-permute-done.7.handed.passed, f32[16,64,128]{2,1,0:T(8,128)S(1)} %collective-permute-done.9.arrived, ...), custom_call_target="tpu_custom_call", output_to_operand_aliasing={{}: (4, {})} | custom-call | bytes 1048576 | tf_op jit(solution)/shard_map/pallas_call | solution.py:420
  (2 shorter events, 0.1 us)
Async XLA Ops:
  1.7 17.3 %collective-permute-start = (f32[16,64,128]{2,1,0:T(8,128)S(1)}, f32[16,64,128]{2,1,0:T(8,128)S(1)}, u32[]{:S(2)}, u32[]{:S(2)}) collective-permute-start(f32[16,64,128]{2,1,0:T(8,128)S(1)} %shard_map.64.refs_0_.first.own), channel_id=1, source_target_pairs={{0,28},{2,30},{4,0},{6,2},{8,4},{10,6},{12,8},{14,10},{16,12},{18,... | collective-permute-start | bytes 1572872 | tf_op jit(solution)/shard_map/ppermute | solution.py:19
  9.5 2.2 %copy-start = (f32[5,64,128]{2,1,0:T(8,128)S(1)}, f32[5,64,128]{2,1,0:T(8,128)}, u32[]{:S(2)}) copy-start(f32[5,64,128]{2,1,0:T(8,128)} %constant.66.clone.decay) | copy-start | bytes 491524
  9.5 2.2 %copy-start.1 = (bf16[256,256]{1,0:T(8,128)(2,1)S(1)}, bf16[256,256]{1,0:T(8,128)(2,1)}, u32[]{:S(2)}) copy-start(bf16[256,256]{1,0:T(8,128)(2,1)} %constant.64.clone.right_ref) | copy-start | bytes 393220
  9.5 2.2 %copy-start.2 = (bf16[64,192]{1,0:T(8,128)(2,1)S(1)}, bf16[64,192]{1,0:T(8,128)(2,1)}, u32[]{:S(2)}) copy-start(bf16[64,192]{1,0:T(8,128)(2,1)} %constant.65.clone.left_ref) | copy-start | bytes 73732
  10.3 0.7 copy-start.3
  19.0 6.0 %collective-permute-start.1 = (f32[16,64,128]{2,1,0:T(8,128)S(1)}, f32[16,64,128]{2,1,0:T(8,128)S(1)}, u32[]{:S(2)}, u32[]{:S(2)}) collective-permute-start(f32[16,64,128]{2,1,0:T(8,128)S(1)} %shard_map.68.after), channel_id=1, source_target_pairs={{0,2},{2,0},{4,6},{6,4},{8,10},{10,8},{12,14},{14,12},{16,18},{18,... | collective-permute-start | bytes 1572872 | tf_op jit(solution)/shard_map/ppermute | solution.py:24
  19.1 17.0 %collective-permute-start.3 = (f32[16,64,128]{2,1,0:T(8,128)S(1)}, f32[16,64,128]{2,1,0:T(8,128)S(1)}, u32[]{:S(2)}, u32[]{:S(2)}) collective-permute-start(f32[16,64,128]{2,1,0:T(8,128)S(1)} %shard_map.65.second.other.own), channel_id=1, source_target_pairs={{0,28},{2,30},{4,0},{6,2},{8,4},{10,6},{12,8},{14,10},{16,12},{18,... | collective-permute-start | bytes 1572872 | tf_op jit(solution)/shard_map/ppermute | solution.py:19
  25.7 5.6 %collective-permute-start.2 = (f32[4,64,128]{2,1,0:T(8,128)S(1)}, f32[4,64,128]{2,1,0:T(8,128)S(1)}, u32[]{:S(2)}, u32[]{:S(2)}) collective-permute-start(f32[4,64,128]{2,1,0:T(8,128)S(1)} %get-tuple-element.30.after.mine), channel_id=1, source_target_pairs={{0,1},{1,0},{2,3},{3,2},{4,5},{5,4},{6,7},{7,6},{8,9},{9,8},{10,11... | collective-permute-start | bytes 393224 | tf_op jit(solution)/shard_map/ppermute | solution.py:24
  32.1 4.9 %collective-permute-start.4 = (f32[16,64,128]{2,1,0:T(8,128)S(1)}, f32[16,64,128]{2,1,0:T(8,128)S(1)}, u32[]{:S(2)}, u32[]{:S(2)}) collective-permute-start(f32[16,64,128]{2,1,0:T(8,128)S(1)} %get-tuple-element.33.after), channel_id=1, source_target_pairs={{0,2},{2,0},{4,6},{6,4},{8,10},{10,8},{12,14},{14,12},{16,18},{18,... | collective-permute-start | bytes 1572872 | tf_op jit(solution)/shard_map/ppermute | solution.py:24
  36.1 2.6 %collective-permute-start.5 = (f32[16,64,128]{2,1,0:T(8,128)S(1)}, f32[16,64,128]{2,1,0:T(8,128)S(1)}, u32[]{:S(2)}, u32[]{:S(2)}) collective-permute-start(f32[16,64,128]{2,1,0:T(8,128)S(1)} %shard_map.72.after), channel_id=1, source_target_pairs={{0,2},{2,0},{4,6},{6,4},{8,10},{10,8},{12,14},{14,12},{16,18},{18,... | collective-permute-start | bytes 1572872 | tf_op jit(solution)/shard_map/ppermute | solution.py:24
  39.5 5.0 %collective-permute-start.6 = (f32[4,64,128]{2,1,0:T(8,128)S(1)}, f32[4,64,128]{2,1,0:T(8,128)S(1)}, u32[]{:S(2)}, u32[]{:S(2)}) collective-permute-start(f32[4,64,128]{2,1,0:T(8,128)S(1)} %get-tuple-element.39.after.mine), channel_id=1, source_target_pairs={{0,1},{1,0},{2,3},{3,2},{4,5},{5,4},{6,7},{7,6},{8,9},{9,8},{10,11... | collective-permute-start | bytes 393224 | tf_op jit(solution)/shard_map/ppermute | solution.py:24
  45.3 2.3 %collective-permute-start.7 = (f32[16,64,128]{2,1,0:T(8,128)S(1)}, f32[16,64,128]{2,1,0:T(8,128)S(1)}, u32[]{:S(2)}, u32[]{:S(2)}) collective-permute-start(f32[16,64,128]{2,1,0:T(8,128)S(1)} %get-tuple-element.43.after), channel_id=1, source_target_pairs={{0,2},{2,0},{4,6},{6,4},{8,10},{10,8},{12,14},{14,12},{16,18},{18,... | collective-permute-start | bytes 1572872 | tf_op jit(solution)/shard_map/ppermute | solution.py:24
  45.4 17.9 %collective-permute-start.10 = (f32[16,64,128]{2,1,0:T(8,128)S(1)}, f32[16,64,128]{2,1,0:T(8,128)S(1)}, u32[]{:S(2)}, u32[]{:S(2)}) collective-permute-start(f32[16,64,128]{2,1,0:T(8,128)S(1)} %shard_map.74.after), channel_id=1, source_target_pairs={{0,4},{2,6},{4,8},{6,10},{8,12},{10,14},{12,16},{14,18},{16,20},{1... | collective-permute-start | bytes 1572872 | tf_op jit(solution)/shard_map/ppermute | solution.py:19
  47.6 26.7 %collective-permute-start.9 = (f32[16,64,128]{2,1,0:T(8,128)S(1)}, f32[16,64,128]{2,1,0:T(8,128)S(1)}, u32[]{:S(2)}, u32[]{:S(2)}) collective-permute-start(f32[16,64,128]{2,1,0:T(8,128)S(1)} %shard_map.79.after), channel_id=1, source_target_pairs={{0,4},{2,6},{4,8},{6,10},{8,12},{10,14},{12,16},{14,18},{16,20},{1... | collective-permute-start | bytes 1572872 | tf_op jit(solution)/shard_map/ppermute | solution.py:19
  47.8 4.3 %collective-permute-start.8 = (f32[2,64,128]{2,1,0:T(8,128)S(1)}, f32[2,64,128]{2,1,0:T(8,128)S(1)}, u32[]{:S(2)}, u32[]{:S(2)}) collective-permute-start(f32[2,64,128]{2,1,0:T(8,128)S(1)} %get-tuple-element.28.after.mine), channel_id=1, source_target_pairs={{0,1},{1,0},{2,3},{3,2},{4,5},{5,4},{6,7},{7,6},{8,9},{9,8},{10,11... | collective-permute-start | bytes 196616 | tf_op jit(solution)/shard_map/ppermute | solution.py:24

commit v3 on v2

--- a/solution.py
+++ b/solution.py
@@ -184,10 +184,7 @@
 
 
 def forward_kernel(base, counts, after, own, other, right_ref, left_ref, decay, *refs):
-    spectrum, moments, mine = refs[-3:]
-    offset = mine.shape[0] - own.shape[0]
-    if offset:
-        mine[:offset] = refs[0][...]
+    spectrum, moments, mine = refs
     owned, rows, side, width = own.shape
     chunks = rows // GROUP
     lower = lax.broadcasted_iota(jnp.int32, (side, width), 1) < width // 2
@@ -219,7 +216,7 @@
         def _():
             power = decay[1]
             ahead, behind = slab_moments(moments, i, decay[4])
-            mine[offset + i] = jnp.where(lower, behind + power * halves(behind), ahead + power * halves(ahead))
+            mine[i] = jnp.where(lower, behind + power * halves(behind), ahead + power * halves(ahead))
 
         return carry
 
@@ -227,7 +224,7 @@
 
 
 def backward_kernel(
-    base, inside, offset, counts, after, own, other, spectrum, moments, mine, arrived,
+    base, inside, counts, after, own, other, spectrum, moments, mine, arrived,
     right_ref, left_ref, decay, *refs
 ):
     edge = refs[-1]
@@ -249,7 +246,7 @@
         def _():
             power, reach = decay[1], decay[4]
             ahead_all, behind_all = slab_moments(moments, i, reach)
-            entering = (arrived[offset + i] + power * power * mine[offset + i]) * decay[3]
+            entering = (arrived[i] + power * power * mine[i]) * decay[3]
             turned = halves(entering)
             ahead = jnp.where(lower, turned, halves(ahead_all) + power * entering)
             behind = jnp.where(lower, halves(behind_all) + power * entering, turned)
@@ -299,11 +296,11 @@
     inside = (REACH * owned) * owned
     place = ((partner % owned) * REACH + distance - 1) * owned + first
     place = jnp.where(distance == 0, inside, place)
-    return jnp.sum(jnp.where(live, lax.shift_left(1, DIGIT * place), 0)).reshape(1)
+    return jnp.sum(jnp.where(live, lax.shift_left(1, DIGIT * place), 0))
 
 
 def count_at(counts, place):
-    return lax.shift_right_logical(counts[0], DIGIT * place) & (2**DIGIT - 1)
+    return lax.shift_right_logical(counts[0], 1 + DIGIT * place) & (2**DIGIT - 1)
 
 
 def on_device(orbitals, pair_list, pair_count):
@@ -355,24 +352,25 @@
     own = call(stack_kernel, both, [vmem, vmem])(*fields)
     flag = (band_index % 2).reshape(1)
     counts = pair_counts(pair_list, pair_count, owned, band_index, band_count)
-
-    def forward(base, after, other, *earlier):
+    counts = (lax.optimization_barrier(counts) * 2 + band_index % 2).reshape(1)
+
+    def forward(base, after, other):
         return call(
             functools.partial(forward_kernel, base),
             (
                 both,
                 jax.ShapeDtypeStruct((owned, chunks, 2) + shape[1:], jnp.float32),
-                jax.ShapeDtypeStruct(((1 + len(earlier)) * owned,) + shape[1:], jnp.float32),
+                jax.ShapeDtypeStruct((owned,) + shape[1:], jnp.float32),
             ),
-            [smem, free] + [vmem] * (5 + len(earlier)),
-        )(counts, after, own, other, right, left, decay, *earlier)
+            [smem, free] + [vmem] * 5,
+        )(counts, after, own, other, right, left, decay)
 
     def exchanged(mine):
         return swapped(mine, "grid")
 
-    def backward(base, after, state, total, inside=False, offset=0):
+    def backward(base, after, state, total, inside=False):
         return call(
-            functools.partial(backward_kernel, base, inside, offset),
+            functools.partial(backward_kernel, base, inside),
             both if inside else (both, one),
             [smem, free] + [vmem] * (9 + len(total)),
             scratch=[pltpu.VMEM((chunks, 2) + shape[1:], jnp.float32)],
@@ -394,12 +392,12 @@
     for row in range(owned):
         base = row * REACH * owned
         distant_state = forward(base + owned, after, far[row])
-        near_state = forward(base, distant_state[2], near, distant_state[2])
+        distant_ends = exchanged(distant_state[2])
+        near_state = forward(base, distant_state[2], near)
         mine = near_state[2]
-        ends = (mine, exchanged(mine))
-        near_state = (near,) + tuple(near_state[:2]) + ends
-        distant_state = (far[row],) + tuple(distant_state[:2]) + ends
-        acc, handed = backward(base, mine, near_state, total, offset=owned)
+        near_state = (near,) + tuple(near_state) + (exchanged(mine),)
+        distant_state = (far[row],) + tuple(distant_state) + (distant_ends,)
+        acc, handed = backward(base, mine, near_state, total)
         handed_over = swapped(handed, "band")
         after = handed
         if row + 1 < owned:

time: 76.1 us -> 78.5 us (1.032)
  Pallas kernels: 15.8 us -> 9.41 us
  waiting for transfers between devices: 40.8 us -> 45.3 us
  starting transfers between devices: 16.9 us -> 19.9 us
  local copies, waits for them, and re-layouts: 0.69 us -> 1.55 us
    ppermute x7 -> x9, waiting for transfers between devices: 10.3 us -> 13.8 us  [swapped(): lax.ppermute(value, axis, [(source, source ^ 1) for source in range(count)])]
    pallas_call x5, Pallas kernels: 4.38 us -> 1.12 us  [forward(): call(functools.partial(forward_kernel, base), (both, jax.ShapeDtypeStruct...]
    ppermute x7 -> x9, starting transfers between devices: 4.89 us -> 8.08 us  [swapped(): lax.ppermute(value, axis, [(source, source ^ 1) for source in range(count)])]
    pallas_call x5, Pallas kernels: 4.74 us -> 1.58 us  [backward(): call(functools.partial(backward_kernel, base, inside), both if inside els...]
    ppermute x4, waiting for transfers between devices: 30.5 us -> 31.5 us  [rotated(): return lax.ppermute(value, axis, pairs)]
    unnamed x8, local copies, waits for them, and re-layouts: 0.69 us -> 1.55 us
  transfers between devices with their start and end apart: 11 -> 13, of which waited for: 7 -> 9; matrix products, arithmetic and copies ran while one was open for 1% -> 1% of each run, Pallas kernels for 15% -> 8%
where the time goes in v3:
time: 78.5 us; the launch traced here: 78.3 us
  waiting for transfers between devices  45.3 us (58%)
  starting transfers between devices  19.9 us (25%)
  Pallas kernels  9.41 us (12%)
  local copies, waits for them, and re-layouts  1.55 us (2%)
  between operations  1.51 us (2%)
    ppermute x4, waiting for transfers between devices, rotated(): return lax.ppermute(value, axis, pairs)  31.5 us
    ppermute x9, waiting for transfers between devices, swapped(): lax.ppermute(value, axis, [(source, source ^ 1) for source in range(count)])  13.8 us
    ppermute x4, starting transfers between devices, rotated(): return lax.ppermute(value, axis, pairs)  11.8 us
    ppermute x9, starting transfers between devices, swapped(): lax.ppermute(value, axis, [(source, source ^ 1) for source in range(count)])  8.08 us
    pallas_call x2, Pallas kernels, on_device(): call(functools.partial(arrange_kernel, row), one, [hbm] + [free] * row, s...  3.35 us
    pallas_call x2, Pallas kernels, on_device(): call(functools.partial(restore_kernel, row), out, [smem] + [vmem] * 3 + [...  3.09 us
    pallas_call x5, Pallas kernels, backward(): call(functools.partial(backward_kernel, base, inside), both if inside els...  1.58 us
  transfers between devices with their start and end apart: 13, of which 9 were waited for; matrix products, arithmetic and copies ran while one was open for 1% of the time, Pallas kernels for 8%

profile of v3, /device:TPU:0, one launch (start us, length us, event | category | flops | bytes accessed | tf_op | source)
XLA Modules:
  0.0 78.3 jit_solution(553201872028772625)
XLA Ops:
  0.0 1.7 %shard_map.64.refs_0_.first.own = f32[16,64,128]{2,1,0:T(8,128)S(1)} custom-call(f32[2,32,4096]{2,1,0:T(8,128)} %source.3), custom_call_target="tpu_custom_call" | custom-call | bytes 1048576 | tf_op jit(solution)/shard_map/pallas_call | solution.py:341
  1.7 6.1 %collective-permute-start = (f32[16,64,128]{2,1,0:T(8,128)S(1)}, f32[16,64,128]{2,1,0:T(8,128)S(1)}, u32[]{:S(2)}, u32[]{:S(2)}) collective-permute-start(f32[16,64,128]{2,1,0:T(8,128)S(1)} %shard_map.64.refs_0_.first.own), channel_id=1, source_target_pairs={{0,28},{2,30},{4,0},{6,2},{8,4},{10,6},{12,8},{14,10},{16,12},{18,... | collective-permute-start | bytes 1572872 | tf_op jit(solution)/shard_map/ppermute | solution.py:19
  7.8 1.7 %shard_map.65.second.other.own = f32[16,64,128]{2,1,0:T(8,128)S(1)} custom-call(f32[2,32,4096]{2,1,0:T(8,128)} %source.3, f32[16,64,128]{2,1,0:T(8,128)S(1)} %shard_map.64.refs_0_.first.own), custom_call_target="tpu_custom_call" | custom-call | bytes 1048576 | tf_op jit(solution)/shard_map/pallas_call | solution.py:341
  10.1 0.0 copy-start.3
  10.1 0.7 copy-done.3
  10.8 0.7 fusion
  12.1 0.0 copy-start
  12.1 0.0 copy-start.1
  12.2 0.0 copy-start.2
  12.2 0.1 shard_map.66.after.own
  12.3 0.8 %copy-done = f32[5,64,128]{2,1,0:T(8,128)S(1)} copy-done((f32[5,64,128]{2,1,0:T(8,128)S(1)}, f32[5,64,128]{2,1,0:T(8,128)}, u32[]{:S(2)}) %copy-start) | copy-done | bytes 163864
  13.1 0.1 copy-done.1
  13.1 0.0 copy-done.2
  13.1 5.8 %collective-permute-done.far.other = f32[16,64,128]{2,1,0:T(8,128)S(1)} collective-permute-done((f32[16,64,128]{2,1,0:T(8,128)S(1)}, f32[16,64,128]{2,1,0:T(8,128)S(1)}, u32[]{:S(2)}, u32[]{:S(2)}) %collective-permute-start) | collective-permute-done | bytes 524320 | tf_op jit(solution)/shard_map/ppermute | solution.py:19
  19.0 0.1 collective-permute-start.1
  19.1 5.2 %collective-permute-start.3 = (f32[16,64,128]{2,1,0:T(8,128)S(1)}, f32[16,64,128]{2,1,0:T(8,128)S(1)}, u32[]{:S(2)}, u32[]{:S(2)}) collective-permute-start(f32[16,64,128]{2,1,0:T(8,128)S(1)} %shard_map.65.second.other.own), channel_id=1, source_target_pairs={{0,28},{2,30},{4,0},{6,2},{8,4},{10,6},{12,8},{14,10},{16,12},{18,... | collective-permute-start | bytes 1572872 | tf_op jit(solution)/shard_map/ppermute | solution.py:19
  24.3 0.0 collective-permute-done.1.other
  24.3 1.6 %collective-permute-start.2 = (f32[2,64,128]{2,1,0:T(8,128)S(1)}, f32[2,64,128]{2,1,0:T(8,128)S(1)}, u32[]{:S(2)}, u32[]{:S(2)}) collective-permute-start(f32[2,64,128]{2,1,0:T(8,128)S(1)} %get-tuple-element.30.after.mine), channel_id=1, source_target_pairs={{0,1},{1,0},{2,3},{3,2},{4,5},{5,4},{6,7},{7,6},{8,9},{9,8},{10,11... | collective-permute-start | bytes 196616 | tf_op jit(solution)/shard_map/ppermute | solution.py:24
  25.9 2.8 %collective-permute-done.2.arrived = f32[2,64,128]{2,1,0:T(8,128)S(1)} collective-permute-done((f32[2,64,128]{2,1,0:T(8,128)S(1)}, f32[2,64,128]{2,1,0:T(8,128)S(1)}, u32[]{:S(2)}, u32[]{:S(2)}) %collective-permute-start.2) | collective-permute-done | bytes 65568 | tf_op jit(solution)/shard_map/ppermute | solution.py:24
  28.7 0.1 shard_map.71
  28.8 0.1 collective-permute-start.5
  28.9 7.2 %collective-permute-done.3.far.other = f32[16,64,128]{2,1,0:T(8,128)S(1)} collective-permute-done((f32[16,64,128]{2,1,0:T(8,128)S(1)}, f32[16,64,128]{2,1,0:T(8,128)S(1)}, u32[]{:S(2)}, u32[]{:S(2)}) %collective-permute-start.3) | collective-permute-done | bytes 524320 | tf_op jit(solution)/shard_map/ppermute | solution.py:19
  36.1 0.1 collective-permute-start.6
  36.2 1.6 %collective-permute-start.4 = (f32[2,64,128]{2,1,0:T(8,128)S(1)}, f32[2,64,128]{2,1,0:T(8,128)S(1)}, u32[]{:S(2)}, u32[]{:S(2)}) collective-permute-start(f32[2,64,128]{2,1,0:T(8,128)S(1)} %get-tuple-element.29.after.mine), channel_id=1, source_target_pairs={{0,1},{1,0},{2,3},{3,2},{4,5},{5,4},{6,7},{7,6},{8,9},{9,8},{10,11... | collective-permute-start | bytes 196616 | tf_op jit(solution)/shard_map/ppermute | solution.py:24
  37.8 2.9 %collective-permute-done.4.arrived = f32[2,64,128]{2,1,0:T(8,128)S(1)} collective-permute-done((f32[2,64,128]{2,1,0:T(8,128)S(1)}, f32[2,64,128]{2,1,0:T(8,128)S(1)}, u32[]{:S(2)}, u32[]{:S(2)}) %collective-permute-start.4) | collective-permute-done | bytes 65568 | tf_op jit(solution)/shard_map/ppermute | solution.py:24
  40.7 0.1 shard_map.73
  40.9 0.0 collective-permute-done.5.handed.passed
  40.9 0.1 shard_map.74.after
  40.9 1.1 %shard_map.75 = (f32[2,16,64,128]{3,2,1,0:T(8,128)S(1)}, f32[2,2,2,64,128]{4,3,2,1,0:T(8,128)S(1)}, f32[2,64,128]{2,1,0:T(8,128)S(1)}) custom-call(s32[1]{0:T(128)} %bitcast.4.counts, f32[16,64,128]{2,1,0:T(8,128)S(1)} %shard_map.74.after, f32[2,16,64,128]{3,2,1,0:T(8,128)S(1)} %shard_map.66.after.own, f32[16,64,128]{2,1,0:T(8,128)S(1)} %collective-permute-done.3.far.other, ...), custom_call_target="tpu_custom_call" | custom-call | bytes 1048576 | tf_op jit(solution)/shard_map/pallas_call | solution.py:358
  42.0 0.0 collective-permute-done.6.other
  42.0 0.1 shard_map.76
  42.1 1.6 %collective-permute-start.7 = (f32[2,64,128]{2,1,0:T(8,128)S(1)}, f32[2,64,128]{2,1,0:T(8,128)S(1)}, u32[]{:S(2)}, u32[]{:S(2)}) collective-permute-start(f32[2,64,128]{2,1,0:T(8,128)S(1)} %get-tuple-element.39.after.mine), channel_id=1, source_target_pairs={{0,1},{1,0},{2,3},{3,2},{4,5},{5,4},{6,7},{7,6},{8,9},{9,8},{10,11... | collective-permute-start | bytes 196616 | tf_op jit(solution)/shard_map/ppermute | solution.py:24
  43.6 2.8 %collective-permute-done.7.arrived = f32[2,64,128]{2,1,0:T(8,128)S(1)} collective-permute-done((f32[2,64,128]{2,1,0:T(8,128)S(1)}, f32[2,64,128]{2,1,0:T(8,128)S(1)}, u32[]{:S(2)}, u32[]{:S(2)}) %collective-permute-start.7) | collective-permute-done | bytes 65568 | tf_op jit(solution)/shard_map/ppermute | solution.py:24
  46.4 0.1 shard_map.77
  46.6 0.1 collective-permute-start.9
  46.6 1.6 %collective-permute-start.8 = (f32[2,64,128]{2,1,0:T(8,128)S(1)}, f32[2,64,128]{2,1,0:T(8,128)S(1)}, u32[]{:S(2)}, u32[]{:S(2)}) collective-permute-start(f32[2,64,128]{2,1,0:T(8,128)S(1)} %get-tuple-element.38.after.mine), channel_id=1, source_target_pairs={{0,1},{1,0},{2,3},{3,2},{4,5},{5,4},{6,7},{7,6},{8,9},{9,8},{10,11... | collective-permute-start | bytes 196616 | tf_op jit(solution)/shard_map/ppermute | solution.py:24
  48.2 0.4 collective-permute-start.12
  48.6 2.5 %collective-permute-done.8.arrived = f32[2,64,128]{2,1,0:T(8,128)S(1)} collective-permute-done((f32[2,64,128]{2,1,0:T(8,128)S(1)}, f32[2,64,128]{2,1,0:T(8,128)S(1)}, u32[]{:S(2)}, u32[]{:S(2)}) %collective-permute-start.8) | collective-permute-done | bytes 65568 | tf_op jit(solution)/shard_map/ppermute | solution.py:24
  51.1 1.1 %shard_map.78 = (f32[2,16,64,128]{3,2,1,0:T(8,128)S(1)}, f32[16,64,128]{2,1,0:T(8,128)S(1)}) custom-call(s32[1]{0:T(128)} %bitcast.4.counts, f32[16,64,128]{2,1,0:T(8,128)S(1)} %get-tuple-element.43.after, f32[2,16,64,128]{3,2,1,0:T(8,128)S(1)} %shard_map.66.after.own, f32[16,64,128]{2,1,0:T(8,128)S(1)} %collective-permute-done.3.far.other, ...), custom_call_target="tpu_custom_call" | custom-call | bytes 1048576 | tf_op jit(solution)/shard_map/pallas_call | solution.py:372
  52.2 0.0 collective-permute-done.9.handed.passed
  52.2 0.1 shard_map.79.after
  52.3 0.1 collective-permute-start.11
  52.3 1.6 %collective-permute-start.10 = (f32[2,64,128]{2,1,0:T(8,128)S(1)}, f32[2,64,128]{2,1,0:T(8,128)S(1)}, u32[]{:S(2)}, u32[]{:S(2)}) collective-permute-start(f32[2,64,128]{2,1,0:T(8,128)S(1)} %get-tuple-element.28.after.mine), channel_id=1, source_target_pairs={{0,1},{1,0},{2,3},{3,2},{4,5},{5,4},{6,7},{7,6},{8,9},{9,8},{10,11... | collective-permute-start | bytes 196616 | tf_op jit(solution)/shard_map/ppermute | solution.py:24
  53.9 2.8 %collective-permute-done.10.arrived = f32[2,64,128]{2,1,0:T(8,128)S(1)} collective-permute-done((f32[2,64,128]{2,1,0:T(8,128)S(1)}, f32[2,64,128]{2,1,0:T(8,128)S(1)}, u32[]{:S(2)}, u32[]{:S(2)}) %collective-permute-start.10) | collective-permute-done | bytes 65568 | tf_op jit(solution)/shard_map/ppermute | solution.py:24
  56.7 0.1 shard_map.80.own
  56.8 9.3 %collective-permute-done.12.arrived = f32[16,64,128]{2,1,0:T(8,128)S(1)} collective-permute-done((f32[16,64,128]{2,1,0:T(8,128)S(1)}, f32[16,64,128]{2,1,0:T(8,128)S(1)}, u32[]{:S(2)}, u32[]{:S(2)}) %collective-permute-start.12) | collective-permute-done | bytes 524320 | tf_op jit(solution)/shard_map/ppermute | solution.py:19
  66.1 1.5 %shard_map.81.refs_0_ = f32[2,32,4096]{2,1,0:T(8,128)} custom-call(s32[1]{0:T(128)} %bitcast.flag, f32[2,16,64,128]{3,2,1,0:T(8,128)S(1)} %shard_map.80.own, f32[16,64,128]{2,1,0:T(8,128)S(1)} %collective-permute-done.5.handed.passed, f32[16,64,128]{2,1,0:T(8,128)S(1)} %collective-permute-done.12.arrived), custom_call_target="tpu_custom_call" | custom-call | bytes 1048576 | tf_op jit(solution)/shard_map/pallas_call | solution.py:418
  67.6 9.1 %collective-permute-done.11.arrived = f32[16,64,128]{2,1,0:T(8,128)S(1)} collective-permute-done((f32[16,64,128]{2,1,0:T(8,128)S(1)}, f32[16,64,128]{2,1,0:T(8,128)S(1)}, u32[]{:S(2)}, u32[]{:S(2)}) %collective-permute-start.11) | collective-permute-done | bytes 524320 | tf_op jit(solution)/shard_map/ppermute | solution.py:19
  76.8 1.5 %shard_map.82 = f32[2,32,4096]{2,1,0:T(8,128)} custom-call(s32[1]{0:T(128)} %bitcast.flag, f32[2,16,64,128]{3,2,1,0:T(8,128)S(1)} %shard_map.80.own, f32[16,64,128]{2,1,0:T(8,128)S(1)} %collective-permute-done.9.handed.passed, f32[16,64,128]{2,1,0:T(8,128)S(1)} %collective-permute-done.11.arrived, ...), custom_call_target="tpu_custom_call", output_to_operand_aliasing={{}: (4, {})} | custom-call | bytes 1048576 | tf_op jit(solution)/shard_map/pallas_call | solution.py:418
  (5 shorter events, 0.1 us)
Async XLA Ops:
  1.7 17.3 %collective-permute-start = (f32[16,64,128]{2,1,0:T(8,128)S(1)}, f32[16,64,128]{2,1,0:T(8,128)S(1)}, u32[]{:S(2)}, u32[]{:S(2)}) collective-permute-start(f32[16,64,128]{2,1,0:T(8,128)S(1)} %shard_map.64.refs_0_.first.own), channel_id=1, source_target_pairs={{0,28},{2,30},{4,0},{6,2},{8,4},{10,6},{12,8},{14,10},{16,12},{18,... | collective-permute-start | bytes 1572872 | tf_op jit(solution)/shard_map/ppermute | solution.py:19
  10.1 0.7 copy-start.3
  12.1 0.9 %copy-start = (f32[5,64,128]{2,1,0:T(8,128)S(1)}, f32[5,64,128]{2,1,0:T(8,128)}, u32[]{:S(2)}) copy-start(f32[5,64,128]{2,1,0:T(8,128)} %constant.68.clone.decay) | copy-start | bytes 491524
  12.1 1.0 %copy-start.1 = (bf16[256,256]{1,0:T(8,128)(2,1)S(1)}, bf16[256,256]{1,0:T(8,128)(2,1)}, u32[]{:S(2)}) copy-start(bf16[256,256]{1,0:T(8,128)(2,1)} %constant.66.clone.right_ref) | copy-start | bytes 393220
  12.2 1.0 %copy-start.2 = (bf16[64,192]{1,0:T(8,128)(2,1)S(1)}, bf16[64,192]{1,0:T(8,128)(2,1)}, u32[]{:S(2)}) copy-start(bf16[64,192]{1,0:T(8,128)(2,1)} %constant.67.clone.left_ref) | copy-start | bytes 73732
  19.0 5.3 %collective-permute-start.1 = (f32[16,64,128]{2,1,0:T(8,128)S(1)}, f32[16,64,128]{2,1,0:T(8,128)S(1)}, u32[]{:S(2)}, u32[]{:S(2)}) collective-permute-start(f32[16,64,128]{2,1,0:T(8,128)S(1)} %shard_map.68.after), channel_id=1, source_target_pairs={{0,2},{2,0},{4,6},{6,4},{8,10},{10,8},{12,14},{14,12},{16,18},{18,... | collective-permute-start | bytes 1572872 | tf_op jit(solution)/shard_map/ppermute | solution.py:24
  19.1 17.0 %collective-permute-start.3 = (f32[16,64,128]{2,1,0:T(8,128)S(1)}, f32[16,64,128]{2,1,0:T(8,128)S(1)}, u32[]{:S(2)}, u32[]{:S(2)}) collective-permute-start(f32[16,64,128]{2,1,0:T(8,128)S(1)} %shard_map.65.second.other.own), channel_id=1, source_target_pairs={{0,28},{2,30},{4,0},{6,2},{8,4},{10,6},{12,8},{14,10},{16,12},{18,... | collective-permute-start | bytes 1572872 | tf_op jit(solution)/shard_map/ppermute | solution.py:19
  24.3 4.3 %collective-permute-start.2 = (f32[2,64,128]{2,1,0:T(8,128)S(1)}, f32[2,64,128]{2,1,0:T(8,128)S(1)}, u32[]{:S(2)}, u32[]{:S(2)}) collective-permute-start(f32[2,64,128]{2,1,0:T(8,128)S(1)} %get-tuple-element.30.after.mine), channel_id=1, source_target_pairs={{0,1},{1,0},{2,3},{3,2},{4,5},{5,4},{6,7},{7,6},{8,9},{9,8},{10,11... | collective-permute-start | bytes 196616 | tf_op jit(solution)/shard_map/ppermute | solution.py:24
  28.8 12.1 %collective-permute-start.5 = (f32[16,64,128]{2,1,0:T(8,128)S(1)}, f32[16,64,128]{2,1,0:T(8,128)S(1)}, u32[]{:S(2)}, u32[]{:S(2)}) collective-permute-start(f32[16,64,128]{2,1,0:T(8,128)S(1)} %get-tuple-element.33.after), channel_id=1, source_target_pairs={{0,2},{2,0},{4,6},{6,4},{8,10},{10,8},{12,14},{14,12},{16,18},{18,... | collective-permute-start | bytes 1572872 | tf_op jit(solution)/shard_map/ppermute | solution.py:24
  36.1 5.9 %collective-permute-start.6 = (f32[16,64,128]{2,1,0:T(8,128)S(1)}, f32[16,64,128]{2,1,0:T(8,128)S(1)}, u32[]{:S(2)}, u32[]{:S(2)}) collective-permute-start(f32[16,64,128]{2,1,0:T(8,128)S(1)} %shard_map.72.after), channel_id=1, source_target_pairs={{0,2},{2,0},{4,6},{6,4},{8,10},{10,8},{12,14},{14,12},{16,18},{18,... | collective-permute-start | bytes 1572872 | tf_op jit(solution)/shard_map/ppermute | solution.py:24
  36.2 4.5 %collective-permute-start.4 = (f32[2,64,128]{2,1,0:T(8,128)S(1)}, f32[2,64,128]{2,1,0:T(8,128)S(1)}, u32[]{:S(2)}, u32[]{:S(2)}) collective-permute-start(f32[2,64,128]{2,1,0:T(8,128)S(1)} %get-tuple-element.29.after.mine), channel_id=1, source_target_pairs={{0,1},{1,0},{2,3},{3,2},{4,5},{5,4},{6,7},{7,6},{8,9},{9,8},{10,11... | collective-permute-start | bytes 196616 | tf_op jit(solution)/shard_map/ppermute | solution.py:24
  42.1 4.3 %collective-permute-start.7 = (f32[2,64,128]{2,1,0:T(8,128)S(1)}, f32[2,64,128]{2,1,0:T(8,128)S(1)}, u32[]{:S(2)}, u32[]{:S(2)}) collective-permute-start(f32[2,64,128]{2,1,0:T(8,128)S(1)} %get-tuple-element.39.after.mine), channel_id=1, source_target_pairs={{0,1},{1,0},{2,3},{3,2},{4,5},{5,4},{6,7},{7,6},{8,9},{9,8},{10,11... | collective-permute-start | bytes 196616 | tf_op jit(solution)/shard_map/ppermute | solution.py:24
  46.6 5.6 %collective-permute-start.9 = (f32[16,64,128]{2,1,0:T(8,128)S(1)}, f32[16,64,128]{2,1,0:T(8,128)S(1)}, u32[]{:S(2)}, u32[]{:S(2)}) collective-permute-start(f32[16,64,128]{2,1,0:T(8,128)S(1)} %get-tuple-element.43.after), channel_id=1, source_target_pairs={{0,2},{2,0},{4,6},{6,4},{8,10},{10,8},{12,14},{14,12},{16,18},{18,... | collective-permute-start | bytes 1572872 | tf_op jit(solution)/shard_map/ppermute | solution.py:24
  46.6 4.5 %collective-permute-start.8 = (f32[2,64,128]{2,1,0:T(8,128)S(1)}, f32[2,64,128]{2,1,0:T(8,128)S(1)}, u32[]{:S(2)}, u32[]{:S(2)}) collective-permute-start(f32[2,64,128]{2,1,0:T(8,128)S(1)} %get-tuple-element.38.after.mine), channel_id=1, source_target_pairs={{0,1},{1,0},{2,3},{3,2},{4,5},{5,4},{6,7},{7,6},{8,9},{9,8},{10,11... | collective-permute-start | bytes 196616 | tf_op jit(solution)/shard_map/ppermute | solution.py:24
  48.2 17.9 %collective-permute-start.12 = (f32[16,64,128]{2,1,0:T(8,128)S(1)}, f32[16,64,128]{2,1,0:T(8,128)S(1)}, u32[]{:S(2)}, u32[]{:S(2)}) collective-permute-start(f32[16,64,128]{2,1,0:T(8,128)S(1)} %shard_map.74.after), channel_id=1, source_target_pairs={{0,4},{2,6},{4,8},{6,10},{8,12},{10,14},{12,16},{14,18},{16,20},{1... | collective-permute-start | bytes 1572872 | tf_op jit(solution)/shard_map/ppermute | solution.py:19
  52.3 24.5 %collective-permute-start.11 = (f32[16,64,128]{2,1,0:T(8,128)S(1)}, f32[16,64,128]{2,1,0:T(8,128)S(1)}, u32[]{:S(2)}, u32[]{:S(2)}) collective-permute-start(f32[16,64,128]{2,1,0:T(8,128)S(1)} %shard_map.79.after), channel_id=1, source_target_pairs={{0,4},{2,6},{4,8},{6,10},{8,12},{10,14},{12,16},{14,18},{16,20},{1... | collective-permute-start | bytes 1572872 | tf_op jit(solution)/shard_map/ppermute | solution.py:19
  52.3 4.3 %collective-permute-start.10 = (f32[2,64,128]{2,1,0:T(8,128)S(1)}, f32[2,64,128]{2,1,0:T(8,128)S(1)}, u32[]{:S(2)}, u32[]{:S(2)}) collective-permute-start(f32[2,64,128]{2,1,0:T(8,128)S(1)} %get-tuple-element.28.after.mine), channel_id=1, source_target_pairs={{0,1},{1,0},{2,3},{3,2},{4,5},{5,4},{6,7},{7,6},{8,9},{9,8},{10,11... | collective-permute-start | bytes 196616 | tf_op jit(solution)/shard_map/ppermute | solution.py:24

commit v4 on v3

--- a/solution.py
+++ b/solution.py
@@ -399,10 +399,7 @@
         distant_state = (far[row],) + tuple(distant_state) + (distant_ends,)
         acc, handed = backward(base, mine, near_state, total)
         handed_over = swapped(handed, "band")
-        after = handed
-        if row + 1 < owned:
-            after, near = brought(row + 1, handed)
-        acc, distant = backward(base + owned, after, distant_state, (acc,))
+        acc, distant = backward(base + owned, handed, distant_state, (acc,))
         total = (acc,)
         joined = call(join_kernel, one, [smem, free, vmem, vmem])(
             flag, distant, distant, handed_over
@@ -410,6 +407,8 @@
         passed.append(handed_over)
         arrived.append(rotated(joined, "band", 2))
         after = joined
+        if row + 1 < owned:
+            after, near = brought(row + 1, joined)
     total = backward(inner_base, after, inner, total, inside=True)
     out = jax.ShapeDtypeStruct(orbitals.shape, jnp.float32)
     result = None

time: 78.5 us -> 83 us (1.057)
  waiting for transfers between devices: 45.3 us -> 48.3 us
  starting transfers between devices: 19.9 us -> 21.3 us
    ppermute x9, waiting for transfers between devices: 13.8 us -> 16.7 us  [swapped(): lax.ppermute(value, axis, [(source, source ^ 1) for source in range(count)])]
    ppermute x4, starting transfers between devices: 11.8 us -> 13.4 us  [rotated(): return lax.ppermute(value, axis, pairs)]
  transfers between devices with their start and end apart: 13 -> 13, of which waited for: 9 -> 11; matrix products, arithmetic and copies ran while one was open for 1% -> 1% of each run, Pallas kernels for 8% -> 7%
where the time goes in v4:
time: 83 us; the launch traced here: 82.8 us
  waiting for transfers between devices  48.3 us (58%)
  starting transfers between devices  21.3 us (26%)
  Pallas kernels  9.41 us (11%)
  local copies, waits for them, and re-layouts  1.55 us (2%)
  between operations  1.51 us (2%)
    ppermute x4, waiting for transfers between devices, rotated(): return lax.ppermute(value, axis, pairs)  31.6 us
    ppermute x9, waiting for transfers between devices, swapped(): lax.ppermute(value, axis, [(source, source ^ 1) for source in range(count)])  16.7 us
    ppermute x4, starting transfers between devices, rotated(): return lax.ppermute(value, axis, pairs)  13.4 us
    ppermute x9, starting transfers between devices, swapped(): lax.ppermute(value, axis, [(source, source ^ 1) for source in range(count)])  7.87 us
    pallas_call x2, Pallas kernels, on_device(): call(functools.partial(arrange_kernel, row), one, [hbm] + [free] * row, s...  3.35 us
    pallas_call x2, Pallas kernels, on_device(): call(functools.partial(restore_kernel, row), out, [smem] + [vmem] * 3 + [...  3.09 us
  transfers between devices with their start and end apart: 13, of which 11 were waited for; matrix products, arithmetic and copies ran while one was open for 1% of the time, Pallas kernels for 7%

profile of v4, /device:TPU:0, one launch (start us, length us, event | category | flops | bytes accessed | tf_op | source)
XLA Modules:
  0.0 82.8 jit_solution(12375149008646357840)
XLA Ops:
  0.0 1.7 %shard_map.64.refs_0_.first.own = f32[16,64,128]{2,1,0:T(8,128)S(1)} custom-call(f32[2,32,4096]{2,1,0:T(8,128)} %source.3), custom_call_target="tpu_custom_call" | custom-call | bytes 1048576 | tf_op jit(solution)/shard_map/pallas_call | solution.py:341
  1.7 6.1 %collective-permute-start = (f32[16,64,128]{2,1,0:T(8,128)S(1)}, f32[16,64,128]{2,1,0:T(8,128)S(1)}, u32[]{:S(2)}, u32[]{:S(2)}) collective-permute-start(f32[16,64,128]{2,1,0:T(8,128)S(1)} %shard_map.64.refs_0_.first.own), channel_id=1, source_target_pairs={{0,28},{2,30},{4,0},{6,2},{8,4},{10,6},{12,8},{14,10},{16,12},{18,... | collective-permute-start | bytes 1572872 | tf_op jit(solution)/shard_map/ppermute | solution.py:19
  7.8 1.7 %shard_map.65.second.other.own = f32[16,64,128]{2,1,0:T(8,128)S(1)} custom-call(f32[2,32,4096]{2,1,0:T(8,128)} %source.3, f32[16,64,128]{2,1,0:T(8,128)S(1)} %shard_map.64.refs_0_.first.own), custom_call_target="tpu_custom_call" | custom-call | bytes 1048576 | tf_op jit(solution)/shard_map/pallas_call | solution.py:341
  10.1 0.0 copy-start.3
  10.1 0.7 copy-done.3
  10.8 0.7 fusion
  12.1 0.0 copy-start
  12.1 0.0 copy-start.1
  12.2 0.0 copy-start.2
  12.2 0.1 shard_map.66.after.own
  12.3 0.8 copy-done
  13.1 0.1 copy-done.1
  13.1 0.0 copy-done.2
  13.1 5.8 %collective-permute-done.far.other = f32[16,64,128]{2,1,0:T(8,128)S(1)} collective-permute-done((f32[16,64,128]{2,1,0:T(8,128)S(1)}, f32[16,64,128]{2,1,0:T(8,128)S(1)}, u32[]{:S(2)}, u32[]{:S(2)}) %collective-permute-start) | collective-permute-done | bytes 524320 | tf_op jit(solution)/shard_map/ppermute | solution.py:19
  19.0 0.1 collective-permute-start.1
  19.1 0.1 shard_map.69
  19.1 1.8 %collective-permute-done.1.other = f32[16,64,128]{2,1,0:T(8,128)S(1)} collective-permute-done((f32[16,64,128]{2,1,0:T(8,128)S(1)}, f32[16,64,128]{2,1,0:T(8,128)S(1)}, u32[]{:S(2)}, u32[]{:S(2)}) %collective-permute-start.1) | collective-permute-done | bytes 524320 | tf_op jit(solution)/shard_map/ppermute | solution.py:24
  21.0 1.5 %collective-permute-start.2 = (f32[2,64,128]{2,1,0:T(8,128)S(1)}, f32[2,64,128]{2,1,0:T(8,128)S(1)}, u32[]{:S(2)}, u32[]{:S(2)}) collective-permute-start(f32[2,64,128]{2,1,0:T(8,128)S(1)} %get-tuple-element.30.after.mine), channel_id=1, source_target_pairs={{0,1},{1,0},{2,3},{3,2},{4,5},{5,4},{6,7},{7,6},{8,9},{9,8},{10,11... | collective-permute-start | bytes 196616 | tf_op jit(solution)/shard_map/ppermute | solution.py:24
  22.5 2.8 %collective-permute-done.2.arrived = f32[2,64,128]{2,1,0:T(8,128)S(1)} collective-permute-done((f32[2,64,128]{2,1,0:T(8,128)S(1)}, f32[2,64,128]{2,1,0:T(8,128)S(1)}, u32[]{:S(2)}, u32[]{:S(2)}) %collective-permute-start.2) | collective-permute-done | bytes 65568 | tf_op jit(solution)/shard_map/ppermute | solution.py:24
  25.2 0.1 shard_map.71
  25.4 0.1 collective-permute-start.4
  25.5 7.3 %collective-permute-start.5 = (f32[16,64,128]{2,1,0:T(8,128)S(1)}, f32[16,64,128]{2,1,0:T(8,128)S(1)}, u32[]{:S(2)}, u32[]{:S(2)}) collective-permute-start(f32[16,64,128]{2,1,0:T(8,128)S(1)} %shard_map.65.second.other.own), channel_id=1, source_target_pairs={{0,28},{2,30},{4,0},{6,2},{8,4},{10,6},{12,8},{14,10},{16,12},{18,... | collective-permute-start | bytes 1572872 | tf_op jit(solution)/shard_map/ppermute | solution.py:19
  32.8 1.5 %collective-permute-start.3 = (f32[2,64,128]{2,1,0:T(8,128)S(1)}, f32[2,64,128]{2,1,0:T(8,128)S(1)}, u32[]{:S(2)}, u32[]{:S(2)}) collective-permute-start(f32[2,64,128]{2,1,0:T(8,128)S(1)} %get-tuple-element.29.after.mine), channel_id=1, source_target_pairs={{0,1},{1,0},{2,3},{3,2},{4,5},{5,4},{6,7},{7,6},{8,9},{9,8},{10,11... | collective-permute-start | bytes 196616 | tf_op jit(solution)/shard_map/ppermute | solution.py:24
  34.2 2.8 %collective-permute-done.3.arrived = f32[2,64,128]{2,1,0:T(8,128)S(1)} collective-permute-done((f32[2,64,128]{2,1,0:T(8,128)S(1)}, f32[2,64,128]{2,1,0:T(8,128)S(1)}, u32[]{:S(2)}, u32[]{:S(2)}) %collective-permute-start.3) | collective-permute-done | bytes 65568 | tf_op jit(solution)/shard_map/ppermute | solution.py:24
  37.0 0.1 shard_map.72
  37.2 0.0 collective-permute-done.4.handed.passed
  37.2 0.1 shard_map.73.after
  37.2 7.3 %collective-permute-done.5.far.other = f32[16,64,128]{2,1,0:T(8,128)S(1)} collective-permute-done((f32[16,64,128]{2,1,0:T(8,128)S(1)}, f32[16,64,128]{2,1,0:T(8,128)S(1)}, u32[]{:S(2)}, u32[]{:S(2)}) %collective-permute-start.5) | collective-permute-done | bytes 524320 | tf_op jit(solution)/shard_map/ppermute | solution.py:19
  44.6 0.1 collective-permute-start.6
  44.7 1.1 %shard_map.75 = (f32[2,16,64,128]{3,2,1,0:T(8,128)S(1)}, f32[2,2,2,64,128]{4,3,2,1,0:T(8,128)S(1)}, f32[2,64,128]{2,1,0:T(8,128)S(1)}) custom-call(s32[1]{0:T(128)} %bitcast.4.counts, f32[16,64,128]{2,1,0:T(8,128)S(1)} %shard_map.74.after, f32[2,16,64,128]{3,2,1,0:T(8,128)S(1)} %shard_map.66.after.own, f32[16,64,128]{2,1,0:T(8,128)S(1)} %collective-permute-done.5.far.other, ...), custom_call_target="tpu_custom_call" | custom-call | bytes 1048576 | tf_op jit(solution)/shard_map/pallas_call | solution.py:358
  45.7 0.8 %collective-permute-done.6.other = f32[16,64,128]{2,1,0:T(8,128)S(1)} collective-permute-done((f32[16,64,128]{2,1,0:T(8,128)S(1)}, f32[16,64,128]{2,1,0:T(8,128)S(1)}, u32[]{:S(2)}, u32[]{:S(2)}) %collective-permute-start.6) | collective-permute-done | bytes 524320 | tf_op jit(solution)/shard_map/ppermute | solution.py:24
  46.6 1.5 %collective-permute-start.7 = (f32[2,64,128]{2,1,0:T(8,128)S(1)}, f32[2,64,128]{2,1,0:T(8,128)S(1)}, u32[]{:S(2)}, u32[]{:S(2)}) collective-permute-start(f32[2,64,128]{2,1,0:T(8,128)S(1)} %get-tuple-element.39.after.mine), channel_id=1, source_target_pairs={{0,1},{1,0},{2,3},{3,2},{4,5},{5,4},{6,7},{7,6},{8,9},{9,8},{10,11... | collective-permute-start | bytes 196616 | tf_op jit(solution)/shard_map/ppermute | solution.py:24
  48.1 2.8 %collective-permute-done.7.arrived = f32[2,64,128]{2,1,0:T(8,128)S(1)} collective-permute-done((f32[2,64,128]{2,1,0:T(8,128)S(1)}, f32[2,64,128]{2,1,0:T(8,128)S(1)}, u32[]{:S(2)}, u32[]{:S(2)}) %collective-permute-start.7) | collective-permute-done | bytes 65568 | tf_op jit(solution)/shard_map/ppermute | solution.py:24
  50.8 0.1 shard_map.77
  51.0 0.1 collective-permute-start.9
  51.1 1.6 %collective-permute-start.8 = (f32[2,64,128]{2,1,0:T(8,128)S(1)}, f32[2,64,128]{2,1,0:T(8,128)S(1)}, u32[]{:S(2)}, u32[]{:S(2)}) collective-permute-start(f32[2,64,128]{2,1,0:T(8,128)S(1)} %get-tuple-element.38.after.mine), channel_id=1, source_target_pairs={{0,1},{1,0},{2,3},{3,2},{4,5},{5,4},{6,7},{7,6},{8,9},{9,8},{10,11... | collective-permute-start | bytes 196616 | tf_op jit(solution)/shard_map/ppermute | solution.py:24
  52.6 0.0 collective-permute-start.12
  52.6 2.9 %collective-permute-done.8.arrived = f32[2,64,128]{2,1,0:T(8,128)S(1)} collective-permute-done((f32[2,64,128]{2,1,0:T(8,128)S(1)}, f32[2,64,128]{2,1,0:T(8,128)S(1)}, u32[]{:S(2)}, u32[]{:S(2)}) %collective-permute-start.8) | collective-permute-done | bytes 65568 | tf_op jit(solution)/shard_map/ppermute | solution.py:24
  55.6 1.1 %shard_map.78 = (f32[2,16,64,128]{3,2,1,0:T(8,128)S(1)}, f32[16,64,128]{2,1,0:T(8,128)S(1)}) custom-call(s32[1]{0:T(128)} %bitcast.4.counts, f32[16,64,128]{2,1,0:T(8,128)S(1)} %get-tuple-element.43.after, f32[2,16,64,128]{3,2,1,0:T(8,128)S(1)} %shard_map.66.after.own, f32[16,64,128]{2,1,0:T(8,128)S(1)} %collective-permute-done.5.far.other, ...), custom_call_target="tpu_custom_call" | custom-call | bytes 1048576 | tf_op jit(solution)/shard_map/pallas_call | solution.py:372
  56.6 0.0 collective-permute-done.9.handed.passed
  56.6 0.1 shard_map.79.after
  56.7 0.1 collective-permute-start.11
  56.8 1.6 %collective-permute-start.10 = (f32[2,64,128]{2,1,0:T(8,128)S(1)}, f32[2,64,128]{2,1,0:T(8,128)S(1)}, u32[]{:S(2)}, u32[]{:S(2)}) collective-permute-start(f32[2,64,128]{2,1,0:T(8,128)S(1)} %get-tuple-element.28.after.mine), channel_id=1, source_target_pairs={{0,1},{1,0},{2,3},{3,2},{4,5},{5,4},{6,7},{7,6},{8,9},{9,8},{10,11... | collective-permute-start | bytes 196616 | tf_op jit(solution)/shard_map/ppermute | solution.py:24
  58.3 2.8 %collective-permute-done.10.arrived = f32[2,64,128]{2,1,0:T(8,128)S(1)} collective-permute-done((f32[2,64,128]{2,1,0:T(8,128)S(1)}, f32[2,64,128]{2,1,0:T(8,128)S(1)}, u32[]{:S(2)}, u32[]{:S(2)}) %collective-permute-start.10) | collective-permute-done | bytes 65568 | tf_op jit(solution)/shard_map/ppermute | solution.py:24
  61.1 0.1 shard_map.80.own
  61.2 9.4 %collective-permute-done.12.arrived = f32[16,64,128]{2,1,0:T(8,128)S(1)} collective-permute-done((f32[16,64,128]{2,1,0:T(8,128)S(1)}, f32[16,64,128]{2,1,0:T(8,128)S(1)}, u32[]{:S(2)}, u32[]{:S(2)}) %collective-permute-start.12) | collective-permute-done | bytes 524320 | tf_op jit(solution)/shard_map/ppermute | solution.py:19
  70.6 1.5 %shard_map.81.refs_0_ = f32[2,32,4096]{2,1,0:T(8,128)} custom-call(s32[1]{0:T(128)} %bitcast.flag, f32[2,16,64,128]{3,2,1,0:T(8,128)S(1)} %shard_map.80.own, f32[16,64,128]{2,1,0:T(8,128)S(1)} %collective-permute-done.4.handed.passed, f32[16,64,128]{2,1,0:T(8,128)S(1)} %collective-permute-done.12.arrived), custom_call_target="tpu_custom_call" | custom-call | bytes 1048576 | tf_op jit(solution)/shard_map/pallas_call | solution.py:417
  72.1 9.1 %collective-permute-done.11.arrived = f32[16,64,128]{2,1,0:T(8,128)S(1)} collective-permute-done((f32[16,64,128]{2,1,0:T(8,128)S(1)}, f32[16,64,128]{2,1,0:T(8,128)S(1)}, u32[]{:S(2)}, u32[]{:S(2)}) %collective-permute-start.11) | collective-permute-done | bytes 524320 | tf_op jit(solution)/shard_map/ppermute | solution.py:19
  81.3 1.5 %shard_map.82 = f32[2,32,4096]{2,1,0:T(8,128)} custom-call(s32[1]{0:T(128)} %bitcast.flag, f32[2,16,64,128]{3,2,1,0:T(8,128)S(1)} %shard_map.80.own, f32[16,64,128]{2,1,0:T(8,128)S(1)} %collective-permute-done.9.handed.passed, f32[16,64,128]{2,1,0:T(8,128)S(1)} %collective-permute-done.11.arrived, ...), custom_call_target="tpu_custom_call", output_to_operand_aliasing={{}: (4, {})} | custom-call | bytes 1048576 | tf_op jit(solution)/shard_map/pallas_call | solution.py:417
  (5 shorter events, 0.1 us)
Async XLA Ops:
  1.7 17.3 %collective-permute-start = (f32[16,64,128]{2,1,0:T(8,128)S(1)}, f32[16,64,128]{2,1,0:T(8,128)S(1)}, u32[]{:S(2)}, u32[]{:S(2)}) collective-permute-start(f32[16,64,128]{2,1,0:T(8,128)S(1)} %shard_map.64.refs_0_.first.own), channel_id=1, source_target_pairs={{0,28},{2,30},{4,0},{6,2},{8,4},{10,6},{12,8},{14,10},{16,12},{18,... | collective-permute-start | bytes 1572872 | tf_op jit(solution)/shard_map/ppermute | solution.py:19
  10.1 0.7 copy-start.3
  12.1 0.9 %copy-start = (f32[5,64,128]{2,1,0:T(8,128)S(1)}, f32[5,64,128]{2,1,0:T(8,128)}, u32[]{:S(2)}) copy-start(f32[5,64,128]{2,1,0:T(8,128)} %constant.68.clone.decay) | copy-start | bytes 491524
  12.1 1.0 %copy-start.1 = (bf16[256,256]{1,0:T(8,128)(2,1)S(1)}, bf16[256,256]{1,0:T(8,128)(2,1)}, u32[]{:S(2)}) copy-start(bf16[256,256]{1,0:T(8,128)(2,1)} %constant.66.clone.right_ref) | copy-start | bytes 393220
  12.2 1.0 %copy-start.2 = (bf16[64,192]{1,0:T(8,128)(2,1)S(1)}, bf16[64,192]{1,0:T(8,128)(2,1)}, u32[]{:S(2)}) copy-start(bf16[64,192]{1,0:T(8,128)(2,1)} %constant.67.clone.left_ref) | copy-start | bytes 73732
  19.0 2.0 %collective-permute-start.1 = (f32[16,64,128]{2,1,0:T(8,128)S(1)}, f32[16,64,128]{2,1,0:T(8,128)S(1)}, u32[]{:S(2)}, u32[]{:S(2)}) collective-permute-start(f32[16,64,128]{2,1,0:T(8,128)S(1)} %shard_map.68.after), channel_id=1, source_target_pairs={{0,2},{2,0},{4,6},{6,4},{8,10},{10,8},{12,14},{14,12},{16,18},{18,... | collective-permute-start | bytes 1572872 | tf_op jit(solution)/shard_map/ppermute | solution.py:24
  21.0 4.3 %collective-permute-start.2 = (f32[2,64,128]{2,1,0:T(8,128)S(1)}, f32[2,64,128]{2,1,0:T(8,128)S(1)}, u32[]{:S(2)}, u32[]{:S(2)}) collective-permute-start(f32[2,64,128]{2,1,0:T(8,128)S(1)} %get-tuple-element.30.after.mine), channel_id=1, source_target_pairs={{0,1},{1,0},{2,3},{3,2},{4,5},{5,4},{6,7},{7,6},{8,9},{9,8},{10,11... | collective-permute-start | bytes 196616 | tf_op jit(solution)/shard_map/ppermute | solution.py:24
  25.4 11.8 %collective-permute-start.4 = (f32[16,64,128]{2,1,0:T(8,128)S(1)}, f32[16,64,128]{2,1,0:T(8,128)S(1)}, u32[]{:S(2)}, u32[]{:S(2)}) collective-permute-start(f32[16,64,128]{2,1,0:T(8,128)S(1)} %get-tuple-element.33.after), channel_id=1, source_target_pairs={{0,2},{2,0},{4,6},{6,4},{8,10},{10,8},{12,14},{14,12},{16,18},{18,... | collective-permute-start | bytes 1572872 | tf_op jit(solution)/shard_map/ppermute | solution.py:24
  25.5 19.1 %collective-permute-start.5 = (f32[16,64,128]{2,1,0:T(8,128)S(1)}, f32[16,64,128]{2,1,0:T(8,128)S(1)}, u32[]{:S(2)}, u32[]{:S(2)}) collective-permute-start(f32[16,64,128]{2,1,0:T(8,128)S(1)} %shard_map.65.second.other.own), channel_id=1, source_target_pairs={{0,28},{2,30},{4,0},{6,2},{8,4},{10,6},{12,8},{14,10},{16,12},{18,... | collective-permute-start | bytes 1572872 | tf_op jit(solution)/shard_map/ppermute | solution.py:19
  32.8 4.3 %collective-permute-start.3 = (f32[2,64,128]{2,1,0:T(8,128)S(1)}, f32[2,64,128]{2,1,0:T(8,128)S(1)}, u32[]{:S(2)}, u32[]{:S(2)}) collective-permute-start(f32[2,64,128]{2,1,0:T(8,128)S(1)} %get-tuple-element.29.after.mine), channel_id=1, source_target_pairs={{0,1},{1,0},{2,3},{3,2},{4,5},{5,4},{6,7},{7,6},{8,9},{9,8},{10,11... | collective-permute-start | bytes 196616 | tf_op jit(solution)/shard_map/ppermute | solution.py:24
  44.6 2.0 %collective-permute-start.6 = (f32[16,64,128]{2,1,0:T(8,128)S(1)}, f32[16,64,128]{2,1,0:T(8,128)S(1)}, u32[]{:S(2)}, u32[]{:S(2)}) collective-permute-start(f32[16,64,128]{2,1,0:T(8,128)S(1)} %shard_map.74.after), channel_id=1, source_target_pairs={{0,2},{2,0},{4,6},{6,4},{8,10},{10,8},{12,14},{14,12},{16,18},{18,... | collective-permute-start | bytes 1572872 | tf_op jit(solution)/shard_map/ppermute | solution.py:24
  46.6 4.3 %collective-permute-start.7 = (f32[2,64,128]{2,1,0:T(8,128)S(1)}, f32[2,64,128]{2,1,0:T(8,128)S(1)}, u32[]{:S(2)}, u32[]{:S(2)}) collective-permute-start(f32[2,64,128]{2,1,0:T(8,128)S(1)} %get-tuple-element.39.after.mine), channel_id=1, source_target_pairs={{0,1},{1,0},{2,3},{3,2},{4,5},{5,4},{6,7},{7,6},{8,9},{9,8},{10,11... | collective-permute-start | bytes 196616 | tf_op jit(solution)/shard_map/ppermute | solution.py:24
  51.0 5.6 %collective-permute-start.9 = (f32[16,64,128]{2,1,0:T(8,128)S(1)}, f32[16,64,128]{2,1,0:T(8,128)S(1)}, u32[]{:S(2)}, u32[]{:S(2)}) collective-permute-start(f32[16,64,128]{2,1,0:T(8,128)S(1)} %get-tuple-element.43.after), channel_id=1, source_target_pairs={{0,2},{2,0},{4,6},{6,4},{8,10},{10,8},{12,14},{14,12},{16,18},{18,... | collective-permute-start | bytes 1572872 | tf_op jit(solution)/shard_map/ppermute | solution.py:24
  51.1 4.5 %collective-permute-start.8 = (f32[2,64,128]{2,1,0:T(8,128)S(1)}, f32[2,64,128]{2,1,0:T(8,128)S(1)}, u32[]{:S(2)}, u32[]{:S(2)}) collective-permute-start(f32[2,64,128]{2,1,0:T(8,128)S(1)} %get-tuple-element.38.after.mine), channel_id=1, source_target_pairs={{0,1},{1,0},{2,3},{3,2},{4,5},{5,4},{6,7},{7,6},{8,9},{9,8},{10,11... | collective-permute-start | bytes 196616 | tf_op jit(solution)/shard_map/ppermute | solution.py:24
  52.6 18.0 %collective-permute-start.12 = (f32[16,64,128]{2,1,0:T(8,128)S(1)}, f32[16,64,128]{2,1,0:T(8,128)S(1)}, u32[]{:S(2)}, u32[]{:S(2)}) collective-permute-start(f32[16,64,128]{2,1,0:T(8,128)S(1)} %shard_map.73.after), channel_id=1, source_target_pairs={{0,4},{2,6},{4,8},{6,10},{8,12},{10,14},{12,16},{14,18},{16,20},{1... | collective-permute-start | bytes 1572872 | tf_op jit(solution)/shard_map/ppermute | solution.py:19
  56.7 24.6 %collective-permute-start.11 = (f32[16,64,128]{2,1,0:T(8,128)S(1)}, f32[16,64,128]{2,1,0:T(8,128)S(1)}, u32[]{:S(2)}, u32[]{:S(2)}) collective-permute-start(f32[16,64,128]{2,1,0:T(8,128)S(1)} %shard_map.79.after), channel_id=1, source_target_pairs={{0,4},{2,6},{4,8},{6,10},{8,12},{10,14},{12,16},{14,18},{16,20},{1... | collective-permute-start | bytes 1572872 | tf_op jit(solution)/shard_map/ppermute | solution.py:19
  56.8 4.3 %collective-permute-start.10 = (f32[2,64,128]{2,1,0:T(8,128)S(1)}, f32[2,64,128]{2,1,0:T(8,128)S(1)}, u32[]{:S(2)}, u32[]{:S(2)}) collective-permute-start(f32[2,64,128]{2,1,0:T(8,128)S(1)} %get-tuple-element.28.after.mine), channel_id=1, source_target_pairs={{0,1},{1,0},{2,3},{3,2},{4,5},{5,4},{6,7},{7,6},{8,9},{9,8},{10,11... | collective-permute-start | bytes 196616 | tf_op jit(solution)/shard_map/ppermute | solution.py:24

commit v5 on v4

--- a/solution.py
+++ b/solution.py
@@ -39,9 +39,10 @@
     wide_high = np.kron(eye, high.astype(np.float32))
     wide_low = np.kron(eye, low.astype(np.float32))
     right = np.block([[wide_high, wide_low], [wide_high, wide_low]]).astype(jnp.bfloat16)
-    left = np.concatenate([high, high, low], 1)
+    order = np.concatenate([points[0::2], points[1::2]])
+    left = np.concatenate([part[order][:, order] for part in (high, high, low)], 1)
     eigenvalues = 2.0 - 2.0 * np.cos(points * (2.0 * math.pi / side))
-    shift = 1.0 / side**2 + eigenvalues[:, None] + np.tile(eigenvalues, 2)[None, :]
+    shift = 1.0 / side**2 + eigenvalues[order][:, None] + np.tile(eigenvalues, 2)[None, :]
     ratio = 1.0 + shift / 2 - np.sqrt(shift + shift**2 / 4)
     power = ratio**half_rows
     reach = ratio**GROUP
@@ -76,44 +77,35 @@
     return pltpu.roll(value, value.shape[-1] // 2, axis=value.ndim - 1)
 
 
-PARTS = 4
 DIGIT = 3
+
+
+def tiled(value, width):
+    count, slab_rows, cells = value.shape
+    value = value.reshape(count, slab_rows // GROUP, GROUP, cells // width, width)
+    return jnp.transpose(value, (0, 1, 3, 2, 4))
 
 
 def arrange_kernel(row, source, *refs):
     packed, raw, arrivals = refs[-3:]
-    slab_rows, cells = raw.shape
-    width = packed.shape[-1]
-    half = slab_rows // 2
-    lower = lax.broadcasted_iota(jnp.int32, (GROUP, width), 1) < width // 2
-    tiles = 4
-    parts = arrivals.shape[0]
-    part = cells // parts
-    copies = []
-    for k in range(parts):
-        lanes = pl.ds(k * part, part)
-        copies.append(
-            pltpu.make_async_copy(source.at[row, :, lanes], raw.at[:, lanes], arrivals.at[k])
-        )
-        copies[-1].start()
-
-    def tile_step(step, carry):
-        ys = pl.ds(pl.multiple_of(step * 2 * tiles, 2 * tiles), 2 * tiles)
-        for start in range(0, half, GROUP):
-            lines = []
-            for k in range(tiles):
-                lanes = pl.ds(pl.multiple_of((step * tiles + k) * width, width), width)
-                near = raw[pl.ds(start, GROUP), lanes]
-                far = raw[pl.ds(start + half, GROUP), lanes]
-                lines.append(jnp.where(lower, near, halves(far)))
-                lines.append(jnp.where(lower, halves(near), far))
-            packed[pl.ds(start, GROUP), ys, :] = jnp.swapaxes(jnp.stack(lines, 0), 0, 1)
-        return carry
-
-    steps = part // (width * tiles)
-    for k in range(parts):
-        copies[k].wait()
-        lax.fori_loop(k * steps, (k + 1) * steps, tile_step, 0)
+    groups, tiles, lines, width = raw.shape
+    flat = raw.reshape(groups * tiles * lines, width)
+    lower = lax.broadcasted_iota(jnp.int32, (tiles, width), 1) < width // 2
+    half = groups // 2
+    copies = [
+        pltpu.make_async_copy(source.at[row, g], raw.at[g], arrivals.at[g]) for g in range(groups)
+    ]
+    for g in range(half):
+        copies[g].start()
+        copies[g + half].start()
+    for g in range(half):
+        copies[g].wait()
+        copies[g + half].wait()
+        for k in range(lines):
+            near = flat[pl.ds(g * tiles * lines + k, tiles, stride=lines), :]
+            far = flat[pl.ds((g + half) * tiles * lines + k, tiles, stride=lines), :]
+            packed[g * lines + k, :tiles] = jnp.where(lower, near, halves(far))
+            packed[g * lines + k, tiles:] = jnp.where(lower, halves(near), far)
 
 
 def stack_kernel(first, second, own):
@@ -123,37 +115,25 @@
 
 def restore_kernel(row, flag, own, passed, arrived, *refs):
     out, raw, departures = refs[-3:]
-    slab_rows, cells = raw.shape
-    width = own.shape[-1]
-    half = slab_rows // 2
-    lower = lax.broadcasted_iota(jnp.int32, (GROUP, width), 1) < width // 2
+    groups, tiles, lines, width = raw.shape
+    flat = raw.reshape(groups * tiles * lines, width)
+    lower = lax.broadcasted_iota(jnp.int32, (tiles, width), 1) < width // 2
+    half = groups // 2
     weight = flag[0].astype(jnp.float32)
-    tiles = 4
-    parts = departures.shape[0]
-    part = cells // parts
-
-    def tile_step(step, carry):
-        ys = pl.ds(pl.multiple_of(step * 2 * tiles, 2 * tiles), 2 * tiles)
-        for start in range(0, half, GROUP):
-            planes = pl.ds(start, GROUP)
-            block = own[row, planes, ys, :] + weight * passed[planes, ys, :] + arrived[planes, ys, :]
-            block = jnp.swapaxes(block, 0, 1)
-            for k in range(tiles):
-                lanes = pl.ds(pl.multiple_of((step * tiles + k) * width, width), width)
-                even, odd = block[2 * k], block[2 * k + 1]
-                raw[planes, lanes] = jnp.where(lower, even, halves(odd))
-                raw[pl.ds(start + half, GROUP), lanes] = jnp.where(lower, halves(even), odd)
-        return carry
-
-    steps = part // (width * tiles)
-    copies = []
-    for k in range(parts):
-        lax.fori_loop(k * steps, (k + 1) * steps, tile_step, 0)
-        lanes = pl.ds(k * part, part)
-        copies.append(
-            pltpu.make_async_copy(raw.at[:, lanes], out.at[row, :, lanes], departures.at[k])
-        )
-        copies[-1].start()
+    copies = [
+        pltpu.make_async_copy(raw.at[g], out.at[row, g], departures.at[g]) for g in range(groups)
+    ]
+    for g in range(half):
+        for k in range(lines):
+            plane = g * lines + k
+            block = own[row, plane] + weight * passed[plane] + arrived[plane]
+            even, odd = block[:tiles], block[tiles:]
+            near = pl.ds(g * tiles * lines + k, tiles, stride=lines)
+            far = pl.ds((g + half) * tiles * lines + k, tiles, stride=lines)
+            flat[near, :] = jnp.where(lower, even, halves(odd))
+            flat[far, :] = jnp.where(lower, halves(even), odd)
+        copies[g].start()
+        copies[g + half].start()
     for copy in copies:
         copy.wait()
 
@@ -335,7 +315,8 @@
             cost_estimate=pl.CostEstimate(flops=0, bytes_accessed=1 << 20, transcendentals=0),
         )
 
-    source = pltpu.with_memory_space_constraint(orbitals, pltpu.HBM)
+    tiles = tiled(orbitals, 2 * side)
+    source = pltpu.with_memory_space_constraint(tiles, pltpu.HBM)
     fields, far = [], []
     for row in range(owned):
         field = call(
@@ -343,8 +324,8 @@
             one,
             [hbm] + [free] * row,
             scratch=[
-                pltpu.VMEM(orbitals.shape[1:], jnp.float32),
-                pltpu.SemaphoreType.DMA((PARTS,)),
+                pltpu.VMEM(tiles.shape[1:], jnp.float32),
+                pltpu.SemaphoreType.DMA(tiles.shape[1:2]),
             ],
         )(source, *fields)
         fields.append(field)
@@ -410,7 +391,7 @@
         if row + 1 < owned:
             after, near = brought(row + 1, joined)
     total = backward(inner_base, after, inner, total, inside=True)
-    out = jax.ShapeDtypeStruct(orbitals.shape, jnp.float32)
+    out = jax.ShapeDtypeStruct(tiles.shape, jnp.float32)
     result = None
     for row in range(owned):
         earlier = [] if result is None else [result]
@@ -420,12 +401,12 @@
             [smem] + [vmem] * 3 + [hbm] * len(earlier),
             out_specs=hbm,
             scratch=[
-                pltpu.VMEM(orbitals.shape[1:], jnp.float32),
-                pltpu.SemaphoreType.DMA((PARTS,)),
+                pltpu.VMEM(tiles.shape[1:], jnp.float32),
+                pltpu.SemaphoreType.DMA(tiles.shape[1:2]),
             ],
             aliases={4: 0} if earlier else {},
         )(flag, total, passed[row], arrived[row], *earlier)
-    return result
+    return jnp.transpose(result, (0, 1, 3, 2, 4)).reshape(orbitals.shape)
 
 
 def solution(mesh):

time: 83 us -> 82.1 us (0.989)
  Pallas kernels: 9.41 us -> 7.5 us
  waiting for transfers between devices: 48.3 us -> 49.3 us
    pallas_call x2, Pallas kernels: 3.09 us -> 1.97 us  [on_device(): call(functools.partial(restore_kernel, row), out, [smem] + [vmem] * 3 + [...]
    ppermute x4, waiting for transfers between devices: 31.6 us -> 32.6 us  [rotated(): return lax.ppermute(value, axis, pairs)]
  transfers between devices with their start and end apart: 13 -> 13, of which waited for: 11 -> 11; matrix products, arithmetic and copies ran while one was open for 1% -> 1% of each run, Pallas kernels for 7% -> 6%
where the time goes in v5:
time: 82.1 us; the launch traced here: 81.9 us
  waiting for transfers between devices  49.3 us (60%)
  starting transfers between devices  21.3 us (26%)
  Pallas kernels  7.5 us (9%)
  local copies, waits for them, and re-layouts  1.55 us (2%)
  between operations  1.51 us (2%)
    ppermute x4, waiting for transfers between devices, rotated(): return lax.ppermute(value, axis, pairs)  32.6 us
    ppermute x9, waiting for transfers between devices, swapped(): lax.ppermute(value, axis, [(source, source ^ 1) for source in range(count)])  16.7 us
    ppermute x4, starting transfers between devices, rotated(): return lax.ppermute(value, axis, pairs)  13.4 us
    ppermute x9, starting transfers between devices, swapped(): lax.ppermute(value, axis, [(source, source ^ 1) for source in range(count)])  7.88 us
    pallas_call x2, Pallas kernels, on_device(): call(functools.partial(arrange_kernel, row), one, [hbm] + [free] * row, s...  2.56 us
    pallas_call x2, Pallas kernels, on_device(): call(functools.partial(restore_kernel, row), out, [smem] + [vmem] * 3 + [...  1.97 us
  transfers between devices with their start and end apart: 13, of which 11 were waited for; matrix products, arithmetic and copies ran while one was open for 1% of the time, Pallas kernels for 6%

profile of v5, /device:TPU:0, one launch (start us, length us, event | category | flops | bytes accessed | tf_op | source)
XLA Modules:
  0.0 81.9 jit_solution(3120330008900875199)
XLA Ops:
  0.0 1.3 %shard_map.64.refs_0_.first.own = f32[16,64,128]{2,1,0:T(8,128)S(1)} custom-call(f32[2,4,32,8,128]{4,3,2,1,0:T(8,128)} %bitcast.29), custom_call_target="tpu_custom_call" | custom-call | bytes 1048576 | tf_op jit(solution)/shard_map/pallas_call | solution.py:322
  1.3 6.1 %collective-permute-start = (f32[16,64,128]{2,1,0:T(8,128)S(1)}, f32[16,64,128]{2,1,0:T(8,128)S(1)}, u32[]{:S(2)}, u32[]{:S(2)}) collective-permute-start(f32[16,64,128]{2,1,0:T(8,128)S(1)} %shard_map.64.refs_0_.first.own), channel_id=1, source_target_pairs={{0,28},{2,30},{4,0},{6,2},{8,4},{10,6},{12,8},{14,10},{16,12},{18,... | collective-permute-start | bytes 1572872 | tf_op jit(solution)/shard_map/ppermute | solution.py:19
  7.4 1.3 %shard_map.65.second.other.own = f32[16,64,128]{2,1,0:T(8,128)S(1)} custom-call(f32[2,4,32,8,128]{4,3,2,1,0:T(8,128)} %bitcast.30, f32[16,64,128]{2,1,0:T(8,128)S(1)} %shard_map.64.refs_0_.first.own), custom_call_target="tpu_custom_call" | custom-call | bytes 1048576 | tf_op jit(solution)/shard_map/pallas_call | solution.py:322
  9.3 0.0 copy-start.3
  9.3 0.7 copy-done.3
  10.0 0.7 fusion
  11.3 0.0 copy-start
  11.3 0.0 copy-start.1
  11.4 0.0 copy-start.2
  11.4 0.1 shard_map.66.after.own
  11.5 0.8 copy-done
  12.3 0.1 copy-done.1
  12.3 0.0 copy-done.2
  12.3 6.2 %collective-permute-done.far.other = f32[16,64,128]{2,1,0:T(8,128)S(1)} collective-permute-done((f32[16,64,128]{2,1,0:T(8,128)S(1)}, f32[16,64,128]{2,1,0:T(8,128)S(1)}, u32[]{:S(2)}, u32[]{:S(2)}) %collective-permute-start) | collective-permute-done | bytes 524320 | tf_op jit(solution)/shard_map/ppermute | solution.py:19
  18.6 0.1 collective-permute-start.1
  18.7 0.1 shard_map.69
  18.7 1.8 %collective-permute-done.1.other = f32[16,64,128]{2,1,0:T(8,128)S(1)} collective-permute-done((f32[16,64,128]{2,1,0:T(8,128)S(1)}, f32[16,64,128]{2,1,0:T(8,128)S(1)}, u32[]{:S(2)}, u32[]{:S(2)}) %collective-permute-start.1) | collective-permute-done | bytes 524320 | tf_op jit(solution)/shard_map/ppermute | solution.py:24
  20.6 1.5 %collective-permute-start.2 = (f32[2,64,128]{2,1,0:T(8,128)S(1)}, f32[2,64,128]{2,1,0:T(8,128)S(1)}, u32[]{:S(2)}, u32[]{:S(2)}) collective-permute-start(f32[2,64,128]{2,1,0:T(8,128)S(1)} %get-tuple-element.30.after.mine), channel_id=1, source_target_pairs={{0,1},{1,0},{2,3},{3,2},{4,5},{5,4},{6,7},{7,6},{8,9},{9,8},{10,11... | collective-permute-start | bytes 196616 | tf_op jit(solution)/shard_map/ppermute | solution.py:24
  22.1 2.8 %collective-permute-done.2.arrived = f32[2,64,128]{2,1,0:T(8,128)S(1)} collective-permute-done((f32[2,64,128]{2,1,0:T(8,128)S(1)}, f32[2,64,128]{2,1,0:T(8,128)S(1)}, u32[]{:S(2)}, u32[]{:S(2)}) %collective-permute-start.2) | collective-permute-done | bytes 65568 | tf_op jit(solution)/shard_map/ppermute | solution.py:24
  24.8 0.1 shard_map.71
  25.0 0.1 collective-permute-start.4
  25.1 7.3 %collective-permute-start.5 = (f32[16,64,128]{2,1,0:T(8,128)S(1)}, f32[16,64,128]{2,1,0:T(8,128)S(1)}, u32[]{:S(2)}, u32[]{:S(2)}) collective-permute-start(f32[16,64,128]{2,1,0:T(8,128)S(1)} %shard_map.65.second.other.own), channel_id=1, source_target_pairs={{0,28},{2,30},{4,0},{6,2},{8,4},{10,6},{12,8},{14,10},{16,12},{18,... | collective-permute-start | bytes 1572872 | tf_op jit(solution)/shard_map/ppermute | solution.py:19
  32.4 1.5 %collective-permute-start.3 = (f32[2,64,128]{2,1,0:T(8,128)S(1)}, f32[2,64,128]{2,1,0:T(8,128)S(1)}, u32[]{:S(2)}, u32[]{:S(2)}) collective-permute-start(f32[2,64,128]{2,1,0:T(8,128)S(1)} %get-tuple-element.29.after.mine), channel_id=1, source_target_pairs={{0,1},{1,0},{2,3},{3,2},{4,5},{5,4},{6,7},{7,6},{8,9},{9,8},{10,11... | collective-permute-start | bytes 196616 | tf_op jit(solution)/shard_map/ppermute | solution.py:24
  33.9 2.8 %collective-permute-done.3.arrived = f32[2,64,128]{2,1,0:T(8,128)S(1)} collective-permute-done((f32[2,64,128]{2,1,0:T(8,128)S(1)}, f32[2,64,128]{2,1,0:T(8,128)S(1)}, u32[]{:S(2)}, u32[]{:S(2)}) %collective-permute-start.3) | collective-permute-done | bytes 65568 | tf_op jit(solution)/shard_map/ppermute | solution.py:24
  36.6 0.1 shard_map.72
  36.8 0.0 collective-permute-done.4.handed.passed
  36.8 0.1 shard_map.73.after
  36.8 7.3 %collective-permute-done.5.far.other = f32[16,64,128]{2,1,0:T(8,128)S(1)} collective-permute-done((f32[16,64,128]{2,1,0:T(8,128)S(1)}, f32[16,64,128]{2,1,0:T(8,128)S(1)}, u32[]{:S(2)}, u32[]{:S(2)}) %collective-permute-start.5) | collective-permute-done | bytes 524320 | tf_op jit(solution)/shard_map/ppermute | solution.py:19
  44.2 0.1 collective-permute-start.6
  44.3 1.1 %shard_map.75 = (f32[2,16,64,128]{3,2,1,0:T(8,128)S(1)}, f32[2,2,2,64,128]{4,3,2,1,0:T(8,128)S(1)}, f32[2,64,128]{2,1,0:T(8,128)S(1)}) custom-call(s32[1]{0:T(128)} %bitcast.4.counts, f32[16,64,128]{2,1,0:T(8,128)S(1)} %shard_map.74.after, f32[2,16,64,128]{3,2,1,0:T(8,128)S(1)} %shard_map.66.after.own, f32[16,64,128]{2,1,0:T(8,128)S(1)} %collective-permute-done.5.far.other, ...), custom_call_target="tpu_custom_call" | custom-call | bytes 1048576 | tf_op jit(solution)/shard_map/pallas_call | solution.py:339
  45.3 0.8 %collective-permute-done.6.other = f32[16,64,128]{2,1,0:T(8,128)S(1)} collective-permute-done((f32[16,64,128]{2,1,0:T(8,128)S(1)}, f32[16,64,128]{2,1,0:T(8,128)S(1)}, u32[]{:S(2)}, u32[]{:S(2)}) %collective-permute-start.6) | collective-permute-done | bytes 524320 | tf_op jit(solution)/shard_map/ppermute | solution.py:24
  46.2 1.5 %collective-permute-start.7 = (f32[2,64,128]{2,1,0:T(8,128)S(1)}, f32[2,64,128]{2,1,0:T(8,128)S(1)}, u32[]{:S(2)}, u32[]{:S(2)}) collective-permute-start(f32[2,64,128]{2,1,0:T(8,128)S(1)} %get-tuple-element.39.after.mine), channel_id=1, source_target_pairs={{0,1},{1,0},{2,3},{3,2},{4,5},{5,4},{6,7},{7,6},{8,9},{9,8},{10,11... | collective-permute-start | bytes 196616 | tf_op jit(solution)/shard_map/ppermute | solution.py:24
  47.7 2.8 %collective-permute-done.7.arrived = f32[2,64,128]{2,1,0:T(8,128)S(1)} collective-permute-done((f32[2,64,128]{2,1,0:T(8,128)S(1)}, f32[2,64,128]{2,1,0:T(8,128)S(1)}, u32[]{:S(2)}, u32[]{:S(2)}) %collective-permute-start.7) | collective-permute-done | bytes 65568 | tf_op jit(solution)/shard_map/ppermute | solution.py:24
  50.4 0.1 shard_map.77
  50.6 0.1 collective-permute-start.9
  50.7 1.6 %collective-permute-start.8 = (f32[2,64,128]{2,1,0:T(8,128)S(1)}, f32[2,64,128]{2,1,0:T(8,128)S(1)}, u32[]{:S(2)}, u32[]{:S(2)}) collective-permute-start(f32[2,64,128]{2,1,0:T(8,128)S(1)} %get-tuple-element.38.after.mine), channel_id=1, source_target_pairs={{0,1},{1,0},{2,3},{3,2},{4,5},{5,4},{6,7},{7,6},{8,9},{9,8},{10,11... | collective-permute-start | bytes 196616 | tf_op jit(solution)/shard_map/ppermute | solution.py:24
  52.2 0.0 collective-permute-start.12
  52.2 2.9 %collective-permute-done.8.arrived = f32[2,64,128]{2,1,0:T(8,128)S(1)} collective-permute-done((f32[2,64,128]{2,1,0:T(8,128)S(1)}, f32[2,64,128]{2,1,0:T(8,128)S(1)}, u32[]{:S(2)}, u32[]{:S(2)}) %collective-permute-start.8) | collective-permute-done | bytes 65568 | tf_op jit(solution)/shard_map/ppermute | solution.py:24
  55.2 1.1 %shard_map.78 = (f32[2,16,64,128]{3,2,1,0:T(8,128)S(1)}, f32[16,64,128]{2,1,0:T(8,128)S(1)}) custom-call(s32[1]{0:T(128)} %bitcast.4.counts, f32[16,64,128]{2,1,0:T(8,128)S(1)} %get-tuple-element.43.after, f32[2,16,64,128]{3,2,1,0:T(8,128)S(1)} %shard_map.66.after.own, f32[16,64,128]{2,1,0:T(8,128)S(1)} %collective-permute-done.5.far.other, ...), custom_call_target="tpu_custom_call" | custom-call | bytes 1048576 | tf_op jit(solution)/shard_map/pallas_call | solution.py:353
  56.2 0.0 collective-permute-done.9.handed.passed
  56.2 0.1 shard_map.79.after
  56.3 0.1 collective-permute-start.11
  56.4 1.6 %collective-permute-start.10 = (f32[2,64,128]{2,1,0:T(8,128)S(1)}, f32[2,64,128]{2,1,0:T(8,128)S(1)}, u32[]{:S(2)}, u32[]{:S(2)}) collective-permute-start(f32[2,64,128]{2,1,0:T(8,128)S(1)} %get-tuple-element.28.after.mine), channel_id=1, source_target_pairs={{0,1},{1,0},{2,3},{3,2},{4,5},{5,4},{6,7},{7,6},{8,9},{9,8},{10,11... | collective-permute-start | bytes 196616 | tf_op jit(solution)/shard_map/ppermute | solution.py:24
  57.9 2.8 %collective-permute-done.10.arrived = f32[2,64,128]{2,1,0:T(8,128)S(1)} collective-permute-done((f32[2,64,128]{2,1,0:T(8,128)S(1)}, f32[2,64,128]{2,1,0:T(8,128)S(1)}, u32[]{:S(2)}, u32[]{:S(2)}) %collective-permute-start.10) | collective-permute-done | bytes 65568 | tf_op jit(solution)/shard_map/ppermute | solution.py:24
  60.7 0.1 shard_map.80.own
  60.8 9.4 %collective-permute-done.12.arrived = f32[16,64,128]{2,1,0:T(8,128)S(1)} collective-permute-done((f32[16,64,128]{2,1,0:T(8,128)S(1)}, f32[16,64,128]{2,1,0:T(8,128)S(1)}, u32[]{:S(2)}, u32[]{:S(2)}) %collective-permute-start.12) | collective-permute-done | bytes 524320 | tf_op jit(solution)/shard_map/ppermute | solution.py:19
  70.2 1.0 %shard_map.81.refs_0_ = f32[2,4,32,8,128]{4,3,2,1,0:T(8,128)} custom-call(s32[1]{0:T(128)} %bitcast.flag, f32[2,16,64,128]{3,2,1,0:T(8,128)S(1)} %shard_map.80.own, f32[16,64,128]{2,1,0:T(8,128)S(1)} %collective-permute-done.4.handed.passed, f32[16,64,128]{2,1,0:T(8,128)S(1)} %collective-permute-done.12.arrived), custom_call_target="tpu_custom_call" | custom-call | bytes 1048576 | tf_op jit(solution)/shard_map/pallas_call | solution.py:398
  71.2 9.7 %collective-permute-done.11.arrived = f32[16,64,128]{2,1,0:T(8,128)S(1)} collective-permute-done((f32[16,64,128]{2,1,0:T(8,128)S(1)}, f32[16,64,128]{2,1,0:T(8,128)S(1)}, u32[]{:S(2)}, u32[]{:S(2)}) %collective-permute-start.11) | collective-permute-done | bytes 524320 | tf_op jit(solution)/shard_map/ppermute | solution.py:19
  80.9 1.0 %shard_map.82 = f32[2,4,32,8,128]{4,3,2,1,0:T(8,128)} custom-call(s32[1]{0:T(128)} %bitcast.flag, f32[2,16,64,128]{3,2,1,0:T(8,128)S(1)} %shard_map.80.own, f32[16,64,128]{2,1,0:T(8,128)S(1)} %collective-permute-done.9.handed.passed, f32[16,64,128]{2,1,0:T(8,128)S(1)} %collective-permute-done.11.arrived, ...), custom_call_target="tpu_custom_call", output_to_operand_aliasing={{}: (4, {})} | custom-call | bytes 1048576 | tf_op jit(solution)/shard_map/pallas_call | solution.py:398
  (5 shorter events, 0.1 us)
Async XLA Ops:
  1.3 17.3 %collective-permute-start = (f32[16,64,128]{2,1,0:T(8,128)S(1)}, f32[16,64,128]{2,1,0:T(8,128)S(1)}, u32[]{:S(2)}, u32[]{:S(2)}) collective-permute-start(f32[16,64,128]{2,1,0:T(8,128)S(1)} %shard_map.64.refs_0_.first.own), channel_id=1, source_target_pairs={{0,28},{2,30},{4,0},{6,2},{8,4},{10,6},{12,8},{14,10},{16,12},{18,... | collective-permute-start | bytes 1572872 | tf_op jit(solution)/shard_map/ppermute | solution.py:19
  9.3 0.7 copy-start.3
  11.3 0.9 %copy-start = (f32[5,64,128]{2,1,0:T(8,128)S(1)}, f32[5,64,128]{2,1,0:T(8,128)}, u32[]{:S(2)}) copy-start(f32[5,64,128]{2,1,0:T(8,128)} %constant.68.clone.decay) | copy-start | bytes 491524
  11.3 1.0 %copy-start.1 = (bf16[256,256]{1,0:T(8,128)(2,1)S(1)}, bf16[256,256]{1,0:T(8,128)(2,1)}, u32[]{:S(2)}) copy-start(bf16[256,256]{1,0:T(8,128)(2,1)} %constant.66.clone.right_ref) | copy-start | bytes 393220
  11.4 1.0 %copy-start.2 = (bf16[64,192]{1,0:T(8,128)(2,1)S(1)}, bf16[64,192]{1,0:T(8,128)(2,1)}, u32[]{:S(2)}) copy-start(bf16[64,192]{1,0:T(8,128)(2,1)} %constant.67.clone.left_ref) | copy-start | bytes 73732
  18.6 2.0 %collective-permute-start.1 = (f32[16,64,128]{2,1,0:T(8,128)S(1)}, f32[16,64,128]{2,1,0:T(8,128)S(1)}, u32[]{:S(2)}, u32[]{:S(2)}) collective-permute-start(f32[16,64,128]{2,1,0:T(8,128)S(1)} %shard_map.68.after), channel_id=1, source_target_pairs={{0,2},{2,0},{4,6},{6,4},{8,10},{10,8},{12,14},{14,12},{16,18},{18,... | collective-permute-start | bytes 1572872 | tf_op jit(solution)/shard_map/ppermute | solution.py:24
  20.6 4.3 %collective-permute-start.2 = (f32[2,64,128]{2,1,0:T(8,128)S(1)}, f32[2,64,128]{2,1,0:T(8,128)S(1)}, u32[]{:S(2)}, u32[]{:S(2)}) collective-permute-start(f32[2,64,128]{2,1,0:T(8,128)S(1)} %get-tuple-element.30.after.mine), channel_id=1, source_target_pairs={{0,1},{1,0},{2,3},{3,2},{4,5},{5,4},{6,7},{7,6},{8,9},{9,8},{10,11... | collective-permute-start | bytes 196616 | tf_op jit(solution)/shard_map/ppermute | solution.py:24
  25.0 11.8 %collective-permute-start.4 = (f32[16,64,128]{2,1,0:T(8,128)S(1)}, f32[16,64,128]{2,1,0:T(8,128)S(1)}, u32[]{:S(2)}, u32[]{:S(2)}) collective-permute-start(f32[16,64,128]{2,1,0:T(8,128)S(1)} %get-tuple-element.33.after), channel_id=1, source_target_pairs={{0,2},{2,0},{4,6},{6,4},{8,10},{10,8},{12,14},{14,12},{16,18},{18,... | collective-permute-start | bytes 1572872 | tf_op jit(solution)/shard_map/ppermute | solution.py:24
  25.1 19.1 %collective-permute-start.5 = (f32[16,64,128]{2,1,0:T(8,128)S(1)}, f32[16,64,128]{2,1,0:T(8,128)S(1)}, u32[]{:S(2)}, u32[]{:S(2)}) collective-permute-start(f32[16,64,128]{2,1,0:T(8,128)S(1)} %shard_map.65.second.other.own), channel_id=1, source_target_pairs={{0,28},{2,30},{4,0},{6,2},{8,4},{10,6},{12,8},{14,10},{16,12},{18,... | collective-permute-start | bytes 1572872 | tf_op jit(solution)/shard_map/ppermute | solution.py:19
  32.4 4.3 %collective-permute-start.3 = (f32[2,64,128]{2,1,0:T(8,128)S(1)}, f32[2,64,128]{2,1,0:T(8,128)S(1)}, u32[]{:S(2)}, u32[]{:S(2)}) collective-permute-start(f32[2,64,128]{2,1,0:T(8,128)S(1)} %get-tuple-element.29.after.mine), channel_id=1, source_target_pairs={{0,1},{1,0},{2,3},{3,2},{4,5},{5,4},{6,7},{7,6},{8,9},{9,8},{10,11... | collective-permute-start | bytes 196616 | tf_op jit(solution)/shard_map/ppermute | solution.py:24
  44.2 2.0 %collective-permute-start.6 = (f32[16,64,128]{2,1,0:T(8,128)S(1)}, f32[16,64,128]{2,1,0:T(8,128)S(1)}, u32[]{:S(2)}, u32[]{:S(2)}) collective-permute-start(f32[16,64,128]{2,1,0:T(8,128)S(1)} %shard_map.74.after), channel_id=1, source_target_pairs={{0,2},{2,0},{4,6},{6,4},{8,10},{10,8},{12,14},{14,12},{16,18},{18,... | collective-permute-start | bytes 1572872 | tf_op jit(solution)/shard_map/ppermute | solution.py:24
  46.2 4.3 %collective-permute-start.7 = (f32[2,64,128]{2,1,0:T(8,128)S(1)}, f32[2,64,128]{2,1,0:T(8,128)S(1)}, u32[]{:S(2)}, u32[]{:S(2)}) collective-permute-start(f32[2,64,128]{2,1,0:T(8,128)S(1)} %get-tuple-element.39.after.mine), channel_id=1, source_target_pairs={{0,1},{1,0},{2,3},{3,2},{4,5},{5,4},{6,7},{7,6},{8,9},{9,8},{10,11... | collective-permute-start | bytes 196616 | tf_op jit(solution)/shard_map/ppermute | solution.py:24
  50.6 5.6 %collective-permute-start.9 = (f32[16,64,128]{2,1,0:T(8,128)S(1)}, f32[16,64,128]{2,1,0:T(8,128)S(1)}, u32[]{:S(2)}, u32[]{:S(2)}) collective-permute-start(f32[16,64,128]{2,1,0:T(8,128)S(1)} %get-tuple-element.43.after), channel_id=1, source_target_pairs={{0,2},{2,0},{4,6},{6,4},{8,10},{10,8},{12,14},{14,12},{16,18},{18,... | collective-permute-start | bytes 1572872 | tf_op jit(solution)/shard_map/ppermute | solution.py:24
  50.7 4.5 %collective-permute-start.8 = (f32[2,64,128]{2,1,0:T(8,128)S(1)}, f32[2,64,128]{2,1,0:T(8,128)S(1)}, u32[]{:S(2)}, u32[]{:S(2)}) collective-permute-start(f32[2,64,128]{2,1,0:T(8,128)S(1)} %get-tuple-element.38.after.mine), channel_id=1, source_target_pairs={{0,1},{1,0},{2,3},{3,2},{4,5},{5,4},{6,7},{7,6},{8,9},{9,8},{10,11... | collective-permute-start | bytes 196616 | tf_op jit(solution)/shard_map/ppermute | solution.py:24
  52.2 18.0 %collective-permute-start.12 = (f32[16,64,128]{2,1,0:T(8,128)S(1)}, f32[16,64,128]{2,1,0:T(8,128)S(1)}, u32[]{:S(2)}, u32[]{:S(2)}) collective-permute-start(f32[16,64,128]{2,1,0:T(8,128)S(1)} %shard_map.73.after), channel_id=1, source_target_pairs={{0,4},{2,6},{4,8},{6,10},{8,12},{10,14},{12,16},{14,18},{16,20},{1... | collective-permute-start | bytes 1572872 | tf_op jit(solution)/shard_map/ppermute | solution.py:19
  56.3 24.6 %collective-permute-start.11 = (f32[16,64,128]{2,1,0:T(8,128)S(1)}, f32[16,64,128]{2,1,0:T(8,128)S(1)}, u32[]{:S(2)}, u32[]{:S(2)}) collective-permute-start(f32[16,64,128]{2,1,0:T(8,128)S(1)} %shard_map.79.after), channel_id=1, source_target_pairs={{0,4},{2,6},{4,8},{6,10},{8,12},{10,14},{12,16},{14,18},{16,20},{1... | collective-permute-start | bytes 1572872 | tf_op jit(solution)/shard_map/ppermute | solution.py:19
  56.4 4.3 %collective-permute-start.10 = (f32[2,64,128]{2,1,0:T(8,128)S(1)}, f32[2,64,128]{2,1,0:T(8,128)S(1)}, u32[]{:S(2)}, u32[]{:S(2)}) collective-permute-start(f32[2,64,128]{2,1,0:T(8,128)S(1)} %get-tuple-element.28.after.mine), channel_id=1, source_target_pairs={{0,1},{1,0},{2,3},{3,2},{4,5},{5,4},{6,7},{7,6},{8,9},{9,8},{10,11... | collective-permute-start | bytes 196616 | tf_op jit(solution)/shard_map/ppermute | solution.py:24

commit v6 on v5

--- a/solution.py
+++ b/solution.py
@@ -13,15 +13,16 @@
 GROUP = 8
 
 
-def rotated(value, axis, steps):
+def rotated(value, axis, steps, parity):
     count = lax.axis_size(axis)
-    pairs = [(source, (source + steps) % count) for source in range(count)]
-    return lax.ppermute(value, axis, pairs)
-
-
-def swapped(value, axis):
+    sources = range(parity, count, 2)
+    return lax.ppermute(value, axis, [(source, (source + steps) % count) for source in sources])
+
+
+def swapped(value, axis, parities=(0, 1)):
     count = lax.axis_size(axis)
-    return lax.ppermute(value, axis, [(source, source ^ 1) for source in range(count)])
+    sources = [source for source in range(count) if source % 2 in parities]
+    return lax.ppermute(value, axis, [(source, source ^ 1) for source in sources])
 
 
 def split(value):
@@ -113,20 +114,22 @@
     own[1] = second[...]
 
 
-def restore_kernel(row, flag, own, passed, arrived, *refs):
+def restore_kernel(row, own, *refs):
+    terms = refs[:3]
     out, raw, departures = refs[-3:]
     groups, tiles, lines, width = raw.shape
     flat = raw.reshape(groups * tiles * lines, width)
     lower = lax.broadcasted_iota(jnp.int32, (tiles, width), 1) < width // 2
     half = groups // 2
-    weight = flag[0].astype(jnp.float32)
     copies = [
         pltpu.make_async_copy(raw.at[g], out.at[row, g], departures.at[g]) for g in range(groups)
     ]
     for g in range(half):
         for k in range(lines):
             plane = g * lines + k
-            block = own[row, plane] + weight * passed[plane] + arrived[plane]
+            block = own[row, plane]
+            for term in terms:
+                block = block + term[plane]
             even, odd = block[:tiles], block[tiles:]
             near = pl.ds(g * tiles * lines + k, tiles, stride=lines)
             far = pl.ds((g + half) * tiles * lines + k, tiles, stride=lines)
@@ -138,19 +141,18 @@
         copy.wait()
 
 
-def pick_kernel(flag, after, far, own, out):
-    @pl.when(flag[0] == 0)
+def pick_kernel(counts, after, even, odd, out):
+    @pl.when(counts[0] & 1 == 0)
     def _():
-        out[...] = far[...]
-
-    @pl.when(flag[0] == 1)
+        out[...] = even[...]
+
+    @pl.when(counts[0] & 1 == 1)
     def _():
-        out[...] = own[...]
-
-
-def join_kernel(flag, after, distant, handed, out):
-    weight = 1.0 - flag[0].astype(jnp.float32)
-    out[...] = distant[...] + weight * handed[...]
+        out[...] = odd[...]
+
+
+def join_kernel(after, distant, handed, out):
+    out[...] = distant[...] + handed[...]
 
 
 def slab_moments(moments, i, reach):
@@ -274,7 +276,8 @@
     live = jnp.arange(first.shape[0]) < pair_count[0]
     distance = (partner // owned - band_index) % band_count
     inside = (REACH * owned) * owned
-    place = ((partner % owned) * REACH + distance - 1) * owned + first
+    side = jnp.where(distance == REACH - band_index % 2, 0, 1)
+    place = ((partner % owned) * REACH + side) * owned + first
     place = jnp.where(distance == 0, inside, place)
     return jnp.sum(jnp.where(live, lax.shift_left(1, DIGIT * place), 0))
 
@@ -317,7 +320,7 @@
 
     tiles = tiled(orbitals, 2 * side)
     source = pltpu.with_memory_space_constraint(tiles, pltpu.HBM)
-    fields, far = [], []
+    fields, leading, neighbour = [], [], []
     for row in range(owned):
         field = call(
             functools.partial(arrange_kernel, row),
@@ -329,9 +332,9 @@
             ],
         )(source, *fields)
         fields.append(field)
-        far.append(rotated(field, "band", -2))
+        leading.append(rotated(field, "band", -2, 0))
+        neighbour.append(swapped(field, "band", (1,)))
     own = call(stack_kernel, both, [vmem, vmem])(*fields)
-    flag = (band_index % 2).reshape(1)
     counts = pair_counts(pair_list, pair_count, owned, band_index, band_count)
     counts = (lax.optimization_barrier(counts) * 2 + band_index % 2).reshape(1)
 
@@ -357,40 +360,53 @@
             scratch=[pltpu.VMEM((chunks, 2) + shape[1:], jnp.float32)],
         )(counts, after, own, *state, right, left, decay, *total)
 
+    def chosen(after, even, odd):
+        return call(pick_kernel, one, [smem, free, vmem, vmem])(counts, after, even, odd)
+
+    def solved(base, after, other):
+        spectrum, moments, mine = forward(base, after, other)
+        return (other, spectrum, moments, mine, exchanged(mine))
+
+    def joined(after, mine, handed):
+        return call(join_kernel, one, [free, vmem, vmem])(after, mine, handed)
+
+    def sent(value, steps, parity):
+        return rotated(value, "band", steps, parity)
+
+    def crossed(value, parity):
+        return swapped(value, "band", (parity,))
+
     inner_base = REACH * owned * owned
-    spectrum, moments, mine = forward(inner_base, own, fields[1])
-    inner = (fields[1], spectrum, moments, mine, exchanged(mine))
-    after = mine
-
-    def brought(row, after):
-        picked = call(pick_kernel, one, [smem, free, vmem, vmem])(
-            flag, after, far[row], fields[row]
-        )
-        return picked, swapped(picked, "band")
-
-    total, passed, arrived = (), [], []
-    after, near = brought(0, after)
-    for row in range(owned):
-        base = row * REACH * owned
-        distant_state = forward(base + owned, after, far[row])
-        distant_ends = exchanged(distant_state[2])
-        near_state = forward(base, distant_state[2], near)
-        mine = near_state[2]
-        near_state = (near,) + tuple(near_state) + (exchanged(mine),)
-        distant_state = (far[row],) + tuple(distant_state) + (distant_ends,)
-        acc, handed = backward(base, mine, near_state, total)
-        handed_over = swapped(handed, "band")
-        acc, distant = backward(base + owned, handed, distant_state, (acc,))
-        total = (acc,)
-        joined = call(join_kernel, one, [smem, free, vmem, vmem])(
-            flag, distant, distant, handed_over
-        )
-        passed.append(handed_over)
-        arrived.append(rotated(joined, "band", 2))
-        after = joined
-        if row + 1 < owned:
-            after, near = brought(row + 1, joined)
-    total = backward(inner_base, after, inner, total, inside=True)
+    step = REACH * owned
+    inner = solved(inner_base, own, fields[1])
+    copies = [crossed(leading[row], 0) for row in range(owned)]
+    trailing = [sent(fields[row], -2, 1) for row in range(owned)]
+
+    picked = chosen(inner[3], leading[0], copies[0])
+    first = solved(0, picked, picked)
+    total, first_part = backward(0, first[3], first, ())
+    first_handed = crossed(first_part, 1)
+    picked = chosen(first_part, leading[1], copies[1])
+    second = solved(step, picked, picked)
+    first_sum = joined(second[3], first_part, first_handed)
+    lead_back = [sent(first_sum, 2, 0)]
+
+    picked = chosen(first_sum, neighbour[0], trailing[0])
+    third = solved(owned, picked, picked)
+    total, second_part = backward(step, third[3], second, (total,))
+    second_handed = crossed(second_part, 1)
+    second_sum = joined(second_part, second_part, second_handed)
+    lead_back.append(sent(second_sum, 2, 0))
+
+    picked = chosen(second_sum, neighbour[1], trailing[1])
+    fourth = solved(step + owned, picked, picked)
+    total, third_part = backward(owned, fourth[3], third, (total,))
+    trail_back = [sent(third_part, 2, 1)]
+    given = [crossed(third_part, 0)]
+    total, fourth_part = backward(step + owned, third_part, fourth, (total,))
+    trail_back.append(sent(fourth_part, 2, 1))
+    given.append(crossed(fourth_part, 0))
+    total = backward(inner_base, fourth_part, inner, (total,), inside=True)
     out = jax.ShapeDtypeStruct(tiles.shape, jnp.float32)
     result = None
     for row in range(owned):
@@ -398,14 +414,14 @@
         result = call(
             functools.partial(restore_kernel, row),
             out,
-            [smem] + [vmem] * 3 + [hbm] * len(earlier),
+            [vmem] * 4 + [hbm] * len(earlier),
             out_specs=hbm,
             scratch=[
                 pltpu.VMEM(tiles.shape[1:], jnp.float32),
                 pltpu.SemaphoreType.DMA(tiles.shape[1:2]),
             ],
             aliases={4: 0} if earlier else {},
-        )(flag, total, passed[row], arrived[row], *earlier)
+        )(total, given[row], lead_back[row], trail_back[row], *earlier)
     return jnp.transpose(result, (0, 1, 3, 2, 4)).reshape(orbitals.shape)
 
 

time: 82.1 us -> 96.2 us (1.17)
  the two profiles are of different devices: /device:TPU:0 before, /device:TPU:1 now
where the time goes in v6:
time: 96.2 us; the launch traced here: 95.6 us
  starting transfers between devices  49.8 us (52%)
  waiting for transfers between devices  33.7 us (35%)
  Pallas kernels  8.84 us (9%)
  between operations  1.82 us (2%)
    ppermute x13, starting transfers between devices, swapped(): lax.ppermute(value, axis, [(source, source ^ 1) for source in sources])  28.3 us
    ppermute x8, waiting for transfers between devices, rotated(): lax.ppermute(value, axis, [(source, (source + steps) % count) for source...  23.7 us
    ppermute x8, starting transfers between devices, rotated(): lax.ppermute(value, axis, [(source, (source + steps) % count) for source...  21.5 us
    ppermute x13, waiting for transfers between devices, swapped(): lax.ppermute(value, axis, [(source, source ^ 1) for source in sources])  10.1 us
    pallas_call x2, Pallas kernels, on_device(): call(functools.partial(arrange_kernel, row), one, [hbm] + [free] * row, s...  2.56 us
    pallas_call x2, Pallas kernels, on_device(): call(functools.partial(restore_kernel, row), out, [vmem] * 4 + [hbm] * le...  1.98 us
  transfers between devices with their start and end apart: 21, of which 6 were waited for; matrix products, arithmetic and copies ran while one was open for 1% of the time, Pallas kernels for 7%

profile of v6, /device:TPU:1, one launch (start us, length us, event | category | flops | bytes accessed | tf_op | source)
XLA Modules:
  0.0 95.6 jit_solution(6749527055045825397)
XLA Ops:
  0.0 1.3 %shard_map.64.refs_0_.first = f32[16,64,128]{2,1,0:T(8,128)S(1)} custom-call(f32[2,4,32,8,128]{4,3,2,1,0:T(8,128)} %bitcast.28), custom_call_target="tpu_custom_call" | custom-call | bytes 1048576 | tf_op jit(solution)/shard_map/pallas_call | solution.py:325
  1.3 0.7 collective-permute-start
  2.0 0.0 collective-permute-done.even
  2.0 1.3 %collective-permute-start.1 = (f32[16,64,128]{2,1,0:T(8,128)S(1)}, f32[16,64,128]{2,1,0:T(8,128)}, u32[]{:S(2)}, u32[]{:S(2)}) collective-permute-start(f32[16,64,128]{2,1,0:T(8,128)S(1)} %collective-permute-done.even), channel_id=1, source_target_pairs={{0,2},{4,6},{8,10},{12,14},{16,18},{20,22},{24,26},{28,30},{1,3},{... | collective-permute-start | bytes 1572872 | tf_op jit(solution)/shard_map/ppermute | solution.py:25
  3.3 1.3 %shard_map.65.second.other = f32[16,64,128]{2,1,0:T(8,128)S(1)} custom-call(f32[2,4,32,8,128]{4,3,2,1,0:T(8,128)} %bitcast.29, f32[16,64,128]{2,1,0:T(8,128)S(1)} %shard_map.64.refs_0_.first), custom_call_target="tpu_custom_call" | custom-call | bytes 1048576 | tf_op jit(solution)/shard_map/pallas_call | solution.py:325
  4.6 0.7 collective-permute-start.3
  5.3 0.0 copy-start
  5.3 0.0 copy-start.1
  5.3 0.0 copy-start.2
  5.3 0.1 shard_map.66.after.own
  6.1 0.0 copy-start.3
  6.1 0.7 copy-done.3
  6.8 0.7 fusion
  8.3 1.0 %shard_map.67 = (f32[2,16,64,128]{3,2,1,0:T(8,128)S(1)}, f32[2,2,2,64,128]{4,3,2,1,0:T(8,128)S(1)}, f32[2,64,128]{2,1,0:T(8,128)S(1)}) custom-call(s32[1]{0:T(128)} %bitcast.3.counts, f32[2,16,64,128]{3,2,1,0:T(8,128)S(1)} %shard_map.66.after.own, f32[2,16,64,128]{3,2,1,0:T(8,128)S(1)} %shard_map.66.after.own, f32[16,64,128]{2,1,0:T(8,128)S(1)} %shard_map.65.second.other, ...), custom_call_target="tpu_custom_call" | custom-call | bytes 1048576 | tf_op jit(solution)/shard_map/pallas_call | solution.py:342
  9.3 9.4 %collective-permute-done.1.odd = f32[16,64,128]{2,1,0:T(8,128)} collective-permute-done((f32[16,64,128]{2,1,0:T(8,128)S(1)}, f32[16,64,128]{2,1,0:T(8,128)}, u32[]{:S(2)}, u32[]{:S(2)}) %collective-permute-start.1) | collective-permute-done | bytes 524320 | tf_op jit(solution)/shard_map/ppermute | solution.py:25
  18.7 1.1 %shard_map.68.after.other = f32[16,64,128]{2,1,0:T(8,128)S(1)} custom-call(s32[1]{0:T(128)} %bitcast.3.counts, f32[2,64,128]{2,1,0:T(8,128)S(1)} %get-tuple-element.28.after.mine, f32[16,64,128]{2,1,0:T(8,128)S(1)} %collective-permute-done.even, f32[16,64,128]{2,1,0:T(8,128)} %collective-permute-done.1.odd), custom_call_target="tpu_custom_call" | custom-call | bytes 1048576 | tf_op jit(solution)/shard_map/pallas_call | solution.py:364
  19.8 0.1 shard_map.69
  19.9 1.3 %collective-permute-start.2 = (f32[2,64,128]{2,1,0:T(8,128)S(1)}, f32[2,64,128]{2,1,0:T(8,128)S(1)}, u32[]{:S(2)}, u32[]{:S(2)}) collective-permute-start(f32[2,64,128]{2,1,0:T(8,128)S(1)} %get-tuple-element.29.after.mine), channel_id=1, source_target_pairs={{0,1},{1,0},{2,3},{3,2},{4,5},{5,4},{6,7},{7,6},{8,9},{9,8},{10,11... | collective-permute-start | bytes 196616 | tf_op jit(solution)/shard_map/ppermute | solution.py:25
  21.1 0.0 collective-permute-done.3.even
  21.2 1.3 %collective-permute-start.4 = (f32[16,64,128]{2,1,0:T(8,128)S(1)}, f32[16,64,128]{2,1,0:T(8,128)S(1)}, u32[]{:S(2)}, u32[]{:S(2)}) collective-permute-start(f32[16,64,128]{2,1,0:T(8,128)S(1)} %collective-permute-done.3.even), channel_id=1, source_target_pairs={{0,2},{4,6},{8,10},{12,14},{16,18},{20,22},{24,26},{28,30},{1,3},{... | collective-permute-start | bytes 1572872 | tf_op jit(solution)/shard_map/ppermute | solution.py:25
  22.4 0.6 collective-permute-done.2.arrived
  23.1 0.1 shard_map.70
  23.2 13.8 %collective-permute-start.5 = (f32[16,64,128]{2,1,0:T(8,128)S(1)}, f32[16,64,128]{2,1,0:T(8,128)S(1)}, u32[]{:S(2)}, u32[]{:S(2)}) collective-permute-start(f32[16,64,128]{2,1,0:T(8,128)S(1)} %get-tuple-element.32.after.distant), channel_id=1, source_target_pairs={{2,0},{6,4},{10,8},{14,12},{18,16},{22,20},{26,24},{30,28},{3,1},{... | collective-permute-start | bytes 1572872 | tf_op jit(solution)/shard_map/ppermute | solution.py:25
  37.0 1.3 %collective-permute-start.6 = (f32[16,64,128]{2,1,0:T(8,128)S(1)}, f32[16,64,128]{2,1,0:T(8,128)S(1)}, u32[]{:S(2)}, u32[]{:S(2)}) collective-permute-start(f32[16,64,128]{2,1,0:T(8,128)S(1)} %shard_map.64.refs_0_.first), channel_id=1, source_target_pairs={{2,0},{6,4},{10,8},{14,12},{18,16},{22,20},{26,24},{30,28},{3,1},{... | collective-permute-start | bytes 1572872 | tf_op jit(solution)/shard_map/ppermute | solution.py:25
  38.4 7.2 %collective-permute-start.7 = (f32[16,64,128]{2,1,0:T(8,128)S(1)}, f32[16,64,128]{2,1,0:T(8,128)S(1)}, u32[]{:S(2)}, u32[]{:S(2)}) collective-permute-start(f32[16,64,128]{2,1,0:T(8,128)S(1)} %shard_map.64.refs_0_.first), channel_id=1, source_target_pairs={{2,30},{6,2},{10,6},{14,10},{18,14},{22,18},{26,22},{30,26},{3,31}... | collective-permute-start | bytes 1572872 | tf_op jit(solution)/shard_map/ppermute | solution.py:19
  45.6 0.0 collective-permute-done.4.odd
  45.6 0.1 shard_map.72
  45.7 1.3 %collective-permute-start.8 = (f32[2,64,128]{2,1,0:T(8,128)S(1)}, f32[2,64,128]{2,1,0:T(8,128)S(1)}, u32[]{:S(2)}, u32[]{:S(2)}) collective-permute-start(f32[2,64,128]{2,1,0:T(8,128)S(1)} %get-tuple-element.33.after.mine), channel_id=1, source_target_pairs={{0,1},{1,0},{2,3},{3,2},{4,5},{5,4},{6,7},{7,6},{8,9},{9,8},{10,11... | collective-permute-start | bytes 196616 | tf_op jit(solution)/shard_map/ppermute | solution.py:25
  47.0 0.0 collective-permute-done.5.handed
  47.0 0.1 shard_map.73.after
  47.0 0.0 collective-permute-done.6.even
  47.1 4.6 %collective-permute-done.7.odd = f32[16,64,128]{2,1,0:T(8,128)S(1)} collective-permute-done((f32[16,64,128]{2,1,0:T(8,128)S(1)}, f32[16,64,128]{2,1,0:T(8,128)S(1)}, u32[]{:S(2)}, u32[]{:S(2)}) %collective-permute-start.7) | collective-permute-done | bytes 524320 | tf_op jit(solution)/shard_map/ppermute | solution.py:19
  51.7 0.1 shard_map.75
  51.8 0.0 collective-permute-done.8.arrived
  51.8 0.1 shard_map.76
  52.0 1.3 %collective-permute-start.9 = (f32[16,64,128]{2,1,0:T(8,128)S(1)}, f32[16,64,128]{2,1,0:T(8,128)S(1)}, u32[]{:S(2)}, u32[]{:S(2)}) collective-permute-start(f32[16,64,128]{2,1,0:T(8,128)S(1)} %get-tuple-element.38.after.distant), channel_id=1, source_target_pairs={{2,0},{6,4},{10,8},{14,12},{18,16},{22,20},{26,24},{30,28},{3,1},{... | collective-permute-start | bytes 1572872 | tf_op jit(solution)/shard_map/ppermute | solution.py:25
  53.3 1.3 %collective-permute-start.10 = (f32[16,64,128]{2,1,0:T(8,128)S(1)}, f32[16,64,128]{2,1,0:T(8,128)S(1)}, u32[]{:S(2)}, u32[]{:S(2)}) collective-permute-start(f32[16,64,128]{2,1,0:T(8,128)S(1)} %shard_map.65.second.other), channel_id=1, source_target_pairs={{2,0},{6,4},{10,8},{14,12},{18,16},{22,20},{26,24},{30,28},{3,1},{... | collective-permute-start | bytes 1572872 | tf_op jit(solution)/shard_map/ppermute | solution.py:25
  54.6 6.5 %collective-permute-start.11 = (f32[16,64,128]{2,1,0:T(8,128)S(1)}, f32[16,64,128]{2,1,0:T(8,128)S(1)}, u32[]{:S(2)}, u32[]{:S(2)}) collective-permute-start(f32[16,64,128]{2,1,0:T(8,128)S(1)} %shard_map.65.second.other), channel_id=1, source_target_pairs={{2,30},{6,2},{10,6},{14,10},{18,14},{22,18},{26,22},{30,26},{3,31}... | collective-permute-start | bytes 1572872 | tf_op jit(solution)/shard_map/ppermute | solution.py:19
  61.1 0.7 collective-permute-start.19
  61.8 1.3 %collective-permute-start.12 = (f32[2,64,128]{2,1,0:T(8,128)S(1)}, f32[2,64,128]{2,1,0:T(8,128)S(1)}, u32[]{:S(2)}, u32[]{:S(2)}) collective-permute-start(f32[2,64,128]{2,1,0:T(8,128)S(1)} %get-tuple-element.34.after.mine), channel_id=1, source_target_pairs={{0,1},{1,0},{2,3},{3,2},{4,5},{5,4},{6,7},{7,6},{8,9},{9,8},{10,11... | collective-permute-start | bytes 196616 | tf_op jit(solution)/shard_map/ppermute | solution.py:25
  63.1 0.0 collective-permute-done.9.handed
  63.1 0.1 shard_map.77.after
  63.2 0.0 collective-permute-done.10.even
  63.2 4.1 %collective-permute-done.11.odd = f32[16,64,128]{2,1,0:T(8,128)S(1)} collective-permute-done((f32[16,64,128]{2,1,0:T(8,128)S(1)}, f32[16,64,128]{2,1,0:T(8,128)S(1)}, u32[]{:S(2)}, u32[]{:S(2)}) %collective-permute-start.11) | collective-permute-done | bytes 524320 | tf_op jit(solution)/shard_map/ppermute | solution.py:19
  67.3 0.1 shard_map.79
  67.3 1.3 %collective-permute-start.13 = (f32[2,64,128]{2,1,0:T(8,128)S(1)}, f32[2,64,128]{2,1,0:T(8,128)S(1)}, u32[]{:S(2)}, u32[]{:S(2)}) collective-permute-start(f32[2,64,128]{2,1,0:T(8,128)S(1)} %get-tuple-element.39.after.mine), channel_id=1, source_target_pairs={{0,1},{1,0},{2,3},{3,2},{4,5},{5,4},{6,7},{7,6},{8,9},{9,8},{10,11... | collective-permute-start | bytes 196616 | tf_op jit(solution)/shard_map/ppermute | solution.py:25
  68.6 0.3 collective-permute-start.14
  68.9 0.0 collective-permute-done.12.arrived
  68.9 0.1 shard_map.80
  69.0 1.3 %collective-permute-start.18 = (f32[16,64,128]{2,1,0:T(8,128)S(1)}, f32[16,64,128]{2,1,0:T(8,128)S(1)}, u32[]{:S(2)}, u32[]{:S(2)}) collective-permute-start(f32[16,64,128]{2,1,0:T(8,128)S(1)} %get-tuple-element.43.after), channel_id=1, source_target_pairs={{0,2},{4,6},{8,10},{12,14},{16,18},{20,22},{24,26},{28,30},{1,3},{... | collective-permute-start | bytes 1572872 | tf_op jit(solution)/shard_map/ppermute | solution.py:25
  70.3 2.2 %collective-permute-start.20 = (f32[16,64,128]{2,1,0:T(8,128)S(1)}, f32[16,64,128]{2,1,0:T(8,128)S(1)}, u32[]{:S(2)}, u32[]{:S(2)}) collective-permute-start(f32[16,64,128]{2,1,0:T(8,128)S(1)} %get-tuple-element.43.after), channel_id=1, source_target_pairs={{2,6},{6,10},{10,14},{14,18},{18,22},{22,26},{26,30},{30,2},{3,7},... | collective-permute-start | bytes 1572872 | tf_op jit(solution)/shard_map/ppermute | solution.py:19
  72.5 0.0 collective-permute-done.13.arrived
  72.5 0.7 collective-permute-start.16
  73.2 0.1 shard_map.81
  73.3 0.0 collective-permute-done.14.arrived
  73.4 1.3 %collective-permute-start.15 = (f32[16,64,128]{2,1,0:T(8,128)S(1)}, f32[16,64,128]{2,1,0:T(8,128)S(1)}, u32[]{:S(2)}, u32[]{:S(2)}) collective-permute-start(f32[16,64,128]{2,1,0:T(8,128)S(1)} %get-tuple-element.47.after), channel_id=1, source_target_pairs={{0,2},{4,6},{8,10},{12,14},{16,18},{20,22},{24,26},{28,30},{1,3},{... | collective-permute-start | bytes 1572872 | tf_op jit(solution)/shard_map/ppermute | solution.py:25
  74.7 0.0 collective-permute-done.19.refs_1_
  74.7 2.9 %collective-permute-start.17 = (f32[16,64,128]{2,1,0:T(8,128)S(1)}, f32[16,64,128]{2,1,0:T(8,128)S(1)}, u32[]{:S(2)}, u32[]{:S(2)}) collective-permute-start(f32[16,64,128]{2,1,0:T(8,128)S(1)} %get-tuple-element.47.after), channel_id=1, source_target_pairs={{2,6},{6,10},{10,14},{14,18},{18,22},{22,26},{26,30},{30,2},{3,7},... | collective-permute-start | bytes 1572872 | tf_op jit(solution)/shard_map/ppermute | solution.py:19
  77.5 1.1 %shard_map.82.own = f32[2,16,64,128]{3,2,1,0:T(8,128)S(1)} custom-call(s32[1]{0:T(128)} %bitcast.3.counts, f32[16,64,128]{2,1,0:T(8,128)S(1)} %get-tuple-element.47.after, f32[2,16,64,128]{3,2,1,0:T(8,128)S(1)} %shard_map.66.after.own, f32[16,64,128]{2,1,0:T(8,128)S(1)} %shard_map.65.second.other, f32[2,16,64,128]{3,2,1,0:T(8,128)S(1)} %get-tuple-element.48.spectrum, ...), custom_call_target="tpu_custom_call" | custom-call | bytes 1048576 | tf_op jit(solution)/shard_map/pallas_call | solution.py:356
  78.6 8.6 %collective-permute-done.20.refs_2_ = f32[16,64,128]{2,1,0:T(8,128)S(1)} collective-permute-done((f32[16,64,128]{2,1,0:T(8,128)S(1)}, f32[16,64,128]{2,1,0:T(8,128)S(1)}, u32[]{:S(2)}, u32[]{:S(2)}) %collective-permute-start.20) | collective-permute-done | bytes 524320 | tf_op jit(solution)/shard_map/ppermute | solution.py:19
  87.2 1.0 %shard_map.83.refs_3_ = f32[2,4,32,8,128]{4,3,2,1,0:T(8,128)} custom-call(f32[2,16,64,128]{3,2,1,0:T(8,128)S(1)} %shard_map.82.own, f32[16,64,128]{2,1,0:T(8,128)S(1)} %collective-permute-done.18.refs_0_, f32[16,64,128]{2,1,0:T(8,128)S(1)} %collective-permute-done.19.refs_1_, f32[16,64,128]{2,1,0:T(8,128)S(1)} %collective-permute-done.20.refs_2_), custom_call_target="tpu_custom_call" | custom-call | bytes 1048576 | tf_op jit(solution)/shard_map/pallas_call | solution.py:414
  88.2 0.0 collective-permute-done.15.refs_0_
  88.3 6.4 %collective-permute-done.17.refs_2_ = f32[16,64,128]{2,1,0:T(8,128)S(1)} collective-permute-done((f32[16,64,128]{2,1,0:T(8,128)S(1)}, f32[16,64,128]{2,1,0:T(8,128)S(1)}, u32[]{:S(2)}, u32[]{:S(2)}) %collective-permute-start.17) | collective-permute-done | bytes 524320 | tf_op jit(solution)/shard_map/ppermute | solution.py:19
  94.6 1.0 %shard_map.84 = f32[2,4,32,8,128]{4,3,2,1,0:T(8,128)} custom-call(f32[2,16,64,128]{3,2,1,0:T(8,128)S(1)} %shard_map.82.own, f32[16,64,128]{2,1,0:T(8,128)S(1)} %collective-permute-done.15.refs_0_, f32[16,64,128]{2,1,0:T(8,128)S(1)} %collective-permute-done.16.refs_1_, ...), custom_call_target="tpu_custom_call", output_to_operand_aliasing={{}: (4, {})} | custom-call | bytes 1048576 | tf_op jit(solution)/shard_map/pallas_call | solution.py:414
  (8 shorter events, 0.1 us)
Async XLA Ops:
  1.3 0.7 collective-permute-start
  2.0 16.7 %collective-permute-start.1 = (f32[16,64,128]{2,1,0:T(8,128)S(1)}, f32[16,64,128]{2,1,0:T(8,128)}, u32[]{:S(2)}, u32[]{:S(2)}) collective-permute-start(f32[16,64,128]{2,1,0:T(8,128)S(1)} %collective-permute-done.even), channel_id=1, source_target_pairs={{0,2},{4,6},{8,10},{12,14},{16,18},{20,22},{24,26},{28,30},{1,3},{... | collective-permute-start | bytes 1572872 | tf_op jit(solution)/shard_map/ppermute | solution.py:25
  4.6 16.6 %collective-permute-start.3 = (f32[16,64,128]{2,1,0:T(8,128)S(1)}, f32[16,64,128]{2,1,0:T(8,128)S(1)}, u32[]{:S(2)}, u32[]{:S(2)}) collective-permute-start(f32[16,64,128]{2,1,0:T(8,128)S(1)} %shard_map.65.second.other), channel_id=1, source_target_pairs={{0,28},{4,0},{8,4},{12,8},{16,12},{20,16},{24,20},{28,24},{1,29},{... | collective-permute-start | bytes 1572872 | tf_op jit(solution)/shard_map/ppermute | solution.py:19
  5.3 2.9 %copy-start = (f32[5,64,128]{2,1,0:T(8,128)S(1)}, f32[5,64,128]{2,1,0:T(8,128)}, u32[]{:S(2)}) copy-start(f32[5,64,128]{2,1,0:T(8,128)} %constant.68.clone.decay) | copy-start | bytes 491524
  5.3 2.9 %copy-start.1 = (bf16[256,256]{1,0:T(8,128)(2,1)S(1)}, bf16[256,256]{1,0:T(8,128)(2,1)}, u32[]{:S(2)}) copy-start(bf16[256,256]{1,0:T(8,128)(2,1)} %constant.66.clone.right_ref) | copy-start | bytes 393220
  5.3 2.9 %copy-start.2 = (bf16[64,192]{1,0:T(8,128)(2,1)S(1)}, bf16[64,192]{1,0:T(8,128)(2,1)}, u32[]{:S(2)}) copy-start(bf16[64,192]{1,0:T(8,128)(2,1)} %constant.67.clone.left_ref) | copy-start | bytes 73732
  6.1 0.7 copy-start.3
  19.9 3.2 %collective-permute-start.2 = (f32[2,64,128]{2,1,0:T(8,128)S(1)}, f32[2,64,128]{2,1,0:T(8,128)S(1)}, u32[]{:S(2)}, u32[]{:S(2)}) collective-permute-start(f32[2,64,128]{2,1,0:T(8,128)S(1)} %get-tuple-element.29.after.mine), channel_id=1, source_target_pairs={{0,1},{1,0},{2,3},{3,2},{4,5},{5,4},{6,7},{7,6},{8,9},{9,8},{10,11... | collective-permute-start | bytes 196616 | tf_op jit(solution)/shard_map/ppermute | solution.py:25
  21.2 24.4 %collective-permute-start.4 = (f32[16,64,128]{2,1,0:T(8,128)S(1)}, f32[16,64,128]{2,1,0:T(8,128)S(1)}, u32[]{:S(2)}, u32[]{:S(2)}) collective-permute-start(f32[16,64,128]{2,1,0:T(8,128)S(1)} %collective-permute-done.3.even), channel_id=1, source_target_pairs={{0,2},{4,6},{8,10},{12,14},{16,18},{20,22},{24,26},{28,30},{1,3},{... | collective-permute-start | bytes 1572872 | tf_op jit(solution)/shard_map/ppermute | solution.py:25
  23.2 23.8 %collective-permute-start.5 = (f32[16,64,128]{2,1,0:T(8,128)S(1)}, f32[16,64,128]{2,1,0:T(8,128)S(1)}, u32[]{:S(2)}, u32[]{:S(2)}) collective-permute-start(f32[16,64,128]{2,1,0:T(8,128)S(1)} %get-tuple-element.32.after.distant), channel_id=1, source_target_pairs={{2,0},{6,4},{10,8},{14,12},{18,16},{22,20},{26,24},{30,28},{3,1},{... | collective-permute-start | bytes 1572872 | tf_op jit(solution)/shard_map/ppermute | solution.py:25
  37.0 10.0 %collective-permute-start.6 = (f32[16,64,128]{2,1,0:T(8,128)S(1)}, f32[16,64,128]{2,1,0:T(8,128)S(1)}, u32[]{:S(2)}, u32[]{:S(2)}) collective-permute-start(f32[16,64,128]{2,1,0:T(8,128)S(1)} %shard_map.64.refs_0_.first), channel_id=1, source_target_pairs={{2,0},{6,4},{10,8},{14,12},{18,16},{22,20},{26,24},{30,28},{3,1},{... | collective-permute-start | bytes 1572872 | tf_op jit(solution)/shard_map/ppermute | solution.py:25
  38.4 13.3 %collective-permute-start.7 = (f32[16,64,128]{2,1,0:T(8,128)S(1)}, f32[16,64,128]{2,1,0:T(8,128)S(1)}, u32[]{:S(2)}, u32[]{:S(2)}) collective-permute-start(f32[16,64,128]{2,1,0:T(8,128)S(1)} %shard_map.64.refs_0_.first), channel_id=1, source_target_pairs={{2,30},{6,2},{10,6},{14,10},{18,14},{22,18},{26,22},{30,26},{3,31}... | collective-permute-start | bytes 1572872 | tf_op jit(solution)/shard_map/ppermute | solution.py:19
  45.7 6.1 %collective-permute-start.8 = (f32[2,64,128]{2,1,0:T(8,128)S(1)}, f32[2,64,128]{2,1,0:T(8,128)S(1)}, u32[]{:S(2)}, u32[]{:S(2)}) collective-permute-start(f32[2,64,128]{2,1,0:T(8,128)S(1)} %get-tuple-element.33.after.mine), channel_id=1, source_target_pairs={{0,1},{1,0},{2,3},{3,2},{4,5},{5,4},{6,7},{7,6},{8,9},{9,8},{10,11... | collective-permute-start | bytes 196616 | tf_op jit(solution)/shard_map/ppermute | solution.py:25
  52.0 11.2 %collective-permute-start.9 = (f32[16,64,128]{2,1,0:T(8,128)S(1)}, f32[16,64,128]{2,1,0:T(8,128)S(1)}, u32[]{:S(2)}, u32[]{:S(2)}) collective-permute-start(f32[16,64,128]{2,1,0:T(8,128)S(1)} %get-tuple-element.38.after.distant), channel_id=1, source_target_pairs={{2,0},{6,4},{10,8},{14,12},{18,16},{22,20},{26,24},{30,28},{3,1},{... | collective-permute-start | bytes 1572872 | tf_op jit(solution)/shard_map/ppermute | solution.py:25
  53.3 9.9 %collective-permute-start.10 = (f32[16,64,128]{2,1,0:T(8,128)S(1)}, f32[16,64,128]{2,1,0:T(8,128)S(1)}, u32[]{:S(2)}, u32[]{:S(2)}) collective-permute-start(f32[16,64,128]{2,1,0:T(8,128)S(1)} %shard_map.65.second.other), channel_id=1, source_target_pairs={{2,0},{6,4},{10,8},{14,12},{18,16},{22,20},{26,24},{30,28},{3,1},{... | collective-permute-start | bytes 1572872 | tf_op jit(solution)/shard_map/ppermute | solution.py:25
  54.6 12.6 %collective-permute-start.11 = (f32[16,64,128]{2,1,0:T(8,128)S(1)}, f32[16,64,128]{2,1,0:T(8,128)S(1)}, u32[]{:S(2)}, u32[]{:S(2)}) collective-permute-start(f32[16,64,128]{2,1,0:T(8,128)S(1)} %shard_map.65.second.other), channel_id=1, source_target_pairs={{2,30},{6,2},{10,6},{14,10},{18,14},{22,18},{26,22},{30,26},{3,31}... | collective-permute-start | bytes 1572872 | tf_op jit(solution)/shard_map/ppermute | solution.py:19
  61.1 13.5 %collective-permute-start.19 = (f32[16,64,128]{2,1,0:T(8,128)S(1)}, f32[16,64,128]{2,1,0:T(8,128)S(1)}, u32[]{:S(2)}, u32[]{:S(2)}) collective-permute-start(f32[16,64,128]{2,1,0:T(8,128)S(1)} %shard_map.73.after), channel_id=1, source_target_pairs={{0,4},{4,8},{8,12},{12,16},{16,20},{20,24},{24,28},{28,0},{1,5},{5... | collective-permute-start | bytes 1572872 | tf_op jit(solution)/shard_map/ppermute | solution.py:19
  61.8 7.0 %collective-permute-start.12 = (f32[2,64,128]{2,1,0:T(8,128)S(1)}, f32[2,64,128]{2,1,0:T(8,128)S(1)}, u32[]{:S(2)}, u32[]{:S(2)}) collective-permute-start(f32[2,64,128]{2,1,0:T(8,128)S(1)} %get-tuple-element.34.after.mine), channel_id=1, source_target_pairs={{0,1},{1,0},{2,3},{3,2},{4,5},{5,4},{6,7},{7,6},{8,9},{9,8},{10,11... | collective-permute-start | bytes 196616 | tf_op jit(solution)/shard_map/ppermute | solution.py:25
  67.3 5.1 %collective-permute-start.13 = (f32[2,64,128]{2,1,0:T(8,128)S(1)}, f32[2,64,128]{2,1,0:T(8,128)S(1)}, u32[]{:S(2)}, u32[]{:S(2)}) collective-permute-start(f32[2,64,128]{2,1,0:T(8,128)S(1)} %get-tuple-element.39.after.mine), channel_id=1, source_target_pairs={{0,1},{1,0},{2,3},{3,2},{4,5},{5,4},{6,7},{7,6},{8,9},{9,8},{10,11... | collective-permute-start | bytes 196616 | tf_op jit(solution)/shard_map/ppermute | solution.py:25
  68.6 4.7 %collective-permute-start.14 = (f32[2,64,128]{2,1,0:T(8,128)S(1)}, f32[2,64,128]{2,1,0:T(8,128)S(1)}, u32[]{:S(2)}, u32[]{:S(2)}) collective-permute-start(f32[2,64,128]{2,1,0:T(8,128)S(1)} %get-tuple-element.28.after.mine), channel_id=1, source_target_pairs={{0,1},{1,0},{2,3},{3,2},{4,5},{5,4},{6,7},{7,6},{8,9},{9,8},{10,11... | collective-permute-start | bytes 196616 | tf_op jit(solution)/shard_map/ppermute | solution.py:25
  69.0 9.6 %collective-permute-start.18 = (f32[16,64,128]{2,1,0:T(8,128)S(1)}, f32[16,64,128]{2,1,0:T(8,128)S(1)}, u32[]{:S(2)}, u32[]{:S(2)}) collective-permute-start(f32[16,64,128]{2,1,0:T(8,128)S(1)} %get-tuple-element.43.after), channel_id=1, source_target_pairs={{0,2},{4,6},{8,10},{12,14},{16,18},{20,22},{24,26},{28,30},{1,3},{... | collective-permute-start | bytes 1572872 | tf_op jit(solution)/shard_map/ppermute | solution.py:25
  70.3 16.9 %collective-permute-start.20 = (f32[16,64,128]{2,1,0:T(8,128)S(1)}, f32[16,64,128]{2,1,0:T(8,128)S(1)}, u32[]{:S(2)}, u32[]{:S(2)}) collective-permute-start(f32[16,64,128]{2,1,0:T(8,128)S(1)} %get-tuple-element.43.after), channel_id=1, source_target_pairs={{2,6},{6,10},{10,14},{14,18},{18,22},{22,26},{26,30},{30,2},{3,7},... | collective-permute-start | bytes 1572872 | tf_op jit(solution)/shard_map/ppermute | solution.py:19
  72.5 15.7 %collective-permute-start.16 = (f32[16,64,128]{2,1,0:T(8,128)S(1)}, f32[16,64,128]{2,1,0:T(8,128)S(1)}, u32[]{:S(2)}, u32[]{:S(2)}) collective-permute-start(f32[16,64,128]{2,1,0:T(8,128)S(1)} %shard_map.77.after), channel_id=1, source_target_pairs={{0,4},{4,8},{8,12},{12,16},{16,20},{20,24},{24,28},{28,0},{1,5},{5... | collective-permute-start | bytes 1572872 | tf_op jit(solution)/shard_map/ppermute | solution.py:19
  73.4 14.9 %collective-permute-start.15 = (f32[16,64,128]{2,1,0:T(8,128)S(1)}, f32[16,64,128]{2,1,0:T(8,128)S(1)}, u32[]{:S(2)}, u32[]{:S(2)}) collective-permute-start(f32[16,64,128]{2,1,0:T(8,128)S(1)} %get-tuple-element.47.after), channel_id=1, source_target_pairs={{0,2},{4,6},{8,10},{12,14},{16,18},{20,22},{24,26},{28,30},{1,3},{... | collective-permute-start | bytes 1572872 | tf_op jit(solution)/shard_map/ppermute | solution.py:25
  74.7 20.0 %collective-permute-start.17 = (f32[16,64,128]{2,1,0:T(8,128)S(1)}, f32[16,64,128]{2,1,0:T(8,128)S(1)}, u32[]{:S(2)}, u32[]{:S(2)}) collective-permute-start(f32[16,64,128]{2,1,0:T(8,128)S(1)} %get-tuple-element.47.after), channel_id=1, source_target_pairs={{2,6},{6,10},{10,14},{14,18},{18,22},{22,26},{26,30},{30,2},{3,7},... | collective-permute-start | bytes 1572872 | tf_op jit(solution)/shard_map/ppermute | solution.py:19

commit v7 on v5

--- a/solution.py
+++ b/solution.py
@@ -119,7 +119,7 @@
     flat = raw.reshape(groups * tiles * lines, width)
     lower = lax.broadcasted_iota(jnp.int32, (tiles, width), 1) < width // 2
     half = groups // 2
-    weight = flag[0].astype(jnp.float32)
+    weight = 1.0 - flag[0].astype(jnp.float32)
     copies = [
         pltpu.make_async_copy(raw.at[g], out.at[row, g], departures.at[g]) for g in range(groups)
     ]
@@ -138,18 +138,18 @@
         copy.wait()
 
 
-def pick_kernel(flag, after, far, own, out):
+def pick_kernel(flag, after, own, far, out):
     @pl.when(flag[0] == 0)
     def _():
-        out[...] = far[...]
+        out[...] = own[...]
 
     @pl.when(flag[0] == 1)
     def _():
-        out[...] = own[...]
+        out[...] = far[...]
 
 
 def join_kernel(flag, after, distant, handed, out):
-    weight = 1.0 - flag[0].astype(jnp.float32)
+    weight = flag[0].astype(jnp.float32)
     out[...] = distant[...] + weight * handed[...]
 
 
@@ -274,9 +274,19 @@
     live = jnp.arange(first.shape[0]) < pair_count[0]
     distance = (partner // owned - band_index) % band_count
     inside = (REACH * owned) * owned
-    place = ((partner % owned) * REACH + distance - 1) * owned + first
+    place = (first * REACH + distance - 1) * owned + partner % owned
     place = jnp.where(distance == 0, inside, place)
-    return jnp.sum(jnp.where(live, lax.shift_left(1, DIGIT * place), 0))
+    counts = jnp.sum(jnp.where(live, lax.shift_left(1, DIGIT * place), 0)).reshape(1)
+    digit = 2**DIGIT - 1
+    kept = digit << (DIGIT * inside)
+    total = counts & kept
+    for distance in range(1, REACH + 1):
+        kept = 0
+        for k in range(owned * owned):
+            spot = (k // owned * REACH + distance - 1) * owned + k % owned
+            kept |= digit << (DIGIT * spot)
+        total = total | (rotated(counts, "band", distance) & kept)
+    return total[0]
 
 
 def count_at(counts, place):
@@ -329,7 +339,7 @@
             ],
         )(source, *fields)
         fields.append(field)
-        far.append(rotated(field, "band", -2))
+        far.append(rotated(field, "band", 2))
     own = call(stack_kernel, both, [vmem, vmem])(*fields)
     flag = (band_index % 2).reshape(1)
     counts = pair_counts(pair_list, pair_count, owned, band_index, band_count)
@@ -364,7 +374,7 @@
 
     def brought(row, after):
         picked = call(pick_kernel, one, [smem, free, vmem, vmem])(
-            flag, after, far[row], fields[row]
+            flag, after, fields[row], far[row]
         )
         return picked, swapped(picked, "band")
 
@@ -386,7 +396,7 @@
             flag, distant, distant, handed_over
         )
         passed.append(handed_over)
-        arrived.append(rotated(joined, "band", 2))
+        arrived.append(rotated(joined, "band", -2))
         after = joined
         if row + 1 < owned:
             after, near = brought(row + 1, joined)

time: 82.1 us -> 78.2 us (0.952)
  starting transfers between devices: 21.3 us -> 15 us
  waiting for transfers between devices: 49.3 us -> 51 us
  between operations: 1.51 us -> 2.97 us
  local copies, waits for them, and re-layouts: 1.55 us -> 0.69 us
    ppermute x4 -> x6, starting transfers between devices: 13.4 us -> 6.99 us  [rotated(): return lax.ppermute(value, axis, pairs)]
    ppermute x4 -> x6, waiting for transfers between devices: 32.6 us -> 35.5 us  [rotated(): return lax.ppermute(value, axis, pairs)]
    ppermute x9, waiting for transfers between devices: 16.7 us -> 15.5 us  [swapped(): lax.ppermute(value, axis, [(source, source ^ 1) for source in range(count)])]
    unnamed x8, local copies, waits for them, and re-layouts: 1.55 us -> 0.69 us
  transfers between devices with their start and end apart: 13 -> 15, of which waited for: 11 -> 12; matrix products, arithmetic and copies ran while one was open for 1% -> 1% of each run, Pallas kernels for 6% -> 6%
where the time goes in v7:
time: 78.2 us; the launch traced here: 78 us
  waiting for transfers between devices  51 us (65%)
  starting transfers between devices  15 us (19%)
  Pallas kernels  7.56 us (10%)
  between operations  2.97 us (4%)
    ppermute x6, waiting for transfers between devices, rotated(): return lax.ppermute(value, axis, pairs)  35.5 us
    ppermute x9, waiting for transfers between devices, swapped(): lax.ppermute(value, axis, [(source, source ^ 1) for source in range(count)])  15.5 us
    ppermute x9, starting transfers between devices, swapped(): lax.ppermute(value, axis, [(source, source ^ 1) for source in range(count)])  8.02 us
    ppermute x6, starting transfers between devices, rotated(): return lax.ppermute(value, axis, pairs)  6.99 us
    pallas_call x2, Pallas kernels, on_device(): call(functools.partial(arrange_kernel, row), one, [hbm] + [free] * row, s...  2.56 us
    pallas_call x2, Pallas kernels, on_device(): call(functools.partial(restore_kernel, row), out, [smem] + [vmem] * 3 + [...  1.98 us
    pallas_call x5, Pallas kernels, backward(): call(functools.partial(backward_kernel, base, inside), both if inside els...  1.61 us
  transfers between devices with their start and end apart: 15, of which 12 were waited for; matrix products, arithmetic and copies ran while one was open for 1% of the time, Pallas kernels for 6%

profile of v7, /device:TPU:0, one launch (start us, length us, event | category | flops | bytes accessed | tf_op | source)
XLA Modules:
  0.0 78.0 jit_solution(13675537856464706122)
XLA Ops:
  0.0 1.3 %shard_map.64.refs_0_.first.own = f32[16,64,128]{2,1,0:T(8,128)S(1)} custom-call(f32[2,4,32,8,128]{4,3,2,1,0:T(8,128)} %bitcast.37), custom_call_target="tpu_custom_call" | custom-call | bytes 1048576 | tf_op jit(solution)/shard_map/pallas_call | solution.py:332
  1.3 3.0 %collective-permute-start.2 = (f32[16,64,128]{2,1,0:T(8,128)S(1)}, f32[16,64,128]{2,1,0:T(8,128)S(1)}, u32[]{:S(2)}, u32[]{:S(2)}) collective-permute-start(f32[16,64,128]{2,1,0:T(8,128)S(1)} %shard_map.64.refs_0_.first.own), channel_id=1, source_target_pairs={{0,4},{2,6},{4,8},{6,10},{8,12},{10,14},{12,16},{14,18},{16,20},{1... | collective-permute-start | bytes 1572872 | tf_op jit(solution)/shard_map/ppermute | solution.py:19
  5.0 0.0 copy-start.3
  5.0 0.7 copy-done.3
  5.7 0.7 fusion.1
  6.4 0.0 collective-permute-start
  6.4 1.5 %collective-permute-start.1 = (s32[1]{0:T(128)}, s32[1]{0:T(128)}, u32[]{:S(2)}, u32[]{:S(2)}) collective-permute-start(s32[1]{0:T(128)} %bitcast.4), channel_id=1, source_target_pairs={{0,4},{2,6},{4,8},{6,10},{8,12},{10,14},{12,16},{14,18},{16,20},{1... | collective-permute-start | bytes 20 | tf_op jit(solution)/shard_map/ppermute | solution.py:19
  7.9 1.3 %shard_map.65.second.other.own = f32[16,64,128]{2,1,0:T(8,128)S(1)} custom-call(f32[2,4,32,8,128]{4,3,2,1,0:T(8,128)} %bitcast.38, f32[16,64,128]{2,1,0:T(8,128)S(1)} %shard_map.64.refs_0_.first.own), custom_call_target="tpu_custom_call" | custom-call | bytes 1048576 | tf_op jit(solution)/shard_map/pallas_call | solution.py:332
  9.9 0.0 copy-start
  9.9 0.0 copy-start.1
  9.9 0.0 copy-start.2
  9.9 0.1 shard_map.66.after.own
  10.0 8.4 %collective-permute-done = s32[1]{0:T(128)} collective-permute-done((s32[1]{0:T(128)}, s32[1]{0:T(128)}, u32[]{:S(2)}, u32[]{:S(2)}) %collective-permute-start) | collective-permute-done | bytes 36 | tf_op jit(solution)/shard_map/ppermute | solution.py:19
  19.1 0.2 collective-permute-done.1
  20.0 0.0 copy-done
  20.0 0.0 copy-done.1
  20.1 0.0 copy-done.2
  20.1 0.1 shard_map.67
  20.1 0.0 collective-permute-done.2.far.other
  20.2 0.3 collective-permute-start.3
  20.5 1.0 %shard_map.69 = (f32[2,16,64,128]{3,2,1,0:T(8,128)S(1)}, f32[2,2,2,64,128]{4,3,2,1,0:T(8,128)S(1)}, f32[2,64,128]{2,1,0:T(8,128)S(1)}) custom-call(s32[1]{0:T(128)} %bitcast.6.counts, f32[16,64,128]{2,1,0:T(8,128)S(1)} %shard_map.68.after, f32[2,16,64,128]{3,2,1,0:T(8,128)S(1)} %shard_map.66.after.own, f32[16,64,128]{2,1,0:T(8,128)S(1)} %collective-permute-done.2.far.other, ...), custom_call_target="tpu_custom_call" | custom-call | bytes 1048576 | tf_op jit(solution)/shard_map/pallas_call | solution.py:349
  21.5 0.6 collective-permute-done.3.other
  22.2 1.5 %collective-permute-start.4 = (f32[2,64,128]{2,1,0:T(8,128)S(1)}, f32[2,64,128]{2,1,0:T(8,128)S(1)}, u32[]{:S(2)}, u32[]{:S(2)}) collective-permute-start(f32[2,64,128]{2,1,0:T(8,128)S(1)} %get-tuple-element.30.after.mine), channel_id=1, source_target_pairs={{0,1},{1,0},{2,3},{3,2},{4,5},{5,4},{6,7},{7,6},{8,9},{9,8},{10,11... | collective-permute-start | bytes 196616 | tf_op jit(solution)/shard_map/ppermute | solution.py:24
  23.7 2.8 %collective-permute-done.4.arrived = f32[2,64,128]{2,1,0:T(8,128)S(1)} collective-permute-done((f32[2,64,128]{2,1,0:T(8,128)S(1)}, f32[2,64,128]{2,1,0:T(8,128)S(1)}, u32[]{:S(2)}, u32[]{:S(2)}) %collective-permute-start.4) | collective-permute-done | bytes 65568 | tf_op jit(solution)/shard_map/ppermute | solution.py:24
  26.4 0.1 shard_map.71
  26.6 0.1 collective-permute-start.6
  26.7 0.2 collective-permute-start.7
  26.9 1.5 %collective-permute-start.5 = (f32[2,64,128]{2,1,0:T(8,128)S(1)}, f32[2,64,128]{2,1,0:T(8,128)S(1)}, u32[]{:S(2)}, u32[]{:S(2)}) collective-permute-start(f32[2,64,128]{2,1,0:T(8,128)S(1)} %get-tuple-element.29.after.mine), channel_id=1, source_target_pairs={{0,1},{1,0},{2,3},{3,2},{4,5},{5,4},{6,7},{7,6},{8,9},{9,8},{10,11... | collective-permute-start | bytes 196616 | tf_op jit(solution)/shard_map/ppermute | solution.py:24
  28.4 2.8 %collective-permute-done.5.arrived = f32[2,64,128]{2,1,0:T(8,128)S(1)} collective-permute-done((f32[2,64,128]{2,1,0:T(8,128)S(1)}, f32[2,64,128]{2,1,0:T(8,128)S(1)}, u32[]{:S(2)}, u32[]{:S(2)}) %collective-permute-start.5) | collective-permute-done | bytes 65568 | tf_op jit(solution)/shard_map/ppermute | solution.py:24
  31.2 1.1 %shard_map.72 = (f32[2,16,64,128]{3,2,1,0:T(8,128)S(1)}, f32[16,64,128]{2,1,0:T(8,128)S(1)}) custom-call(s32[1]{0:T(128)} %bitcast.6.counts, f32[16,64,128]{2,1,0:T(8,128)S(1)} %get-tuple-element.33.after, f32[2,16,64,128]{3,2,1,0:T(8,128)S(1)} %shard_map.66.after.own, f32[16,64,128]{2,1,0:T(8,128)S(1)} %collective-permute-done.2.far.other, ...), custom_call_target="tpu_custom_call" | custom-call | bytes 1048576 | tf_op jit(solution)/shard_map/pallas_call | solution.py:363
  32.3 0.0 collective-permute-done.6.handed.passed
  32.3 0.1 shard_map.73.after
  32.3 11.4 %collective-permute-done.7.far.other = f32[16,64,128]{2,1,0:T(8,128)S(1)} collective-permute-done((f32[16,64,128]{2,1,0:T(8,128)S(1)}, f32[16,64,128]{2,1,0:T(8,128)S(1)}, u32[]{:S(2)}, u32[]{:S(2)}) %collective-permute-start.7) | collective-permute-done | bytes 524320 | tf_op jit(solution)/shard_map/ppermute | solution.py:19
  43.7 0.1 collective-permute-start.8
  43.8 0.1 shard_map.75
  43.9 1.8 %collective-permute-done.8.other = f32[16,64,128]{2,1,0:T(8,128)S(1)} collective-permute-done((f32[16,64,128]{2,1,0:T(8,128)S(1)}, f32[16,64,128]{2,1,0:T(8,128)S(1)}, u32[]{:S(2)}, u32[]{:S(2)}) %collective-permute-start.8) | collective-permute-done | bytes 524320 | tf_op jit(solution)/shard_map/ppermute | solution.py:24
  45.7 1.5 %collective-permute-start.9 = (f32[2,64,128]{2,1,0:T(8,128)S(1)}, f32[2,64,128]{2,1,0:T(8,128)S(1)}, u32[]{:S(2)}, u32[]{:S(2)}) collective-permute-start(f32[2,64,128]{2,1,0:T(8,128)S(1)} %get-tuple-element.39.after.mine), channel_id=1, source_target_pairs={{0,1},{1,0},{2,3},{3,2},{4,5},{5,4},{6,7},{7,6},{8,9},{9,8},{10,11... | collective-permute-start | bytes 196616 | tf_op jit(solution)/shard_map/ppermute | solution.py:24
  47.2 2.8 %collective-permute-done.9.arrived = f32[2,64,128]{2,1,0:T(8,128)S(1)} collective-permute-done((f32[2,64,128]{2,1,0:T(8,128)S(1)}, f32[2,64,128]{2,1,0:T(8,128)S(1)}, u32[]{:S(2)}, u32[]{:S(2)}) %collective-permute-start.9) | collective-permute-done | bytes 65568 | tf_op jit(solution)/shard_map/ppermute | solution.py:24
  50.0 0.1 shard_map.77
  50.1 0.1 collective-permute-start.11
  50.2 1.6 %collective-permute-start.10 = (f32[2,64,128]{2,1,0:T(8,128)S(1)}, f32[2,64,128]{2,1,0:T(8,128)S(1)}, u32[]{:S(2)}, u32[]{:S(2)}) collective-permute-start(f32[2,64,128]{2,1,0:T(8,128)S(1)} %get-tuple-element.38.after.mine), channel_id=1, source_target_pairs={{0,1},{1,0},{2,3},{3,2},{4,5},{5,4},{6,7},{7,6},{8,9},{9,8},{10,11... | collective-permute-start | bytes 196616 | tf_op jit(solution)/shard_map/ppermute | solution.py:24
  51.8 1.1 %collective-permute-start.14 = (f32[16,64,128]{2,1,0:T(8,128)S(1)}, f32[16,64,128]{2,1,0:T(8,128)S(1)}, u32[]{:S(2)}, u32[]{:S(2)}) collective-permute-start(f32[16,64,128]{2,1,0:T(8,128)S(1)} %shard_map.73.after), channel_id=1, source_target_pairs={{0,28},{2,30},{4,0},{6,2},{8,4},{10,6},{12,8},{14,10},{16,12},{18,... | collective-permute-start | bytes 1572872 | tf_op jit(solution)/shard_map/ppermute | solution.py:19
  52.8 1.9 %collective-permute-done.10.arrived = f32[2,64,128]{2,1,0:T(8,128)S(1)} collective-permute-done((f32[2,64,128]{2,1,0:T(8,128)S(1)}, f32[2,64,128]{2,1,0:T(8,128)S(1)}, u32[]{:S(2)}, u32[]{:S(2)}) %collective-permute-start.10) | collective-permute-done | bytes 65568 | tf_op jit(solution)/shard_map/ppermute | solution.py:24
  54.7 0.1 shard_map.78
  54.8 0.0 collective-permute-done.11.handed.passed
  54.9 0.1 shard_map.79.after
  54.9 1.1 %collective-permute-start.13 = (f32[16,64,128]{2,1,0:T(8,128)S(1)}, f32[16,64,128]{2,1,0:T(8,128)S(1)}, u32[]{:S(2)}, u32[]{:S(2)}) collective-permute-start(f32[16,64,128]{2,1,0:T(8,128)S(1)} %shard_map.79.after), channel_id=1, source_target_pairs={{0,28},{2,30},{4,0},{6,2},{8,4},{10,6},{12,8},{14,10},{16,12},{18,... | collective-permute-start | bytes 1572872 | tf_op jit(solution)/shard_map/ppermute | solution.py:19
  56.1 1.5 %collective-permute-start.12 = (f32[2,64,128]{2,1,0:T(8,128)S(1)}, f32[2,64,128]{2,1,0:T(8,128)S(1)}, u32[]{:S(2)}, u32[]{:S(2)}) collective-permute-start(f32[2,64,128]{2,1,0:T(8,128)S(1)} %get-tuple-element.28.after.mine), channel_id=1, source_target_pairs={{0,1},{1,0},{2,3},{3,2},{4,5},{5,4},{6,7},{7,6},{8,9},{9,8},{10,11... | collective-permute-start | bytes 196616 | tf_op jit(solution)/shard_map/ppermute | solution.py:24
  57.5 2.8 %collective-permute-done.12.arrived = f32[2,64,128]{2,1,0:T(8,128)S(1)} collective-permute-done((f32[2,64,128]{2,1,0:T(8,128)S(1)}, f32[2,64,128]{2,1,0:T(8,128)S(1)}, u32[]{:S(2)}, u32[]{:S(2)}) %collective-permute-start.12) | collective-permute-done | bytes 65568 | tf_op jit(solution)/shard_map/ppermute | solution.py:24
  60.3 0.1 shard_map.80.own
  60.4 6.1 %collective-permute-done.14.arrived = f32[16,64,128]{2,1,0:T(8,128)S(1)} collective-permute-done((f32[16,64,128]{2,1,0:T(8,128)S(1)}, f32[16,64,128]{2,1,0:T(8,128)S(1)}, u32[]{:S(2)}, u32[]{:S(2)}) %collective-permute-start.14) | collective-permute-done | bytes 524320 | tf_op jit(solution)/shard_map/ppermute | solution.py:19
  66.6 1.0 %shard_map.81.refs_0_ = f32[2,4,32,8,128]{4,3,2,1,0:T(8,128)} custom-call(s32[1]{0:T(128)} %bitcast.flag, f32[2,16,64,128]{3,2,1,0:T(8,128)S(1)} %shard_map.80.own, f32[16,64,128]{2,1,0:T(8,128)S(1)} %collective-permute-done.6.handed.passed, f32[16,64,128]{2,1,0:T(8,128)S(1)} %collective-permute-done.14.arrived), custom_call_target="tpu_custom_call" | custom-call | bytes 1048576 | tf_op jit(solution)/shard_map/pallas_call | solution.py:408
  67.5 9.4 %collective-permute-done.13.arrived = f32[16,64,128]{2,1,0:T(8,128)S(1)} collective-permute-done((f32[16,64,128]{2,1,0:T(8,128)S(1)}, f32[16,64,128]{2,1,0:T(8,128)S(1)}, u32[]{:S(2)}, u32[]{:S(2)}) %collective-permute-start.13) | collective-permute-done | bytes 524320 | tf_op jit(solution)/shard_map/ppermute | solution.py:19
  77.0 1.0 %shard_map.82 = f32[2,4,32,8,128]{4,3,2,1,0:T(8,128)} custom-call(s32[1]{0:T(128)} %bitcast.flag, f32[2,16,64,128]{3,2,1,0:T(8,128)S(1)} %shard_map.80.own, f32[16,64,128]{2,1,0:T(8,128)S(1)} %collective-permute-done.11.handed.passed, f32[16,64,128]{2,1,0:T(8,128)S(1)} %collective-permute-done.13.arrived, ...), custom_call_target="tpu_custom_call", output_to_operand_aliasing={{}: (4, {})} | custom-call | bytes 1048576 | tf_op jit(solution)/shard_map/pallas_call | solution.py:408
  (4 shorter events, 0.1 us)
Async XLA Ops:
  1.3 18.8 %collective-permute-start.2 = (f32[16,64,128]{2,1,0:T(8,128)S(1)}, f32[16,64,128]{2,1,0:T(8,128)S(1)}, u32[]{:S(2)}, u32[]{:S(2)}) collective-permute-start(f32[16,64,128]{2,1,0:T(8,128)S(1)} %shard_map.64.refs_0_.first.own), channel_id=1, source_target_pairs={{0,4},{2,6},{4,8},{6,10},{8,12},{10,14},{12,16},{14,18},{16,20},{1... | collective-permute-start | bytes 1572872 | tf_op jit(solution)/shard_map/ppermute | solution.py:19
  5.0 0.7 copy-start.3
  6.4 12.0 %collective-permute-start = (s32[1]{0:T(128)}, s32[1]{0:T(128)}, u32[]{:S(2)}, u32[]{:S(2)}) collective-permute-start(s32[1]{0:T(128)} %bitcast.4), channel_id=1, source_target_pairs={{0,2},{2,4},{4,6},{6,8},{8,10},{10,12},{12,14},{14,16},{16,18},{18... | collective-permute-start | bytes 20 | tf_op jit(solution)/shard_map/ppermute | solution.py:19
  6.4 12.9 %collective-permute-start.1 = (s32[1]{0:T(128)}, s32[1]{0:T(128)}, u32[]{:S(2)}, u32[]{:S(2)}) collective-permute-start(s32[1]{0:T(128)} %bitcast.4), channel_id=1, source_target_pairs={{0,4},{2,6},{4,8},{6,10},{8,12},{10,14},{12,16},{14,18},{16,20},{1... | collective-permute-start | bytes 20 | tf_op jit(solution)/shard_map/ppermute | solution.py:19
  9.9 10.1 %copy-start = (f32[5,64,128]{2,1,0:T(8,128)S(1)}, f32[5,64,128]{2,1,0:T(8,128)}, u32[]{:S(2)}) copy-start(f32[5,64,128]{2,1,0:T(8,128)} %constant.74.clone.decay) | copy-start | bytes 491524
  9.9 10.1 %copy-start.1 = (bf16[256,256]{1,0:T(8,128)(2,1)S(1)}, bf16[256,256]{1,0:T(8,128)(2,1)}, u32[]{:S(2)}) copy-start(bf16[256,256]{1,0:T(8,128)(2,1)} %constant.72.clone.right_ref) | copy-start | bytes 393220
  9.9 10.1 %copy-start.2 = (bf16[64,192]{1,0:T(8,128)(2,1)S(1)}, bf16[64,192]{1,0:T(8,128)(2,1)}, u32[]{:S(2)}) copy-start(bf16[64,192]{1,0:T(8,128)(2,1)} %constant.73.clone.left_ref) | copy-start | bytes 73732
  20.2 2.0 %collective-permute-start.3 = (f32[16,64,128]{2,1,0:T(8,128)S(1)}, f32[16,64,128]{2,1,0:T(8,128)S(1)}, u32[]{:S(2)}, u32[]{:S(2)}) collective-permute-start(f32[16,64,128]{2,1,0:T(8,128)S(1)} %shard_map.68.after), channel_id=1, source_target_pairs={{0,2},{2,0},{4,6},{6,4},{8,10},{10,8},{12,14},{14,12},{16,18},{18,... | collective-permute-start | bytes 1572872 | tf_op jit(solution)/shard_map/ppermute | solution.py:24
  22.2 4.3 %collective-permute-start.4 = (f32[2,64,128]{2,1,0:T(8,128)S(1)}, f32[2,64,128]{2,1,0:T(8,128)S(1)}, u32[]{:S(2)}, u32[]{:S(2)}) collective-permute-start(f32[2,64,128]{2,1,0:T(8,128)S(1)} %get-tuple-element.30.after.mine), channel_id=1, source_target_pairs={{0,1},{1,0},{2,3},{3,2},{4,5},{5,4},{6,7},{7,6},{8,9},{9,8},{10,11... | collective-permute-start | bytes 196616 | tf_op jit(solution)/shard_map/ppermute | solution.py:24
  26.6 5.7 %collective-permute-start.6 = (f32[16,64,128]{2,1,0:T(8,128)S(1)}, f32[16,64,128]{2,1,0:T(8,128)S(1)}, u32[]{:S(2)}, u32[]{:S(2)}) collective-permute-start(f32[16,64,128]{2,1,0:T(8,128)S(1)} %get-tuple-element.33.after), channel_id=1, source_target_pairs={{0,2},{2,0},{4,6},{6,4},{8,10},{10,8},{12,14},{14,12},{16,18},{18,... | collective-permute-start | bytes 1572872 | tf_op jit(solution)/shard_map/ppermute | solution.py:24
  26.7 17.0 %collective-permute-start.7 = (f32[16,64,128]{2,1,0:T(8,128)S(1)}, f32[16,64,128]{2,1,0:T(8,128)S(1)}, u32[]{:S(2)}, u32[]{:S(2)}) collective-permute-start(f32[16,64,128]{2,1,0:T(8,128)S(1)} %shard_map.65.second.other.own), channel_id=1, source_target_pairs={{0,4},{2,6},{4,8},{6,10},{8,12},{10,14},{12,16},{14,18},{16,20},{1... | collective-permute-start | bytes 1572872 | tf_op jit(solution)/shard_map/ppermute | solution.py:19
  26.9 4.3 %collective-permute-start.5 = (f32[2,64,128]{2,1,0:T(8,128)S(1)}, f32[2,64,128]{2,1,0:T(8,128)S(1)}, u32[]{:S(2)}, u32[]{:S(2)}) collective-permute-start(f32[2,64,128]{2,1,0:T(8,128)S(1)} %get-tuple-element.29.after.mine), channel_id=1, source_target_pairs={{0,1},{1,0},{2,3},{3,2},{4,5},{5,4},{6,7},{7,6},{8,9},{9,8},{10,11... | collective-permute-start | bytes 196616 | tf_op jit(solution)/shard_map/ppermute | solution.py:24
  43.7 2.0 %collective-permute-start.8 = (f32[16,64,128]{2,1,0:T(8,128)S(1)}, f32[16,64,128]{2,1,0:T(8,128)S(1)}, u32[]{:S(2)}, u32[]{:S(2)}) collective-permute-start(f32[16,64,128]{2,1,0:T(8,128)S(1)} %shard_map.74.after), channel_id=1, source_target_pairs={{0,2},{2,0},{4,6},{6,4},{8,10},{10,8},{12,14},{14,12},{16,18},{18,... | collective-permute-start | bytes 1572872 | tf_op jit(solution)/shard_map/ppermute | solution.py:24
  45.7 4.3 %collective-permute-start.9 = (f32[2,64,128]{2,1,0:T(8,128)S(1)}, f32[2,64,128]{2,1,0:T(8,128)S(1)}, u32[]{:S(2)}, u32[]{:S(2)}) collective-permute-start(f32[2,64,128]{2,1,0:T(8,128)S(1)} %get-tuple-element.39.after.mine), channel_id=1, source_target_pairs={{0,1},{1,0},{2,3},{3,2},{4,5},{5,4},{6,7},{7,6},{8,9},{9,8},{10,11... | collective-permute-start | bytes 196616 | tf_op jit(solution)/shard_map/ppermute | solution.py:24
  50.1 4.7 %collective-permute-start.11 = (f32[16,64,128]{2,1,0:T(8,128)S(1)}, f32[16,64,128]{2,1,0:T(8,128)S(1)}, u32[]{:S(2)}, u32[]{:S(2)}) collective-permute-start(f32[16,64,128]{2,1,0:T(8,128)S(1)} %get-tuple-element.43.after), channel_id=1, source_target_pairs={{0,2},{2,0},{4,6},{6,4},{8,10},{10,8},{12,14},{14,12},{16,18},{18,... | collective-permute-start | bytes 1572872 | tf_op jit(solution)/shard_map/ppermute | solution.py:24
  50.2 4.5 %collective-permute-start.10 = (f32[2,64,128]{2,1,0:T(8,128)S(1)}, f32[2,64,128]{2,1,0:T(8,128)S(1)}, u32[]{:S(2)}, u32[]{:S(2)}) collective-permute-start(f32[2,64,128]{2,1,0:T(8,128)S(1)} %get-tuple-element.38.after.mine), channel_id=1, source_target_pairs={{0,1},{1,0},{2,3},{3,2},{4,5},{5,4},{6,7},{7,6},{8,9},{9,8},{10,11... | collective-permute-start | bytes 196616 | tf_op jit(solution)/shard_map/ppermute | solution.py:24
  51.8 14.8 %collective-permute-start.14 = (f32[16,64,128]{2,1,0:T(8,128)S(1)}, f32[16,64,128]{2,1,0:T(8,128)S(1)}, u32[]{:S(2)}, u32[]{:S(2)}) collective-permute-start(f32[16,64,128]{2,1,0:T(8,128)S(1)} %shard_map.73.after), channel_id=1, source_target_pairs={{0,28},{2,30},{4,0},{6,2},{8,4},{10,6},{12,8},{14,10},{16,12},{18,... | collective-permute-start | bytes 1572872 | tf_op jit(solution)/shard_map/ppermute | solution.py:19
  54.9 22.1 %collective-permute-start.13 = (f32[16,64,128]{2,1,0:T(8,128)S(1)}, f32[16,64,128]{2,1,0:T(8,128)S(1)}, u32[]{:S(2)}, u32[]{:S(2)}) collective-permute-start(f32[16,64,128]{2,1,0:T(8,128)S(1)} %shard_map.79.after), channel_id=1, source_target_pairs={{0,28},{2,30},{4,0},{6,2},{8,4},{10,6},{12,8},{14,10},{16,12},{18,... | collective-permute-start | bytes 1572872 | tf_op jit(solution)/shard_map/ppermute | solution.py:19
  56.1 4.3 %collective-permute-start.12 = (f32[2,64,128]{2,1,0:T(8,128)S(1)}, f32[2,64,128]{2,1,0:T(8,128)S(1)}, u32[]{:S(2)}, u32[]{:S(2)}) collective-permute-start(f32[2,64,128]{2,1,0:T(8,128)S(1)} %get-tuple-element.28.after.mine), channel_id=1, source_target_pairs={{0,1},{1,0},{2,3},{3,2},{4,5},{5,4},{6,7},{7,6},{8,9},{9,8},{10,11... | collective-permute-start | bytes 196616 | tf_op jit(solution)/shard_map/ppermute | solution.py:24

commit v8 on v7

--- a/solution.py
+++ b/solution.py
@@ -278,15 +278,14 @@
     place = jnp.where(distance == 0, inside, place)
     counts = jnp.sum(jnp.where(live, lax.shift_left(1, DIGIT * place), 0)).reshape(1)
     digit = 2**DIGIT - 1
-    kept = digit << (DIGIT * inside)
-    total = counts & kept
+    total = jnp.int32(0)
     for distance in range(1, REACH + 1):
         kept = 0
         for k in range(owned * owned):
             spot = (k // owned * REACH + distance - 1) * owned + k % owned
             kept |= digit << (DIGIT * spot)
-        total = total | (rotated(counts, "band", distance) & kept)
-    return total[0]
+        total = total | (lax.optimization_barrier(rotated(counts, "band", distance)[0]) & kept)
+    return counts[0], total
 
 
 def count_at(counts, place):
@@ -342,10 +341,11 @@
         far.append(rotated(field, "band", 2))
     own = call(stack_kernel, both, [vmem, vmem])(*fields)
     flag = (band_index % 2).reshape(1)
-    counts = pair_counts(pair_list, pair_count, owned, band_index, band_count)
-    counts = (lax.optimization_barrier(counts) * 2 + band_index % 2).reshape(1)
-
-    def forward(base, after, other):
+    listed, counts = pair_counts(pair_list, pair_count, owned, band_index, band_count)
+    listed = (lax.optimization_barrier(listed) * 2 + band_index % 2).reshape(1)
+    counts = (counts * 2 + band_index % 2).reshape(1)
+
+    def forward(base, after, other, counts=counts):
         return call(
             functools.partial(forward_kernel, base),
             (
@@ -360,15 +360,16 @@
         return swapped(mine, "grid")
 
     def backward(base, after, state, total, inside=False):
+        numbers = listed if inside else counts
         return call(
             functools.partial(backward_kernel, base, inside),
             both if inside else (both, one),
             [smem, free] + [vmem] * (9 + len(total)),
             scratch=[pltpu.VMEM((chunks, 2) + shape[1:], jnp.float32)],
-        )(counts, after, own, *state, right, left, decay, *total)
+        )(numbers, after, own, *state, right, left, decay, *total)
 
     inner_base = REACH * owned * owned
-    spectrum, moments, mine = forward(inner_base, own, fields[1])
+    spectrum, moments, mine = forward(inner_base, own, fields[1], listed)
     inner = (fields[1], spectrum, moments, mine, exchanged(mine))
     after = mine
 

time: 78.2 us -> 84.8 us (1.084)
  waiting for transfers between devices: 51 us -> 59.6 us
  starting transfers between devices: 15 us -> 11.7 us
  local copies, waits for them, and re-layouts: 0.69 us -> 2.27 us
    ppermute x6, waiting for transfers between devices: 35.5 us -> 43.6 us  [rotated(): return lax.ppermute(value, axis, pairs)]
    ppermute x6, starting transfers between devices: 6.99 us -> 3.67 us  [rotated(): return lax.ppermute(value, axis, pairs)]
    unnamed x8 -> x16, local copies, waits for them, and re-layouts: 0.69 us -> 2.27 us
where the time goes in v8:
time: 84.8 us; the launch traced here: 84.6 us
  waiting for transfers between devices  59.6 us (70%)
  starting transfers between devices  11.7 us (14%)
  Pallas kernels  7.56 us (9%)
  between operations  2.76 us (3%)
  local copies, waits for them, and re-layouts  2.27 us (3%)
    ppermute x6, waiting for transfers between devices, rotated(): return lax.ppermute(value, axis, pairs)  43.6 us
    ppermute x9, waiting for transfers between devices, swapped(): lax.ppermute(value, axis, [(source, source ^ 1) for source in range(count)])  16 us
    ppermute x9, starting transfers between devices, swapped(): lax.ppermute(value, axis, [(source, source ^ 1) for source in range(count)])  8.01 us
    ppermute x6, starting transfers between devices, rotated(): return lax.ppermute(value, axis, pairs)  3.67 us
    pallas_call x2, Pallas kernels, on_device(): call(functools.partial(arrange_kernel, row), one, [hbm] + [free] * row, s...  2.56 us
    unnamed x16, local copies, waits for them, and re-layouts  2.27 us
    pallas_call x2, Pallas kernels, on_device(): call(functools.partial(restore_kernel, row), out, [smem] + [vmem] * 3 + [...  1.98 us
  transfers between devices with their start and end apart: 15, of which 12 were waited for; matrix products, arithmetic and copies ran while one was open for 1% of the time, Pallas kernels for 6%

profile of v8, /device:TPU:0, one launch (start us, length us, event | category | flops | bytes accessed | tf_op | source)
XLA Modules:
  0.0 84.6 jit_solution(18185879760091122965)
XLA Ops:
  0.0 1.3 %shard_map.64.refs_0_.first.own = f32[16,64,128]{2,1,0:T(8,128)S(1)} custom-call(f32[2,4,32,8,128]{4,3,2,1,0:T(8,128)} %bitcast.39), custom_call_target="tpu_custom_call" | custom-call | bytes 1048576 | tf_op jit(solution)/shard_map/pallas_call | solution.py:331
  1.3 3.0 %collective-permute-start.2 = (f32[16,64,128]{2,1,0:T(8,128)S(1)}, f32[16,64,128]{2,1,0:T(8,128)S(1)}, u32[]{:S(2)}, u32[]{:S(2)}) collective-permute-start(f32[16,64,128]{2,1,0:T(8,128)S(1)} %shard_map.64.refs_0_.first.own), channel_id=1, source_target_pairs={{0,4},{2,6},{4,8},{6,10},{8,12},{10,14},{12,16},{14,18},{16,20},{1... | collective-permute-start | bytes 1572872 | tf_op jit(solution)/shard_map/ppermute | solution.py:19
  4.3 1.3 %shard_map.65.second.other.own = f32[16,64,128]{2,1,0:T(8,128)S(1)} custom-call(f32[2,4,32,8,128]{4,3,2,1,0:T(8,128)} %bitcast.40, f32[16,64,128]{2,1,0:T(8,128)S(1)} %shard_map.64.refs_0_.first.own), custom_call_target="tpu_custom_call" | custom-call | bytes 1048576 | tf_op jit(solution)/shard_map/pallas_call | solution.py:331
  6.3 0.0 copy-start.7
  6.3 0.7 copy-done.7
  7.0 0.7 fusion.1
  8.3 0.0 copy-start
  8.3 0.0 copy-start.1
  8.3 0.0 copy-start.2
  8.3 0.1 shard_map.66.after.own
  8.4 0.8 copy-done
  9.2 0.1 copy-done.1
  9.3 0.0 copy-done.2
  9.3 0.0 copy-start.5
  9.3 0.7 copy-done.5
  10.0 0.0 copy-start.3
  10.0 9.3 %collective-permute-done.2.far.other = f32[16,64,128]{2,1,0:T(8,128)S(1)} collective-permute-done((f32[16,64,128]{2,1,0:T(8,128)S(1)}, f32[16,64,128]{2,1,0:T(8,128)S(1)}, u32[]{:S(2)}, u32[]{:S(2)}) %collective-permute-start.2) | collective-permute-done | bytes 524320 | tf_op jit(solution)/shard_map/ppermute | solution.py:19
  19.3 0.0 copy-done.3
  19.4 0.1 collective-permute-start.3
  19.4 0.5 collective-permute-start
  19.9 0.0 collective-permute-start.1
  19.9 5.6 %collective-permute-done = s32[1]{0:T(128)} collective-permute-done((s32[1]{0:T(128)}, s32[1]{0:T(128)}, u32[]{:S(2)}, u32[]{:S(2)}) %collective-permute-start) | collective-permute-done | bytes 36 | tf_op jit(solution)/shard_map/ppermute | solution.py:19
  25.5 0.9 %collective-permute-done.1 = s32[1]{0:T(128)} collective-permute-done((s32[1]{0:T(128)}, s32[1]{0:T(128)}, u32[]{:S(2)}, u32[]{:S(2)}) %collective-permute-start.1) | collective-permute-done | bytes 36 | tf_op jit(solution)/shard_map/ppermute | solution.py:19
  27.6 1.0 %shard_map.69 = (f32[2,16,64,128]{3,2,1,0:T(8,128)S(1)}, f32[2,2,2,64,128]{4,3,2,1,0:T(8,128)S(1)}, f32[2,64,128]{2,1,0:T(8,128)S(1)}) custom-call(s32[1]{0:T(128)} %bitcast.8.counts, f32[16,64,128]{2,1,0:T(8,128)S(1)} %shard_map.68.after, f32[2,16,64,128]{3,2,1,0:T(8,128)S(1)} %shard_map.66.after.own, f32[16,64,128]{2,1,0:T(8,128)S(1)} %collective-permute-done.2.far.other, ...), custom_call_target="tpu_custom_call" | custom-call | bytes 1048576 | tf_op jit(solution)/shard_map/pallas_call | solution.py:349
  28.6 0.0 collective-permute-done.3.other
  28.6 0.1 shard_map.70
  28.7 1.6 %collective-permute-start.4 = (f32[2,64,128]{2,1,0:T(8,128)S(1)}, f32[2,64,128]{2,1,0:T(8,128)S(1)}, u32[]{:S(2)}, u32[]{:S(2)}) collective-permute-start(f32[2,64,128]{2,1,0:T(8,128)S(1)} %get-tuple-element.30.after.mine), channel_id=1, source_target_pairs={{0,1},{1,0},{2,3},{3,2},{4,5},{5,4},{6,7},{7,6},{8,9},{9,8},{10,11... | collective-permute-start | bytes 196616 | tf_op jit(solution)/shard_map/ppermute | solution.py:24
  30.2 2.8 %collective-permute-done.4.arrived = f32[2,64,128]{2,1,0:T(8,128)S(1)} collective-permute-done((f32[2,64,128]{2,1,0:T(8,128)S(1)}, f32[2,64,128]{2,1,0:T(8,128)S(1)}, u32[]{:S(2)}, u32[]{:S(2)}) %collective-permute-start.4) | collective-permute-done | bytes 65568 | tf_op jit(solution)/shard_map/ppermute | solution.py:24
  33.0 0.1 shard_map.71
  33.2 0.1 collective-permute-start.6
  33.2 0.1 collective-permute-start.7
  33.3 1.6 %collective-permute-start.5 = (f32[2,64,128]{2,1,0:T(8,128)S(1)}, f32[2,64,128]{2,1,0:T(8,128)S(1)}, u32[]{:S(2)}, u32[]{:S(2)}) collective-permute-start(f32[2,64,128]{2,1,0:T(8,128)S(1)} %get-tuple-element.29.after.mine), channel_id=1, source_target_pairs={{0,1},{1,0},{2,3},{3,2},{4,5},{5,4},{6,7},{7,6},{8,9},{9,8},{10,11... | collective-permute-start | bytes 196616 | tf_op jit(solution)/shard_map/ppermute | solution.py:24
  34.9 2.9 %collective-permute-done.5.arrived = f32[2,64,128]{2,1,0:T(8,128)S(1)} collective-permute-done((f32[2,64,128]{2,1,0:T(8,128)S(1)}, f32[2,64,128]{2,1,0:T(8,128)S(1)}, u32[]{:S(2)}, u32[]{:S(2)}) %collective-permute-start.5) | collective-permute-done | bytes 65568 | tf_op jit(solution)/shard_map/ppermute | solution.py:24
  37.7 1.1 %shard_map.72 = (f32[2,16,64,128]{3,2,1,0:T(8,128)S(1)}, f32[16,64,128]{2,1,0:T(8,128)S(1)}) custom-call(s32[1]{0:T(128)} %bitcast.8.counts, f32[16,64,128]{2,1,0:T(8,128)S(1)} %get-tuple-element.33.after, f32[2,16,64,128]{3,2,1,0:T(8,128)S(1)} %shard_map.66.after.own, f32[16,64,128]{2,1,0:T(8,128)S(1)} %collective-permute-done.2.far.other, ...), custom_call_target="tpu_custom_call" | custom-call | bytes 1048576 | tf_op jit(solution)/shard_map/pallas_call | solution.py:364
  38.8 0.0 collective-permute-done.6.handed.passed
  38.8 0.1 shard_map.73.after
  38.9 11.4 %collective-permute-done.7.far.other = f32[16,64,128]{2,1,0:T(8,128)S(1)} collective-permute-done((f32[16,64,128]{2,1,0:T(8,128)S(1)}, f32[16,64,128]{2,1,0:T(8,128)S(1)}, u32[]{:S(2)}, u32[]{:S(2)}) %collective-permute-start.7) | collective-permute-done | bytes 524320 | tf_op jit(solution)/shard_map/ppermute | solution.py:19
  50.3 0.1 collective-permute-start.8
  50.4 0.1 shard_map.75
  50.4 1.8 %collective-permute-done.8.other = f32[16,64,128]{2,1,0:T(8,128)S(1)} collective-permute-done((f32[16,64,128]{2,1,0:T(8,128)S(1)}, f32[16,64,128]{2,1,0:T(8,128)S(1)}, u32[]{:S(2)}, u32[]{:S(2)}) %collective-permute-start.8) | collective-permute-done | bytes 524320 | tf_op jit(solution)/shard_map/ppermute | solution.py:24
  52.3 1.5 %collective-permute-start.9 = (f32[2,64,128]{2,1,0:T(8,128)S(1)}, f32[2,64,128]{2,1,0:T(8,128)S(1)}, u32[]{:S(2)}, u32[]{:S(2)}) collective-permute-start(f32[2,64,128]{2,1,0:T(8,128)S(1)} %get-tuple-element.39.after.mine), channel_id=1, source_target_pairs={{0,1},{1,0},{2,3},{3,2},{4,5},{5,4},{6,7},{7,6},{8,9},{9,8},{10,11... | collective-permute-start | bytes 196616 | tf_op jit(solution)/shard_map/ppermute | solution.py:24
  53.8 2.8 %collective-permute-done.9.arrived = f32[2,64,128]{2,1,0:T(8,128)S(1)} collective-permute-done((f32[2,64,128]{2,1,0:T(8,128)S(1)}, f32[2,64,128]{2,1,0:T(8,128)S(1)}, u32[]{:S(2)}, u32[]{:S(2)}) %collective-permute-start.9) | collective-permute-done | bytes 65568 | tf_op jit(solution)/shard_map/ppermute | solution.py:24
  56.6 0.1 shard_map.77
  56.7 0.1 collective-permute-start.11
  56.8 1.6 %collective-permute-start.10 = (f32[2,64,128]{2,1,0:T(8,128)S(1)}, f32[2,64,128]{2,1,0:T(8,128)S(1)}, u32[]{:S(2)}, u32[]{:S(2)}) collective-permute-start(f32[2,64,128]{2,1,0:T(8,128)S(1)} %get-tuple-element.38.after.mine), channel_id=1, source_target_pairs={{0,1},{1,0},{2,3},{3,2},{4,5},{5,4},{6,7},{7,6},{8,9},{9,8},{10,11... | collective-permute-start | bytes 196616 | tf_op jit(solution)/shard_map/ppermute | solution.py:24
  58.3 0.0 collective-permute-start.14
  58.3 2.9 %collective-permute-done.10.arrived = f32[2,64,128]{2,1,0:T(8,128)S(1)} collective-permute-done((f32[2,64,128]{2,1,0:T(8,128)S(1)}, f32[2,64,128]{2,1,0:T(8,128)S(1)}, u32[]{:S(2)}, u32[]{:S(2)}) %collective-permute-start.10) | collective-permute-done | bytes 65568 | tf_op jit(solution)/shard_map/ppermute | solution.py:24
  61.3 0.1 shard_map.78
  61.4 0.0 collective-permute-done.11.handed.passed
  61.4 0.0 copy-start.4
  61.4 0.0 copy-start.6
  61.5 0.1 shard_map.79.after
  61.5 0.1 collective-permute-start.13
  61.6 1.6 %collective-permute-start.12 = (f32[2,64,128]{2,1,0:T(8,128)S(1)}, f32[2,64,128]{2,1,0:T(8,128)S(1)}, u32[]{:S(2)}, u32[]{:S(2)}) collective-permute-start(f32[2,64,128]{2,1,0:T(8,128)S(1)} %get-tuple-element.28.after.mine), channel_id=1, source_target_pairs={{0,1},{1,0},{2,3},{3,2},{4,5},{5,4},{6,7},{7,6},{8,9},{9,8},{10,11... | collective-permute-start | bytes 196616 | tf_op jit(solution)/shard_map/ppermute | solution.py:24
  63.1 2.8 %collective-permute-done.12.arrived = f32[2,64,128]{2,1,0:T(8,128)S(1)} collective-permute-done((f32[2,64,128]{2,1,0:T(8,128)S(1)}, f32[2,64,128]{2,1,0:T(8,128)S(1)}, u32[]{:S(2)}, u32[]{:S(2)}) %collective-permute-start.12) | collective-permute-done | bytes 65568 | tf_op jit(solution)/shard_map/ppermute | solution.py:24
  65.9 0.0 copy-done.4
  65.9 0.0 copy-done.6
  65.9 0.1 shard_map.80.own
  66.0 7.1 %collective-permute-done.14.arrived = f32[16,64,128]{2,1,0:T(8,128)S(1)} collective-permute-done((f32[16,64,128]{2,1,0:T(8,128)S(1)}, f32[16,64,128]{2,1,0:T(8,128)S(1)}, u32[]{:S(2)}, u32[]{:S(2)}) %collective-permute-start.14) | collective-permute-done | bytes 524320 | tf_op jit(solution)/shard_map/ppermute | solution.py:19
  73.1 1.0 %shard_map.81.refs_0_ = f32[2,4,32,8,128]{4,3,2,1,0:T(8,128)} custom-call(s32[1]{0:T(128)} %bitcast.flag, f32[2,16,64,128]{3,2,1,0:T(8,128)S(1)} %shard_map.80.own, f32[16,64,128]{2,1,0:T(8,128)S(1)} %collective-permute-done.6.handed.passed, f32[16,64,128]{2,1,0:T(8,128)S(1)} %collective-permute-done.14.arrived), custom_call_target="tpu_custom_call" | custom-call | bytes 1048576 | tf_op jit(solution)/shard_map/pallas_call | solution.py:409
  74.1 9.4 %collective-permute-done.13.arrived = f32[16,64,128]{2,1,0:T(8,128)S(1)} collective-permute-done((f32[16,64,128]{2,1,0:T(8,128)S(1)}, f32[16,64,128]{2,1,0:T(8,128)S(1)}, u32[]{:S(2)}, u32[]{:S(2)}) %collective-permute-start.13) | collective-permute-done | bytes 524320 | tf_op jit(solution)/shard_map/ppermute | solution.py:19
  83.6 1.0 %shard_map.82 = f32[2,4,32,8,128]{4,3,2,1,0:T(8,128)} custom-call(s32[1]{0:T(128)} %bitcast.flag, f32[2,16,64,128]{3,2,1,0:T(8,128)S(1)} %shard_map.80.own, f32[16,64,128]{2,1,0:T(8,128)S(1)} %collective-permute-done.11.handed.passed, f32[16,64,128]{2,1,0:T(8,128)S(1)} %collective-permute-done.13.arrived, ...), custom_call_target="tpu_custom_call", output_to_operand_aliasing={{}: (4, {})} | custom-call | bytes 1048576 | tf_op jit(solution)/shard_map/pallas_call | solution.py:409
  (4 shorter events, 0.1 us)
Async XLA Ops:
  1.3 18.0 %collective-permute-start.2 = (f32[16,64,128]{2,1,0:T(8,128)S(1)}, f32[16,64,128]{2,1,0:T(8,128)S(1)}, u32[]{:S(2)}, u32[]{:S(2)}) collective-permute-start(f32[16,64,128]{2,1,0:T(8,128)S(1)} %shard_map.64.refs_0_.first.own), channel_id=1, source_target_pairs={{0,4},{2,6},{4,8},{6,10},{8,12},{10,14},{12,16},{14,18},{16,20},{1... | collective-permute-start | bytes 1572872 | tf_op jit(solution)/shard_map/ppermute | solution.py:19
  6.3 0.7 copy-start.7
  8.3 0.9 %copy-start = (f32[5,64,128]{2,1,0:T(8,128)S(1)}, f32[5,64,128]{2,1,0:T(8,128)}, u32[]{:S(2)}) copy-start(f32[5,64,128]{2,1,0:T(8,128)} %constant.74.clone.decay) | copy-start | bytes 491524
  8.3 1.0 %copy-start.1 = (bf16[256,256]{1,0:T(8,128)(2,1)S(1)}, bf16[256,256]{1,0:T(8,128)(2,1)}, u32[]{:S(2)}) copy-start(bf16[256,256]{1,0:T(8,128)(2,1)} %constant.72.clone.right_ref) | copy-start | bytes 393220
  8.3 1.0 %copy-start.2 = (bf16[64,192]{1,0:T(8,128)(2,1)S(1)}, bf16[64,192]{1,0:T(8,128)(2,1)}, u32[]{:S(2)}) copy-start(bf16[64,192]{1,0:T(8,128)(2,1)} %constant.73.clone.left_ref) | copy-start | bytes 73732
  9.3 0.7 copy-start.5
  10.0 9.3 %copy-start.3 = (f32[2,16,64,128]{3,2,1,0:T(8,128)}, f32[2,16,64,128]{3,2,1,0:T(8,128)S(1)}, u32[]{:S(2)}) copy-start(f32[2,16,64,128]{3,2,1,0:T(8,128)S(1)} %get-tuple-element.48.spectrum) | copy-start | bytes 3145732
  19.4 9.3 %collective-permute-start.3 = (f32[16,64,128]{2,1,0:T(8,128)S(1)}, f32[16,64,128]{2,1,0:T(8,128)S(1)}, u32[]{:S(2)}, u32[]{:S(2)}) collective-permute-start(f32[16,64,128]{2,1,0:T(8,128)S(1)} %shard_map.68.after), channel_id=1, source_target_pairs={{0,2},{2,0},{4,6},{6,4},{8,10},{10,8},{12,14},{14,12},{16,18},{18,... | collective-permute-start | bytes 1572872 | tf_op jit(solution)/shard_map/ppermute | solution.py:24
  19.4 6.1 %collective-permute-start = (s32[1]{0:T(128)}, s32[1]{0:T(128)}, u32[]{:S(2)}, u32[]{:S(2)}) collective-permute-start(s32[1]{0:T(128)} %bitcast.5), channel_id=1, source_target_pairs={{0,2},{2,4},{4,6},{6,8},{8,10},{10,12},{12,14},{14,16},{16,18},{18... | collective-permute-start | bytes 20 | tf_op jit(solution)/shard_map/ppermute | solution.py:19
  19.9 6.4 %collective-permute-start.1 = (s32[1]{0:T(128)}, s32[1]{0:T(128)}, u32[]{:S(2)}, u32[]{:S(2)}) collective-permute-start(s32[1]{0:T(128)} %bitcast.5), channel_id=1, source_target_pairs={{0,4},{2,6},{4,8},{6,10},{8,12},{10,14},{12,16},{14,18},{16,20},{1... | collective-permute-start | bytes 20 | tf_op jit(solution)/shard_map/ppermute | solution.py:19
  28.7 4.3 %collective-permute-start.4 = (f32[2,64,128]{2,1,0:T(8,128)S(1)}, f32[2,64,128]{2,1,0:T(8,128)S(1)}, u32[]{:S(2)}, u32[]{:S(2)}) collective-permute-start(f32[2,64,128]{2,1,0:T(8,128)S(1)} %get-tuple-element.30.after.mine), channel_id=1, source_target_pairs={{0,1},{1,0},{2,3},{3,2},{4,5},{5,4},{6,7},{7,6},{8,9},{9,8},{10,11... | collective-permute-start | bytes 196616 | tf_op jit(solution)/shard_map/ppermute | solution.py:24
  33.2 5.7 %collective-permute-start.6 = (f32[16,64,128]{2,1,0:T(8,128)S(1)}, f32[16,64,128]{2,1,0:T(8,128)S(1)}, u32[]{:S(2)}, u32[]{:S(2)}) collective-permute-start(f32[16,64,128]{2,1,0:T(8,128)S(1)} %get-tuple-element.33.after), channel_id=1, source_target_pairs={{0,2},{2,0},{4,6},{6,4},{8,10},{10,8},{12,14},{14,12},{16,18},{18,... | collective-permute-start | bytes 1572872 | tf_op jit(solution)/shard_map/ppermute | solution.py:24
  33.2 17.0 %collective-permute-start.7 = (f32[16,64,128]{2,1,0:T(8,128)S(1)}, f32[16,64,128]{2,1,0:T(8,128)S(1)}, u32[]{:S(2)}, u32[]{:S(2)}) collective-permute-start(f32[16,64,128]{2,1,0:T(8,128)S(1)} %shard_map.65.second.other.own), channel_id=1, source_target_pairs={{0,4},{2,6},{4,8},{6,10},{8,12},{10,14},{12,16},{14,18},{16,20},{1... | collective-permute-start | bytes 1572872 | tf_op jit(solution)/shard_map/ppermute | solution.py:19
  33.3 4.4 %collective-permute-start.5 = (f32[2,64,128]{2,1,0:T(8,128)S(1)}, f32[2,64,128]{2,1,0:T(8,128)S(1)}, u32[]{:S(2)}, u32[]{:S(2)}) collective-permute-start(f32[2,64,128]{2,1,0:T(8,128)S(1)} %get-tuple-element.29.after.mine), channel_id=1, source_target_pairs={{0,1},{1,0},{2,3},{3,2},{4,5},{5,4},{6,7},{7,6},{8,9},{9,8},{10,11... | collective-permute-start | bytes 196616 | tf_op jit(solution)/shard_map/ppermute | solution.py:24
  50.3 2.0 %collective-permute-start.8 = (f32[16,64,128]{2,1,0:T(8,128)S(1)}, f32[16,64,128]{2,1,0:T(8,128)S(1)}, u32[]{:S(2)}, u32[]{:S(2)}) collective-permute-start(f32[16,64,128]{2,1,0:T(8,128)S(1)} %shard_map.74.after), channel_id=1, source_target_pairs={{0,2},{2,0},{4,6},{6,4},{8,10},{10,8},{12,14},{14,12},{16,18},{18,... | collective-permute-start | bytes 1572872 | tf_op jit(solution)/shard_map/ppermute | solution.py:24
  52.3 4.3 %collective-permute-start.9 = (f32[2,64,128]{2,1,0:T(8,128)S(1)}, f32[2,64,128]{2,1,0:T(8,128)S(1)}, u32[]{:S(2)}, u32[]{:S(2)}) collective-permute-start(f32[2,64,128]{2,1,0:T(8,128)S(1)} %get-tuple-element.39.after.mine), channel_id=1, source_target_pairs={{0,1},{1,0},{2,3},{3,2},{4,5},{5,4},{6,7},{7,6},{8,9},{9,8},{10,11... | collective-permute-start | bytes 196616 | tf_op jit(solution)/shard_map/ppermute | solution.py:24
  56.7 4.7 %collective-permute-start.11 = (f32[16,64,128]{2,1,0:T(8,128)S(1)}, f32[16,64,128]{2,1,0:T(8,128)S(1)}, u32[]{:S(2)}, u32[]{:S(2)}) collective-permute-start(f32[16,64,128]{2,1,0:T(8,128)S(1)} %get-tuple-element.43.after), channel_id=1, source_target_pairs={{0,2},{2,0},{4,6},{6,4},{8,10},{10,8},{12,14},{14,12},{16,18},{18,... | collective-permute-start | bytes 1572872 | tf_op jit(solution)/shard_map/ppermute | solution.py:24
  56.8 4.5 %collective-permute-start.10 = (f32[2,64,128]{2,1,0:T(8,128)S(1)}, f32[2,64,128]{2,1,0:T(8,128)S(1)}, u32[]{:S(2)}, u32[]{:S(2)}) collective-permute-start(f32[2,64,128]{2,1,0:T(8,128)S(1)} %get-tuple-element.38.after.mine), channel_id=1, source_target_pairs={{0,1},{1,0},{2,3},{3,2},{4,5},{5,4},{6,7},{7,6},{8,9},{9,8},{10,11... | collective-permute-start | bytes 196616 | tf_op jit(solution)/shard_map/ppermute | solution.py:24
  58.3 14.8 %collective-permute-start.14 = (f32[16,64,128]{2,1,0:T(8,128)S(1)}, f32[16,64,128]{2,1,0:T(8,128)S(1)}, u32[]{:S(2)}, u32[]{:S(2)}) collective-permute-start(f32[16,64,128]{2,1,0:T(8,128)S(1)} %shard_map.73.after), channel_id=1, source_target_pairs={{0,28},{2,30},{4,0},{6,2},{8,4},{10,6},{12,8},{14,10},{16,12},{18,... | collective-permute-start | bytes 1572872 | tf_op jit(solution)/shard_map/ppermute | solution.py:19
  61.4 4.5 %copy-start.4 = (f32[2,16,64,128]{3,2,1,0:T(8,128)S(1)}, f32[2,16,64,128]{3,2,1,0:T(8,128)}, u32[]{:S(2)}) copy-start(f32[2,16,64,128]{3,2,1,0:T(8,128)} %copy-done.3) | copy-start | bytes 3145732
  61.4 4.5 %copy-start.6 = (f32[2,2,2,64,128]{4,3,2,1,0:T(8,128)S(1)}, f32[2,2,2,64,128]{4,3,2,1,0:T(8,128)}, u32[]{:S(2)}) copy-start(f32[2,2,2,64,128]{4,3,2,1,0:T(8,128)} %copy-done.5) | copy-start | bytes 786436
  61.5 22.0 %collective-permute-start.13 = (f32[16,64,128]{2,1,0:T(8,128)S(1)}, f32[16,64,128]{2,1,0:T(8,128)S(1)}, u32[]{:S(2)}, u32[]{:S(2)}) collective-permute-start(f32[16,64,128]{2,1,0:T(8,128)S(1)} %shard_map.79.after), channel_id=1, source_target_pairs={{0,28},{2,30},{4,0},{6,2},{8,4},{10,6},{12,8},{14,10},{16,12},{18,... | collective-permute-start | bytes 1572872 | tf_op jit(solution)/shard_map/ppermute | solution.py:19
  61.6 4.3 %collective-permute-start.12 = (f32[2,64,128]{2,1,0:T(8,128)S(1)}, f32[2,64,128]{2,1,0:T(8,128)S(1)}, u32[]{:S(2)}, u32[]{:S(2)}) collective-permute-start(f32[2,64,128]{2,1,0:T(8,128)S(1)} %get-tuple-element.28.after.mine), channel_id=1, source_target_pairs={{0,1},{1,0},{2,3},{3,2},{4,5},{5,4},{6,7},{7,6},{8,9},{9,8},{10,11... | collective-permute-start | bytes 196616 | tf_op jit(solution)/shard_map/ppermute | solution.py:24

commit v9 on v8

--- a/solution.py
+++ b/solution.py
@@ -139,11 +139,11 @@
 
 
 def pick_kernel(flag, after, own, far, out):
-    @pl.when(flag[0] == 0)
+    @pl.when(flag[0] & 1 == 0)
     def _():
         out[...] = own[...]
 
-    @pl.when(flag[0] == 1)
+    @pl.when(flag[0] & 1 == 1)
     def _():
         out[...] = far[...]
 
@@ -165,7 +165,7 @@
 
 def forward_kernel(base, counts, after, own, other, right_ref, left_ref, decay, *refs):
     spectrum, moments, mine = refs
-    owned, rows, side, width = own.shape
+    _, rows, side, width = own.shape
     chunks = rows // GROUP
     lower = lax.broadcasted_iota(jnp.int32, (side, width), 1) < width // 2
 
@@ -200,7 +200,7 @@
 
         return carry
 
-    lax.fori_loop(0, owned, orbital_step, 0)
+    lax.fori_loop(0, spectrum.shape[0], orbital_step, 0)
 
 
 def backward_kernel(
@@ -215,7 +215,7 @@
         total, partner = refs[-3:-1]
         total[...] = refs[0][...] if len(refs) > 3 else jnp.zeros_like(total)
         partner[...] = jnp.zeros_like(partner)
-    owned, rows, side, width = own.shape
+    _, rows, side, width = own.shape
     chunks = rows // GROUP
     lower = lax.broadcasted_iota(jnp.int32, (side, width), 1) < width // 2
 
@@ -266,7 +266,7 @@
         lax.fori_loop(0, jnp.where(number > 0, chunks, 0), chunk_step, 0)
         return carry
 
-    lax.fori_loop(0, owned, orbital_step, 0)
+    lax.fori_loop(0, spectrum.shape[0], orbital_step, 0)
 
 
 def pair_counts(pair_list, pair_count, owned, band_index, band_count):
@@ -345,13 +345,14 @@
     listed = (lax.optimization_barrier(listed) * 2 + band_index % 2).reshape(1)
     counts = (counts * 2 + band_index % 2).reshape(1)
 
-    def forward(base, after, other, counts=counts):
+    def forward(base, after, other, counts=counts, inside=False):
+        lines = (1 if inside else owned,)
         return call(
             functools.partial(forward_kernel, base),
             (
-                both,
-                jax.ShapeDtypeStruct((owned, chunks, 2) + shape[1:], jnp.float32),
-                jax.ShapeDtypeStruct((owned,) + shape[1:], jnp.float32),
+                jax.ShapeDtypeStruct(lines + shape, jnp.float32),
+                jax.ShapeDtypeStruct(lines + (chunks, 2) + shape[1:], jnp.float32),
+                jax.ShapeDtypeStruct(lines + shape[1:], jnp.float32),
             ),
             [smem, free] + [vmem] * 5,
         )(counts, after, own, other, right, left, decay)
@@ -369,13 +370,13 @@
         )(numbers, after, own, *state, right, left, decay, *total)
 
     inner_base = REACH * owned * owned
-    spectrum, moments, mine = forward(inner_base, own, fields[1], listed)
+    spectrum, moments, mine = forward(inner_base, own, fields[1], listed, inside=True)
     inner = (fields[1], spectrum, moments, mine, exchanged(mine))
     after = mine
 
     def brought(row, after):
         picked = call(pick_kernel, one, [smem, free, vmem, vmem])(
-            flag, after, fields[row], far[row]
+            counts, after, fields[row], far[row]
         )
         return picked, swapped(picked, "band")
 

time: 84.8 us -> 78.7 us (0.928)
  waiting for transfers between devices: 59.6 us -> 52.5 us
  starting transfers between devices: 11.7 us -> 12.8 us
    ppermute x6, waiting for transfers between devices: 43.6 us -> 36.2 us  [rotated(): return lax.ppermute(value, axis, pairs)]
    ppermute x6, starting transfers between devices: 3.67 us -> 5.01 us  [rotated(): return lax.ppermute(value, axis, pairs)]
    unnamed x16 -> x12, local copies, waits for them, and re-layouts: 2.27 us -> 2.21 us
where the time goes in v9:
time: 78.7 us; the launch traced here: 78.5 us
  waiting for transfers between devices  52.5 us (67%)
  starting transfers between devices  12.8 us (16%)
  Pallas kernels  7.5 us (10%)
  between operations  2.83 us (4%)
  local copies, waits for them, and re-layouts  2.21 us (3%)
    ppermute x6, waiting for transfers between devices, rotated(): return lax.ppermute(value, axis, pairs)  36.2 us
    ppermute x9, waiting for transfers between devices, swapped(): lax.ppermute(value, axis, [(source, source ^ 1) for source in range(count)])  16.3 us
    ppermute x9, starting transfers between devices, swapped(): lax.ppermute(value, axis, [(source, source ^ 1) for source in range(count)])  7.8 us
    ppermute x6, starting transfers between devices, rotated(): return lax.ppermute(value, axis, pairs)  5.01 us
    pallas_call x2, Pallas kernels, on_device(): call(functools.partial(arrange_kernel, row), one, [hbm] + [free] * row, s...  2.56 us
    unnamed x12, local copies, waits for them, and re-layouts  2.21 us
    pallas_call x2, Pallas kernels, on_device(): call(functools.partial(restore_kernel, row), out, [smem] + [vmem] * 3 + [...  1.98 us
  transfers between devices with their start and end apart: 15, of which 12 were waited for; matrix products, arithmetic and copies ran while one was open for 1% of the time, Pallas kernels for 6%

profile of v9, /device:TPU:0, one launch (start us, length us, event | category | flops | bytes accessed | tf_op | source)
XLA Modules:
  0.0 78.5 jit_solution(16116796722809787180)
XLA Ops:
  0.0 1.3 %shard_map.64.refs_0_.first.own = f32[16,64,128]{2,1,0:T(8,128)S(1)} custom-call(f32[2,4,32,8,128]{4,3,2,1,0:T(8,128)} %bitcast.39), custom_call_target="tpu_custom_call" | custom-call | bytes 1048576 | tf_op jit(solution)/shard_map/pallas_call | solution.py:331
  1.3 3.0 %collective-permute-start.2 = (f32[16,64,128]{2,1,0:T(8,128)S(1)}, f32[16,64,128]{2,1,0:T(8,128)S(1)}, u32[]{:S(2)}, u32[]{:S(2)}) collective-permute-start(f32[16,64,128]{2,1,0:T(8,128)S(1)} %shard_map.64.refs_0_.first.own), channel_id=1, source_target_pairs={{0,4},{2,6},{4,8},{6,10},{8,12},{10,14},{12,16},{14,18},{16,20},{1... | collective-permute-start | bytes 1572872 | tf_op jit(solution)/shard_map/ppermute | solution.py:19
  5.0 0.0 copy-start.5
  5.0 0.7 copy-done.5
  5.7 0.7 fusion.1
  6.3 0.0 collective-permute-start
  6.3 1.5 %collective-permute-start.1 = (s32[1]{0:T(128)}, s32[1]{0:T(128)}, u32[]{:S(2)}, u32[]{:S(2)}) collective-permute-start(s32[1]{0:T(128)} %bitcast.5), channel_id=1, source_target_pairs={{0,4},{2,6},{4,8},{6,10},{8,12},{10,14},{12,16},{14,18},{16,20},{1... | collective-permute-start | bytes 20 | tf_op jit(solution)/shard_map/ppermute | solution.py:19
  7.9 1.3 %shard_map.65.second.other.own = f32[16,64,128]{2,1,0:T(8,128)S(1)} custom-call(f32[2,4,32,8,128]{4,3,2,1,0:T(8,128)} %bitcast.40, f32[16,64,128]{2,1,0:T(8,128)S(1)} %shard_map.64.refs_0_.first.own), custom_call_target="tpu_custom_call" | custom-call | bytes 1048576 | tf_op jit(solution)/shard_map/pallas_call | solution.py:331
  9.8 0.0 copy-start
  9.8 0.0 copy-start.1
  9.8 0.0 copy-start.2
  9.8 0.1 shard_map.66.after.own
  9.9 0.8 %copy-done = f32[5,64,128]{2,1,0:T(8,128)S(1)} copy-done((f32[5,64,128]{2,1,0:T(8,128)S(1)}, f32[5,64,128]{2,1,0:T(8,128)}, u32[]{:S(2)}) %copy-start) | copy-done | bytes 163864
  10.7 0.1 copy-done.1
  10.8 0.0 copy-done.2
  10.8 0.0 copy-start.3
  10.8 0.7 copy-done.3
  11.4 7.0 %collective-permute-done = s32[1]{0:T(128)} collective-permute-done((s32[1]{0:T(128)}, s32[1]{0:T(128)}, u32[]{:S(2)}, u32[]{:S(2)}) %collective-permute-start) | collective-permute-done | bytes 36 | tf_op jit(solution)/shard_map/ppermute | solution.py:19
  18.4 0.9 %collective-permute-done.1 = s32[1]{0:T(128)} collective-permute-done((s32[1]{0:T(128)}, s32[1]{0:T(128)}, u32[]{:S(2)}, u32[]{:S(2)}) %collective-permute-start.1) | collective-permute-done | bytes 36 | tf_op jit(solution)/shard_map/ppermute | solution.py:19
  20.7 0.0 collective-permute-done.2.far.other
  20.7 0.1 collective-permute-start.3
  20.8 1.0 %shard_map.69 = (f32[2,16,64,128]{3,2,1,0:T(8,128)S(1)}, f32[2,2,2,64,128]{4,3,2,1,0:T(8,128)S(1)}, f32[2,64,128]{2,1,0:T(8,128)S(1)}) custom-call(s32[1]{0:T(128)} %bitcast.8.flag.counts, f32[16,64,128]{2,1,0:T(8,128)S(1)} %shard_map.68.after, f32[2,16,64,128]{3,2,1,0:T(8,128)S(1)} %shard_map.66.after.own, ...), custom_call_target="tpu_custom_call" | custom-call | bytes 1048576 | tf_op jit(solution)/shard_map/pallas_call | solution.py:350
  21.9 0.8 %collective-permute-done.3.other = f32[16,64,128]{2,1,0:T(8,128)S(1)} collective-permute-done((f32[16,64,128]{2,1,0:T(8,128)S(1)}, f32[16,64,128]{2,1,0:T(8,128)S(1)}, u32[]{:S(2)}, u32[]{:S(2)}) %collective-permute-start.3) | collective-permute-done | bytes 524320 | tf_op jit(solution)/shard_map/ppermute | solution.py:24
  22.7 1.5 %collective-permute-start.4 = (f32[2,64,128]{2,1,0:T(8,128)S(1)}, f32[2,64,128]{2,1,0:T(8,128)S(1)}, u32[]{:S(2)}, u32[]{:S(2)}) collective-permute-start(f32[2,64,128]{2,1,0:T(8,128)S(1)} %get-tuple-element.30.after.mine), channel_id=1, source_target_pairs={{0,1},{1,0},{2,3},{3,2},{4,5},{5,4},{6,7},{7,6},{8,9},{9,8},{10,11... | collective-permute-start | bytes 196616 | tf_op jit(solution)/shard_map/ppermute | solution.py:24
  24.2 2.8 %collective-permute-done.4.arrived = f32[2,64,128]{2,1,0:T(8,128)S(1)} collective-permute-done((f32[2,64,128]{2,1,0:T(8,128)S(1)}, f32[2,64,128]{2,1,0:T(8,128)S(1)}, u32[]{:S(2)}, u32[]{:S(2)}) %collective-permute-start.4) | collective-permute-done | bytes 65568 | tf_op jit(solution)/shard_map/ppermute | solution.py:24
  27.0 0.1 shard_map.71
  27.1 0.1 collective-permute-start.6
  27.2 0.2 collective-permute-start.7
  27.4 1.5 %collective-permute-start.5 = (f32[2,64,128]{2,1,0:T(8,128)S(1)}, f32[2,64,128]{2,1,0:T(8,128)S(1)}, u32[]{:S(2)}, u32[]{:S(2)}) collective-permute-start(f32[2,64,128]{2,1,0:T(8,128)S(1)} %get-tuple-element.29.after.mine), channel_id=1, source_target_pairs={{0,1},{1,0},{2,3},{3,2},{4,5},{5,4},{6,7},{7,6},{8,9},{9,8},{10,11... | collective-permute-start | bytes 196616 | tf_op jit(solution)/shard_map/ppermute | solution.py:24
  28.9 2.8 %collective-permute-done.5.arrived = f32[2,64,128]{2,1,0:T(8,128)S(1)} collective-permute-done((f32[2,64,128]{2,1,0:T(8,128)S(1)}, f32[2,64,128]{2,1,0:T(8,128)S(1)}, u32[]{:S(2)}, u32[]{:S(2)}) %collective-permute-start.5) | collective-permute-done | bytes 65568 | tf_op jit(solution)/shard_map/ppermute | solution.py:24
  31.7 1.1 %shard_map.72 = (f32[2,16,64,128]{3,2,1,0:T(8,128)S(1)}, f32[16,64,128]{2,1,0:T(8,128)S(1)}) custom-call(s32[1]{0:T(128)} %bitcast.8.flag.counts, f32[16,64,128]{2,1,0:T(8,128)S(1)} %get-tuple-element.33.after, f32[2,16,64,128]{3,2,1,0:T(8,128)S(1)} %shard_map.66.after.own, f32[16,64,128]{2,1,0:T(8,128)S(1)} %collective-permute-done.2.far.other, ...), custom_call_target="tpu_custom_call" | custom-call | bytes 1048576 | tf_op jit(solution)/shard_map/pallas_call | solution.py:365
  32.8 0.0 collective-permute-done.6.handed.passed
  32.8 0.1 shard_map.73.after
  32.9 11.4 %collective-permute-done.7.far.other = f32[16,64,128]{2,1,0:T(8,128)S(1)} collective-permute-done((f32[16,64,128]{2,1,0:T(8,128)S(1)}, f32[16,64,128]{2,1,0:T(8,128)S(1)}, u32[]{:S(2)}, u32[]{:S(2)}) %collective-permute-start.7) | collective-permute-done | bytes 524320 | tf_op jit(solution)/shard_map/ppermute | solution.py:19
  44.3 0.1 collective-permute-start.8
  44.3 0.1 shard_map.75
  44.4 1.8 %collective-permute-done.8.other = f32[16,64,128]{2,1,0:T(8,128)S(1)} collective-permute-done((f32[16,64,128]{2,1,0:T(8,128)S(1)}, f32[16,64,128]{2,1,0:T(8,128)S(1)}, u32[]{:S(2)}, u32[]{:S(2)}) %collective-permute-start.8) | collective-permute-done | bytes 524320 | tf_op jit(solution)/shard_map/ppermute | solution.py:24
  46.2 1.5 %collective-permute-start.9 = (f32[2,64,128]{2,1,0:T(8,128)S(1)}, f32[2,64,128]{2,1,0:T(8,128)S(1)}, u32[]{:S(2)}, u32[]{:S(2)}) collective-permute-start(f32[2,64,128]{2,1,0:T(8,128)S(1)} %get-tuple-element.39.after.mine), channel_id=1, source_target_pairs={{0,1},{1,0},{2,3},{3,2},{4,5},{5,4},{6,7},{7,6},{8,9},{9,8},{10,11... | collective-permute-start | bytes 196616 | tf_op jit(solution)/shard_map/ppermute | solution.py:24
  47.7 2.8 %collective-permute-done.9.arrived = f32[2,64,128]{2,1,0:T(8,128)S(1)} collective-permute-done((f32[2,64,128]{2,1,0:T(8,128)S(1)}, f32[2,64,128]{2,1,0:T(8,128)S(1)}, u32[]{:S(2)}, u32[]{:S(2)}) %collective-permute-start.9) | collective-permute-done | bytes 65568 | tf_op jit(solution)/shard_map/ppermute | solution.py:24
  50.5 0.1 shard_map.77
  50.7 0.1 collective-permute-start.11
  50.7 1.6 %collective-permute-start.10 = (f32[2,64,128]{2,1,0:T(8,128)S(1)}, f32[2,64,128]{2,1,0:T(8,128)S(1)}, u32[]{:S(2)}, u32[]{:S(2)}) collective-permute-start(f32[2,64,128]{2,1,0:T(8,128)S(1)} %get-tuple-element.38.after.mine), channel_id=1, source_target_pairs={{0,1},{1,0},{2,3},{3,2},{4,5},{5,4},{6,7},{7,6},{8,9},{9,8},{10,11... | collective-permute-start | bytes 196616 | tf_op jit(solution)/shard_map/ppermute | solution.py:24
  52.3 0.1 collective-permute-start.14
  52.4 2.8 %collective-permute-done.10.arrived = f32[2,64,128]{2,1,0:T(8,128)S(1)} collective-permute-done((f32[2,64,128]{2,1,0:T(8,128)S(1)}, f32[2,64,128]{2,1,0:T(8,128)S(1)}, u32[]{:S(2)}, u32[]{:S(2)}) %collective-permute-start.10) | collective-permute-done | bytes 65568 | tf_op jit(solution)/shard_map/ppermute | solution.py:24
  55.2 0.1 shard_map.78
  55.4 0.0 collective-permute-done.11.handed.passed
  55.4 0.0 copy-start.4
  55.4 0.1 shard_map.79.after
  55.5 0.1 collective-permute-start.13
  55.6 1.5 %collective-permute-start.12 = (f32[1,64,128]{2,1,0:T(8,128)S(1)}, f32[1,64,128]{2,1,0:T(8,128)S(1)}, u32[]{:S(2)}, u32[]{:S(2)}) collective-permute-start(f32[1,64,128]{2,1,0:T(8,128)S(1)} %get-tuple-element.28.after.mine), channel_id=1, source_target_pairs={{0,1},{1,0},{2,3},{3,2},{4,5},{5,4},{6,7},{7,6},{8,9},{9,8},{10,11... | collective-permute-start | bytes 98312 | tf_op jit(solution)/shard_map/ppermute | solution.py:24
  57.1 2.4 %collective-permute-done.12.arrived = f32[1,64,128]{2,1,0:T(8,128)S(1)} collective-permute-done((f32[1,64,128]{2,1,0:T(8,128)S(1)}, f32[1,64,128]{2,1,0:T(8,128)S(1)}, u32[]{:S(2)}, u32[]{:S(2)}) %collective-permute-start.12) | collective-permute-done | bytes 32800 | tf_op jit(solution)/shard_map/ppermute | solution.py:24
  59.5 0.0 copy-done.4
  59.5 0.1 shard_map.80.own
  59.6 7.5 %collective-permute-done.14.arrived = f32[16,64,128]{2,1,0:T(8,128)S(1)} collective-permute-done((f32[16,64,128]{2,1,0:T(8,128)S(1)}, f32[16,64,128]{2,1,0:T(8,128)S(1)}, u32[]{:S(2)}, u32[]{:S(2)}) %collective-permute-start.14) | collective-permute-done | bytes 524320 | tf_op jit(solution)/shard_map/ppermute | solution.py:19
  67.1 1.0 %shard_map.81.refs_0_ = f32[2,4,32,8,128]{4,3,2,1,0:T(8,128)} custom-call(s32[1]{0:T(128)} %bitcast.flag, f32[2,16,64,128]{3,2,1,0:T(8,128)S(1)} %shard_map.80.own, f32[16,64,128]{2,1,0:T(8,128)S(1)} %collective-permute-done.6.handed.passed, f32[16,64,128]{2,1,0:T(8,128)S(1)} %collective-permute-done.14.arrived), custom_call_target="tpu_custom_call" | custom-call | bytes 1048576 | tf_op jit(solution)/shard_map/pallas_call | solution.py:410
  68.1 9.4 %collective-permute-done.13.arrived = f32[16,64,128]{2,1,0:T(8,128)S(1)} collective-permute-done((f32[16,64,128]{2,1,0:T(8,128)S(1)}, f32[16,64,128]{2,1,0:T(8,128)S(1)}, u32[]{:S(2)}, u32[]{:S(2)}) %collective-permute-start.13) | collective-permute-done | bytes 524320 | tf_op jit(solution)/shard_map/ppermute | solution.py:19
  77.5 1.0 %shard_map.82 = f32[2,4,32,8,128]{4,3,2,1,0:T(8,128)} custom-call(s32[1]{0:T(128)} %bitcast.flag, f32[2,16,64,128]{3,2,1,0:T(8,128)S(1)} %shard_map.80.own, f32[16,64,128]{2,1,0:T(8,128)S(1)} %collective-permute-done.11.handed.passed, f32[16,64,128]{2,1,0:T(8,128)S(1)} %collective-permute-done.13.arrived, ...), custom_call_target="tpu_custom_call", output_to_operand_aliasing={{}: (4, {})} | custom-call | bytes 1048576 | tf_op jit(solution)/shard_map/pallas_call | solution.py:410
  (5 shorter events, 0.1 us)
Async XLA Ops:
  1.3 19.4 %collective-permute-start.2 = (f32[16,64,128]{2,1,0:T(8,128)S(1)}, f32[16,64,128]{2,1,0:T(8,128)S(1)}, u32[]{:S(2)}, u32[]{:S(2)}) collective-permute-start(f32[16,64,128]{2,1,0:T(8,128)S(1)} %shard_map.64.refs_0_.first.own), channel_id=1, source_target_pairs={{0,4},{2,6},{4,8},{6,10},{8,12},{10,14},{12,16},{14,18},{16,20},{1... | collective-permute-start | bytes 1572872 | tf_op jit(solution)/shard_map/ppermute | solution.py:19
  5.0 0.7 copy-start.5
  6.3 12.1 %collective-permute-start = (s32[1]{0:T(128)}, s32[1]{0:T(128)}, u32[]{:S(2)}, u32[]{:S(2)}) collective-permute-start(s32[1]{0:T(128)} %bitcast.5), channel_id=1, source_target_pairs={{0,2},{2,4},{4,6},{6,8},{8,10},{10,12},{12,14},{14,16},{16,18},{18... | collective-permute-start | bytes 20 | tf_op jit(solution)/shard_map/ppermute | solution.py:19
  6.3 13.0 %collective-permute-start.1 = (s32[1]{0:T(128)}, s32[1]{0:T(128)}, u32[]{:S(2)}, u32[]{:S(2)}) collective-permute-start(s32[1]{0:T(128)} %bitcast.5), channel_id=1, source_target_pairs={{0,4},{2,6},{4,8},{6,10},{8,12},{10,14},{12,16},{14,18},{16,20},{1... | collective-permute-start | bytes 20 | tf_op jit(solution)/shard_map/ppermute | solution.py:19
  9.8 0.9 %copy-start = (f32[5,64,128]{2,1,0:T(8,128)S(1)}, f32[5,64,128]{2,1,0:T(8,128)}, u32[]{:S(2)}) copy-start(f32[5,64,128]{2,1,0:T(8,128)} %constant.74.clone.decay) | copy-start | bytes 491524
  9.8 1.0 %copy-start.1 = (bf16[256,256]{1,0:T(8,128)(2,1)S(1)}, bf16[256,256]{1,0:T(8,128)(2,1)}, u32[]{:S(2)}) copy-start(bf16[256,256]{1,0:T(8,128)(2,1)} %constant.72.clone.right_ref) | copy-start | bytes 393220
  9.8 1.0 %copy-start.2 = (bf16[64,192]{1,0:T(8,128)(2,1)S(1)}, bf16[64,192]{1,0:T(8,128)(2,1)}, u32[]{:S(2)}) copy-start(bf16[64,192]{1,0:T(8,128)(2,1)} %constant.73.clone.left_ref) | copy-start | bytes 73732
  10.8 0.7 copy-start.3
  20.7 2.0 %collective-permute-start.3 = (f32[16,64,128]{2,1,0:T(8,128)S(1)}, f32[16,64,128]{2,1,0:T(8,128)S(1)}, u32[]{:S(2)}, u32[]{:S(2)}) collective-permute-start(f32[16,64,128]{2,1,0:T(8,128)S(1)} %shard_map.68.after), channel_id=1, source_target_pairs={{0,2},{2,0},{4,6},{6,4},{8,10},{10,8},{12,14},{14,12},{16,18},{18,... | collective-permute-start | bytes 1572872 | tf_op jit(solution)/shard_map/ppermute | solution.py:24
  22.7 4.3 %collective-permute-start.4 = (f32[2,64,128]{2,1,0:T(8,128)S(1)}, f32[2,64,128]{2,1,0:T(8,128)S(1)}, u32[]{:S(2)}, u32[]{:S(2)}) collective-permute-start(f32[2,64,128]{2,1,0:T(8,128)S(1)} %get-tuple-element.30.after.mine), channel_id=1, source_target_pairs={{0,1},{1,0},{2,3},{3,2},{4,5},{5,4},{6,7},{7,6},{8,9},{9,8},{10,11... | collective-permute-start | bytes 196616 | tf_op jit(solution)/shard_map/ppermute | solution.py:24
  27.1 5.7 %collective-permute-start.6 = (f32[16,64,128]{2,1,0:T(8,128)S(1)}, f32[16,64,128]{2,1,0:T(8,128)S(1)}, u32[]{:S(2)}, u32[]{:S(2)}) collective-permute-start(f32[16,64,128]{2,1,0:T(8,128)S(1)} %get-tuple-element.33.after), channel_id=1, source_target_pairs={{0,2},{2,0},{4,6},{6,4},{8,10},{10,8},{12,14},{14,12},{16,18},{18,... | collective-permute-start | bytes 1572872 | tf_op jit(solution)/shard_map/ppermute | solution.py:24
  27.2 17.0 %collective-permute-start.7 = (f32[16,64,128]{2,1,0:T(8,128)S(1)}, f32[16,64,128]{2,1,0:T(8,128)S(1)}, u32[]{:S(2)}, u32[]{:S(2)}) collective-permute-start(f32[16,64,128]{2,1,0:T(8,128)S(1)} %shard_map.65.second.other.own), channel_id=1, source_target_pairs={{0,4},{2,6},{4,8},{6,10},{8,12},{10,14},{12,16},{14,18},{16,20},{1... | collective-permute-start | bytes 1572872 | tf_op jit(solution)/shard_map/ppermute | solution.py:19
  27.4 4.3 %collective-permute-start.5 = (f32[2,64,128]{2,1,0:T(8,128)S(1)}, f32[2,64,128]{2,1,0:T(8,128)S(1)}, u32[]{:S(2)}, u32[]{:S(2)}) collective-permute-start(f32[2,64,128]{2,1,0:T(8,128)S(1)} %get-tuple-element.29.after.mine), channel_id=1, source_target_pairs={{0,1},{1,0},{2,3},{3,2},{4,5},{5,4},{6,7},{7,6},{8,9},{9,8},{10,11... | collective-permute-start | bytes 196616 | tf_op jit(solution)/shard_map/ppermute | solution.py:24
  44.3 2.0 %collective-permute-start.8 = (f32[16,64,128]{2,1,0:T(8,128)S(1)}, f32[16,64,128]{2,1,0:T(8,128)S(1)}, u32[]{:S(2)}, u32[]{:S(2)}) collective-permute-start(f32[16,64,128]{2,1,0:T(8,128)S(1)} %shard_map.74.after), channel_id=1, source_target_pairs={{0,2},{2,0},{4,6},{6,4},{8,10},{10,8},{12,14},{14,12},{16,18},{18,... | collective-permute-start | bytes 1572872 | tf_op jit(solution)/shard_map/ppermute | solution.py:24
  46.2 4.3 %collective-permute-start.9 = (f32[2,64,128]{2,1,0:T(8,128)S(1)}, f32[2,64,128]{2,1,0:T(8,128)S(1)}, u32[]{:S(2)}, u32[]{:S(2)}) collective-permute-start(f32[2,64,128]{2,1,0:T(8,128)S(1)} %get-tuple-element.39.after.mine), channel_id=1, source_target_pairs={{0,1},{1,0},{2,3},{3,2},{4,5},{5,4},{6,7},{7,6},{8,9},{9,8},{10,11... | collective-permute-start | bytes 196616 | tf_op jit(solution)/shard_map/ppermute | solution.py:24
  50.7 4.7 %collective-permute-start.11 = (f32[16,64,128]{2,1,0:T(8,128)S(1)}, f32[16,64,128]{2,1,0:T(8,128)S(1)}, u32[]{:S(2)}, u32[]{:S(2)}) collective-permute-start(f32[16,64,128]{2,1,0:T(8,128)S(1)} %get-tuple-element.43.after), channel_id=1, source_target_pairs={{0,2},{2,0},{4,6},{6,4},{8,10},{10,8},{12,14},{14,12},{16,18},{18,... | collective-permute-start | bytes 1572872 | tf_op jit(solution)/shard_map/ppermute | solution.py:24
  50.7 4.5 %collective-permute-start.10 = (f32[2,64,128]{2,1,0:T(8,128)S(1)}, f32[2,64,128]{2,1,0:T(8,128)S(1)}, u32[]{:S(2)}, u32[]{:S(2)}) collective-permute-start(f32[2,64,128]{2,1,0:T(8,128)S(1)} %get-tuple-element.38.after.mine), channel_id=1, source_target_pairs={{0,1},{1,0},{2,3},{3,2},{4,5},{5,4},{6,7},{7,6},{8,9},{9,8},{10,11... | collective-permute-start | bytes 196616 | tf_op jit(solution)/shard_map/ppermute | solution.py:24
  52.3 14.8 %collective-permute-start.14 = (f32[16,64,128]{2,1,0:T(8,128)S(1)}, f32[16,64,128]{2,1,0:T(8,128)S(1)}, u32[]{:S(2)}, u32[]{:S(2)}) collective-permute-start(f32[16,64,128]{2,1,0:T(8,128)S(1)} %shard_map.73.after), channel_id=1, source_target_pairs={{0,28},{2,30},{4,0},{6,2},{8,4},{10,6},{12,8},{14,10},{16,12},{18,... | collective-permute-start | bytes 1572872 | tf_op jit(solution)/shard_map/ppermute | solution.py:19
  55.4 4.1 %copy-start.4 = (f32[1,2,2,64,128]{4,3,2,1,0:T(8,128)S(1)}, f32[1,2,2,64,128]{4,3,2,1,0:T(8,128)}, u32[]{:S(2)}) copy-start(f32[1,2,2,64,128]{4,3,2,1,0:T(8,128)} %copy-done.3) | copy-start | bytes 393220
  55.5 22.0 %collective-permute-start.13 = (f32[16,64,128]{2,1,0:T(8,128)S(1)}, f32[16,64,128]{2,1,0:T(8,128)S(1)}, u32[]{:S(2)}, u32[]{:S(2)}) collective-permute-start(f32[16,64,128]{2,1,0:T(8,128)S(1)} %shard_map.79.after), channel_id=1, source_target_pairs={{0,28},{2,30},{4,0},{6,2},{8,4},{10,6},{12,8},{14,10},{16,12},{18,... | collective-permute-start | bytes 1572872 | tf_op jit(solution)/shard_map/ppermute | solution.py:19
  55.6 3.9 %collective-permute-start.12 = (f32[1,64,128]{2,1,0:T(8,128)S(1)}, f32[1,64,128]{2,1,0:T(8,128)S(1)}, u32[]{:S(2)}, u32[]{:S(2)}) collective-permute-start(f32[1,64,128]{2,1,0:T(8,128)S(1)} %get-tuple-element.28.after.mine), channel_id=1, source_target_pairs={{0,1},{1,0},{2,3},{3,2},{4,5},{5,4},{6,7},{7,6},{8,9},{9,8},{10,11... | collective-permute-start | bytes 98312 | tf_op jit(solution)/shard_map/ppermute | solution.py:24
